TPU v7x, 32 devices: a whole 2x2x4 slice. The times are simulated.
32 devices in a mesh: seq: 8 (over z, x), head: 4 (over y, core).
Axes of the slice: x: 2, y: 2, z: 4, core: 2. Of those that a mesh axis runs over, the one named last changes fastest.
Arguments:
- queries: bfloat16 [2048, 2048], P('seq', 'head'), may hold values from -8 to 8
- keys: bfloat16 [2048, 512], P('seq', 'head'), may hold values from -4 to 4
- values: bfloat16 [2048, 512], P('seq', 'head'), may hold values from -6 to 6
- doc_ids: int32 [2048], replicated, may hold values from 0 to 15, never falling along the last dimension, each value on 1 to 1024 neighbouring positions
- span_order: int32 [16], replicated, may hold values from 0 to 15, each once
- out_weight: bfloat16 [2048, 4096], P('head', 'seq'), may hold values from -0.1875 to 0.1875
Outputs:
- layer_out: bfloat16 [2048, 4096], P('seq', 'head')
All inputs are finite; a program needn't handle non-finite values.
Results may differ from a plain program's by a relative error of at most 0.012.
Values may be sent and summed in bfloat16 or wider, within the bound.
No kernel may reach another device: no remote copies, remote signals or barrier semaphores. Data moves between devices by JAX's collectives and lax.ppermute only.
A program may use at most 64 MiB of HBM per device.

v0:
```python
import functools
import math

import jax
import jax.numpy as jnp
from jax import lax
from jax.experimental import pallas as pl
from jax.experimental.pallas import tpu as pltpu
from jax.sharding import PartitionSpec as P


DH = 128
LANES = 128
NONE = -1000
VMEM = pl.BlockSpec(memory_space=pltpu.VMEM)
SMEM = pl.BlockSpec(memory_space=pltpu.SMEM)
NONE = 15


def limit(mib):
    return pltpu.CompilerParams(vmem_limit_bytes=mib * 2**20)


def lookup(values, index):
    words = []
    for i in range(0, len(values), 8):
        word = sum(v << 4 * k for k, v in enumerate(values[i : i + 8]))
        words.append(word - 2**32 if word >= 2**31 else word)
    word = jnp.int32(words[0])
    for i in range(1, len(words)):
        word = jnp.where(index // 8 == i, jnp.int32(words[i]), word)
    return (word >> (4 * (index % 8))) & 15


def ring_order(n):
    return list(range(0, n, 2)) + list(range(n - 1, 0, -2))


def attention_kernel(n, span, group, sources, order_ref, docid_ref, docs_ref, q_ref, *rest):
    kv_refs, (out_ref, s_ref, m_ref, l_ref, acc_ref) = rest[:n], rest[n:]
    base2 = math.log2(math.e) / math.sqrt(DH)
    mine = lax.axis_index("seq")
    dims = (((1,), (1,)), ((), ()))
    kposs = []
    for i in range(n):
        source = lookup([row[i] for row in sources], mine)
        kposs += [order_ref[2 * source], order_ref[2 * source + 1]]

    for part in range(2):
        rows = pl.ds(part * span, span)
        qpos = order_ref[2 * mine + part]
        q = jnp.concatenate(
            [q_ref[rows, h * DH : (h + 1) * DH] for h in range(group)], axis=0
        )
        qdoc = jnp.transpose(
            jnp.broadcast_to(docs_ref[pl.ds(qpos, 1), :], (span, span)).astype(jnp.float32)
        )
        qfirst = docid_ref[qpos * span]
        ahead = lax.broadcasted_iota(jnp.int32, (span, span), 1) - lax.broadcasted_iota(
            jnp.int32, (span, span), 0
        )
        m_ref[...] = jnp.full_like(m_ref, -1e30)
        l_ref[...] = jnp.zeros_like(l_ref)
        acc_ref[...] = jnp.zeros_like(acc_ref)
        lives = [(k <= qpos) & (docid_ref[k * span + span - 1] >= qfirst) for k in kposs]

        for j in range(2 * n):

            @pl.when(lives[j])
            def _():
                k = kv_refs[j // 2][(j % 2) * span : (j % 2 + 1) * span, :DH]
                s = lax.dot_general(q, k, dims, preferred_element_type=jnp.float32)
                kdoc = docs_ref[pl.ds(kposs[j], 1), :].astype(jnp.float32)
                visible = (qdoc == kdoc) & (ahead <= (qpos - kposs[j]) * span)
                s = jnp.where(visible[None], s.reshape(group, span, span), -1e30)
                s = s.reshape(group * span, span)
                s_ref[:, j * span : (j + 1) * span] = s
                m_ref[...] = jnp.maximum(m_ref[...], s)

        largest = jnp.max(m_ref[...], axis=1, keepdims=True) * base2

        for j in range(2 * n):

            @pl.when(lives[j])
            def _():
                p = jnp.exp2(s_ref[:, j * span : (j + 1) * span] * base2 - largest)
                l_ref[...] += p
                v = kv_refs[j // 2][(j % 2) * span : (j % 2 + 1) * span, DH:]
                acc_ref[...] += jnp.dot(
                    p.astype(jnp.bfloat16), v, preferred_element_type=jnp.float32
                )

        total = jnp.sum(l_ref[...], axis=1, keepdims=True)
        attended = (acc_ref[...] / total).astype(jnp.bfloat16)
        for h in range(group):
            out_ref[rows, h * DH : (h + 1) * DH] = attended[h * span : (h + 1) * span]


def place():
    return lax.axis_index("seq") * lax.axis_size("head") + lax.axis_index("head")


def project_kernel(codes, per, a_ref, b_ref, *rest):
    w_refs, out_refs = rest[: 2 * len(codes)], rest[2 * len(codes) :]
    me = place()
    for i, values in enumerate(codes):
        at = lookup(values, me)
        c = jnp.dot(a_ref[...], w_refs[2 * i][...], preferred_element_type=jnp.float32)
        c += jnp.dot(b_ref[...], w_refs[2 * i + 1][...], preferred_element_type=jnp.float32)
        c = c.astype(jnp.bfloat16)
        for k, out_ref in enumerate(out_refs):

            @pl.when((at >= k * per) & (at < (k + 1) * per))
            def _():
                out_ref[at - k * per] = c


def finish_kernel(codes, heads, *rest):
    out_ref = rest[-1]
    me = place()
    core = lax.axis_index("head") & 1
    for r, slots in enumerate(codes):
        shares = rest[heads * r : heads * (r + 1)]
        for i, values in enumerate(slots):
            part = lookup(values, me)

            @pl.when(part != NONE)
            def _():
                width = shares[0].shape[2]
                for side in range(2):
                    c = shares[side][i].astype(jnp.float32)
                    for k in range(2 + side, heads, 2):
                        c += shares[k][i].astype(jnp.float32)
                    start = pl.multiple_of((2 * part + (core ^ side)) * width, LANES)
                    out_ref[:, pl.ds(start, width)] = c.astype(out_ref.dtype)


def reduce_plan(n, heads, sources, rounds):
    per = n // heads
    devices = [(s, h) for s in range(n) for h in range(heads)]
    plan = []
    for places in rounds:
        codes, pairs = [[] for _ in places], [[] for _ in range(heads)]
        owned = {d: [] for d in devices}
        for s, h in devices:
            counts = [0] * heads
            for i, p in enumerate(places):
                block = sources[s][p]
                k = (block // per) ^ h
                codes[i].append(k * per + counts[k])
                counts[k] += 1
                if not k:
                    owned[s, h].append(block % per)
            for k in range(heads):
                if counts[k]:
                    pairs[k].append((s * heads + h, s * heads + (h ^ k)))
        count = max(len(v) for v in owned.values())
        ends = [[v[i] if i < len(v) else NONE for v in owned.values()] for i in range(count)]
        plan.append((codes, pairs, count, ends))
    return plan


def ring_device(n, heads, queries, keys, values, doc_ids, span_order, out_weight):
    tok_rows = queries.shape[0]
    span = tok_rows // 2
    group = queries.shape[1] // DH
    width = out_weight.shape[1]
    per = n // heads
    hops = n // 2
    ring = ring_order(n)
    where = {s: i for i, s in enumerate(ring)}
    sources = []
    for s in range(n):
        row = [s]
        for hop in range(1, hops):
            row += [ring[(where[s] - hop) % n], ring[(where[s] + hop) % n]]
        sources.append(row + [ring[(where[s] + hops) % n]])

    def gather(pieces):
        def move(way, x):
            step = 1 if way == "up" else -1
            pairs = [(ring[p], ring[(p + step) % n]) for p in range(n)]
            return lax.ppermute(x, "seq", pairs)

        ups, downs = list(pieces), list(pieces)
        late = (len(pieces) + 1) // 2
        got = [list(pieces)]
        for hop in range(1, hops + 1):
            last = hop == hops
            for i in range(len(pieces)):
                if not last or i < late:
                    ups[i] = move("up", ups[i])
                if not last or i >= late:
                    downs[i] = move("dn", downs[i])
            if last:
                got.append(ups[:late] + downs[late:])
            else:
                got += [list(ups), list(downs)]
        return got

    both = jnp.concatenate([keys, values], axis=1)
    kv = [g[0] for g in gather([both])]
    out_weight, both = lax.optimization_barrier((out_weight, both))
    half = width // 2
    first = (lax.axis_index("head") & 1) == 0
    mine = jnp.where(first, out_weight[:, :half], out_weight[:, half:])
    other = jnp.where(first, out_weight[:, half:], out_weight[:, :half])
    beside = [(h, h ^ 1) for h in range(heads)]
    other = lax.ppermute(other, "head", beside)
    w = gather([mine, other])

    attended = pl.pallas_call(
        functools.partial(attention_kernel, n, span, group, sources),
        out_shape=jax.ShapeDtypeStruct((tok_rows, group * DH), jnp.bfloat16),
        in_specs=[SMEM, SMEM] + [VMEM] * (2 + n),
        out_specs=VMEM,
        scratch_shapes=[
            pltpu.VMEM((group * span, 2 * n * span), jnp.float32),
            pltpu.VMEM((group * span, span), jnp.float32),
            pltpu.VMEM((group * span, span), jnp.float32),
            pltpu.VMEM((group * span, DH), jnp.float32),
        ],
        compiler_params=limit(16),
        cost_estimate=pl.CostEstimate(
            flops=4 * group * tok_rows * n * tok_rows * DH,
            bytes_accessed=n * tok_rows * 4 * DH,
            transcendentals=group * tok_rows * n * tok_rows,
        ),
        name="attention",
    )(span_order, doc_ids, doc_ids.reshape(-1, span), queries, *kv)
    paired = lax.ppermute(attended, "head", beside)

    rounds = [list(range(n - 3)), [n - 3, n - 2], [n - 1]]
    shares, ends = [], []
    for r, (codes, pairs, count, end) in enumerate(reduce_plan(n, heads, sources, rounds)):
        pieces = [piece for p in rounds[r] for piece in w[p]]
        block = jax.ShapeDtypeStruct((count, tok_rows, half), jnp.bfloat16)
        made = pl.pallas_call(
            functools.partial(project_kernel, codes, per),
            out_shape=(block,) * heads,
            in_specs=[VMEM] * (2 + len(pieces)),
            out_specs=(VMEM,) * heads,
            compiler_params=limit(8),
            cost_estimate=pl.CostEstimate(
                flops=2 * tok_rows * group * DH * half * len(pieces),
                bytes_accessed=2 * group * DH * half * len(pieces),
                transcendentals=0,
            ),
            name="project",
        )(attended, paired, *pieces)
        shares.append(made[0])
        for k in range(1, heads):
            shares.append(lax.ppermute(made[k], ("seq", "head"), pairs[k]))
        ends.append(end)

    return pl.pallas_call(
        functools.partial(finish_kernel, ends, heads),
        out_shape=jax.ShapeDtypeStruct((tok_rows, per * width), jnp.bfloat16),
        in_specs=[VMEM] * len(shares),
        out_specs=VMEM,
        compiler_params=limit(8),
        name="finish",
    )(*shares)


def on_device(queries, keys, values, doc_ids, span_order, out_weight):
    tok_rows = queries.shape[0]
    span = tok_rows // 2
    local_heads = queries.shape[1] // DH
    local_kv = keys.shape[1] // DH
    group_size = local_heads // local_kv
    n_blocks = span_order.shape[0]
    scale = 1.0 / math.sqrt(DH)
    mine = lax.axis_index("seq")
    own_blocks = lax.dynamic_slice_in_dim(span_order, 2 * mine, 2, 0)
    local_rows = jnp.arange(tok_rows, dtype=jnp.int32)
    qpos = jnp.where(local_rows < span, own_blocks[0], own_blocks[1]) * span + local_rows % span
    qdoc = jnp.take(doc_ids, qpos)
    q_heads = queries.reshape(tok_rows, local_kv, group_size, DH)

    def update(state, kblk, vblk, kpos, kdoc):
        largest, total, summed = state
        count = kblk.shape[0]
        k_heads = kblk.reshape(count, local_kv, DH)
        v_heads = vblk.reshape(count, local_kv, DH)
        scores = (
            jnp.einsum("qhgd,khd->hgqk", q_heads, k_heads, preferred_element_type=jnp.float32)
            * scale
        )
        visible = (qdoc[:, None] == kdoc[None, :]) & (kpos[None, :] <= qpos[:, None])
        masked = jnp.where(visible, scores, jnp.float32(-1e30))
        new_largest = jnp.maximum(largest, jnp.max(masked, axis=-1))
        factor = jnp.exp(largest - new_largest)
        weights = jnp.where(visible, jnp.exp(masked - new_largest[..., None]), jnp.float32(0.0))
        total = total * factor + jnp.sum(weights, axis=-1)
        weights_b = weights.astype(jnp.bfloat16)
        added = jnp.einsum("hgqk,khd->qhgd", weights_b, v_heads, preferred_element_type=jnp.float32)
        summed = summed * jnp.transpose(factor, (2, 0, 1))[..., None] + added
        return (new_largest, total, summed)

    initial = (
        jnp.full((local_kv, group_size, tok_rows), -1e30, jnp.float32),
        jnp.zeros((local_kv, group_size, tok_rows), jnp.float32),
        jnp.zeros((tok_rows, local_kv, group_size, DH), jnp.float32),
    )
    state = initial
    kpiece = lax.all_gather(keys, "seq", axis=0, tiled=True)
    vpiece = lax.all_gather(values, "seq", axis=0, tiled=True)
    count = kpiece.shape[0]
    width = math.gcd(count, 1024)
    steps = count // width
    rows = jnp.arange(count, dtype=jnp.int32)
    match = (rows // span)[:, None] == jnp.arange(n_blocks, dtype=jnp.int32)[None, :]
    owner = jnp.sum(jnp.where(match, span_order[None, :], 0), axis=1)
    kpos = owner * span + rows % span
    kdoc = jnp.take(doc_ids, kpos)
    kparts = kpiece.reshape(steps, width, kpiece.shape[1])
    vparts = vpiece.reshape(steps, width, vpiece.shape[1])

    def one_step(carry, items):
        kblk, vblk, pblk, dblk = items
        carry = update(carry, kblk, vblk, pblk, dblk)
        return (carry, None)

    state, _ = lax.scan(
        one_step, state, (kparts, vparts, kpos.reshape(steps, width), kdoc.reshape(steps, width))
    )
    _, total, summed = state
    attended = (summed / jnp.transpose(total, (2, 0, 1))[..., None]).astype(jnp.bfloat16)
    attended = attended.reshape(tok_rows, local_heads * DH)
    partial_out = jnp.dot(
        attended,
        lax.all_gather(out_weight, "seq", axis=1, tiled=True),
        preferred_element_type=jnp.float32,
    )
    return lax.psum_scatter(
        partial_out.astype(jnp.bfloat16), "head", scatter_dimension=1, tiled=True
    )


def solution(mesh):
    n, heads = mesh.shape["seq"], mesh.shape["head"]

    def on_each(queries, keys, values, doc_ids, span_order, out_weight):
        span = queries.shape[0] // 2
        ring = (
            4 <= n <= 16
            and n % 2 == 0
            and n % heads == 0
            and heads & (heads - 1) == 0
            and keys.shape[1] == DH
            and span % LANES == 0
            and out_weight.shape[1] % (2 * LANES) == 0
        )
        args = (queries, keys, values, doc_ids, span_order, out_weight)
        if not ring:
            return on_device(*args)
        return ring_device(n, heads, *args)

    return jax.shard_map(
        on_each,
        mesh=mesh,
        in_specs=(P("seq", "head"), P("seq", "head"), P("seq", "head"), P(), P(), P("head", "seq")),
        out_specs=P("seq", "head"),
        check_vma=False,
    )
```

profile of v0, /device:TPU:0, one launch (start us, length us, event | category | flops | bytes accessed | tf_op | source)
XLA Modules:
  0.0 79.6 jit_solution(849191330756662380)
XLA Ops:
  2.6 2.6 %collective-permute-start = (bf16[256,256]{1,0:T(8,128)(2,1)S(1)}, bf16[256,256]{1,0:T(8,128)(2,1)S(1)}, u32[]{:S(2)}, u32[]{:S(2)}) collective-permute-start(bf16[256,256]{1,0:T(8,128)(2,1)S(1)} %constant_dynamic-update-slice_fusion.rest_0_), channel_id=1, source_target_pairs={{0,8},{8,16},{16,24},{24,28},{28,20},{20,12},{12,4},{4,0},{1,9},{9... | collective-permute-start | bytes 393224 | tf_op jit(solution)/shard_map/ppermute | solution.py:183
  5.3 1.6 %collective-permute-start.9 = (bf16[512,256]{1,0:T(8,128)(2,1)S(1)}, bf16[512,256]{1,0:T(8,128)(2,1)S(1)}, u32[]{:S(2)}, u32[]{:S(2)}) collective-permute-start(bf16[512,256]{1,0:T(8,128)(2,1)S(1)} %get-tuple-element.32.rest_0_), channel_id=1, source_target_pairs={{0,8},{8,16},{16,24},{24,28},{28,20},{20,12},{12,4},{4,0},{1,9},{9... | collective-permute-start | bytes 786440 | tf_op jit(solution)/shard_map/ppermute | solution.py:183
  8.2 1.6 %collective-permute-start.11 = (bf16[512,256]{1,0:T(8,128)(2,1)S(1)}, bf16[512,256]{1,0:T(8,128)(2,1)S(1)}, u32[]{:S(2)}, u32[]{:S(2)}) collective-permute-start(bf16[512,256]{1,0:T(8,128)(2,1)S(1)} %get-tuple-element.32.rest_0_), channel_id=1, source_target_pairs={{0,4},{8,0},{16,8},{24,16},{28,24},{20,28},{12,20},{4,12},{1,5},{9... | collective-permute-start | bytes 786440 | tf_op jit(solution)/shard_map/ppermute | solution.py:183
  9.8 1.8 %collective-permute-start.2 = (bf16[256,256]{1,0:T(8,128)(2,1)S(1)}, bf16[256,256]{1,0:T(8,128)(2,1)S(1)}, u32[]{:S(2)}, u32[]{:S(2)}) collective-permute-start(bf16[256,256]{1,0:T(8,128)(2,1)S(1)} %collective-permute-done.rest_1_), channel_id=1, source_target_pairs={{0,8},{8,16},{16,24},{24,28},{28,20},{20,12},{12,4},{4,0},{1,9},{9... | collective-permute-start | bytes 393224 | tf_op jit(solution)/shard_map/ppermute | solution.py:183
  11.6 7.2 %collective-permute-done.1.rest_2_ = bf16[256,256]{1,0:T(8,128)(2,1)S(1)} collective-permute-done((bf16[256,256]{1,0:T(8,128)(2,1)S(1)}, bf16[256,256]{1,0:T(8,128)(2,1)S(1)}, u32[]{:S(2)}, u32[]{:S(2)}) %collective-permute-start.1) | collective-permute-done | bytes 131104 | tf_op jit(solution)/shard_map/ppermute | solution.py:183
  19.3 1.6 %collective-permute-start.10 = (bf16[512,256]{1,0:T(8,128)(2,1)S(1)}, bf16[512,256]{1,0:T(8,128)(2,1)S(1)}, u32[]{:S(2)}, u32[]{:S(2)}) collective-permute-start(bf16[512,256]{1,0:T(8,128)(2,1)S(1)} %collective-permute-done.8.rest_1_), channel_id=1, source_target_pairs={{0,8},{8,16},{16,24},{24,28},{28,20},{20,12},{12,4},{4,0},{1,9},{9... | collective-permute-start | bytes 786440 | tf_op jit(solution)/shard_map/ppermute | solution.py:183
  20.9 1.6 %collective-permute-start.13 = (bf16[512,256]{1,0:T(8,128)(2,1)S(1)}, bf16[512,256]{1,0:T(8,128)(2,1)S(1)}, u32[]{:S(2)}, u32[]{:S(2)}) collective-permute-start(bf16[512,256]{1,0:T(8,128)(2,1)S(1)} %collective-permute-done.9.rest_2_), channel_id=1, source_target_pairs={{0,8},{8,16},{16,24},{24,28},{28,20},{20,12},{12,4},{4,0},{1,9},{9... | collective-permute-start | bytes 786440 | tf_op jit(solution)/shard_map/ppermute | solution.py:183
  22.9 4.4 %collective-permute-done.3.rest_4_ = bf16[256,256]{1,0:T(8,128)(2,1)S(1)} collective-permute-done((bf16[256,256]{1,0:T(8,128)(2,1)S(1)}, bf16[256,256]{1,0:T(8,128)(2,1)S(1)}, u32[]{:S(2)}, u32[]{:S(2)}) %collective-permute-start.3) | collective-permute-done | bytes 131104 | tf_op jit(solution)/shard_map/ppermute | solution.py:183
  27.2 1.6 %collective-permute-start.4 = (bf16[256,256]{1,0:T(8,128)(2,1)S(1)}, bf16[256,256]{1,0:T(8,128)(2,1)S(1)}, u32[]{:S(2)}, u32[]{:S(2)}) collective-permute-start(bf16[256,256]{1,0:T(8,128)(2,1)S(1)} %collective-permute-done.2.rest_3_), channel_id=1, source_target_pairs={{0,8},{8,16},{16,24},{24,28},{28,20},{20,12},{12,4},{4,0},{1,9},{9... | collective-permute-start | bytes 393224 | tf_op jit(solution)/shard_map/ppermute | solution.py:183
  29.3 4.9 %collective-permute-done.4.rest_5_ = bf16[256,256]{1,0:T(8,128)(2,1)S(1)} collective-permute-done((bf16[256,256]{1,0:T(8,128)(2,1)S(1)}, bf16[256,256]{1,0:T(8,128)(2,1)S(1)}, u32[]{:S(2)}, u32[]{:S(2)}) %collective-permute-start.4) | collective-permute-done | bytes 131104 | tf_op jit(solution)/shard_map/ppermute | solution.py:183
  34.2 1.6 %collective-permute-start.6 = (bf16[256,256]{1,0:T(8,128)(2,1)S(1)}, bf16[256,256]{1,0:T(8,128)(2,1)S(1)}, u32[]{:S(2)}, u32[]{:S(2)}) collective-permute-start(bf16[256,256]{1,0:T(8,128)(2,1)S(1)} %collective-permute-done.4.rest_5_), channel_id=1, source_target_pairs={{0,8},{8,16},{16,24},{24,28},{28,20},{20,12},{12,4},{4,0},{1,9},{9... | collective-permute-start | bytes 393224 | tf_op jit(solution)/shard_map/ppermute | solution.py:183
  36.2 1.6 %collective-permute-start.14 = (bf16[512,256]{1,0:T(8,128)(2,1)S(1)}, bf16[512,256]{1,0:T(8,128)(2,1)S(1)}, u32[]{:S(2)}, u32[]{:S(2)}) collective-permute-start(bf16[512,256]{1,0:T(8,128)(2,1)S(1)} %collective-permute-done.10.rest_3_), channel_id=1, source_target_pairs={{0,8},{8,16},{16,24},{24,28},{28,20},{20,12},{12,4},{4,0},{1,9},{9... | collective-permute-start | bytes 786440 | tf_op jit(solution)/shard_map/ppermute | solution.py:183
  37.8 1.6 %collective-permute-start.20 = (bf16[512,256]{1,0:T(8,128)(2,1)S(1)}, bf16[512,256]{1,0:T(8,128)(2,1)S(1)}, u32[]{:S(2)}, u32[]{:S(2)}) collective-permute-start(bf16[512,256]{1,0:T(8,128)(2,1)S(1)} %collective-permute-done.13.rest_6_), channel_id=1, source_target_pairs={{0,8},{8,16},{16,24},{24,28},{28,20},{20,12},{12,4},{4,0},{1,9},{9... | collective-permute-start | bytes 786440 | tf_op jit(solution)/shard_map/ppermute | solution.py:183
  40.6 4.3 %attention.1.a_ref = bf16[256,512]{1,0:T(8,128)(2,1)S(1)} custom-call(s32[16]{0:T(128)S(1)} %copy-done.2, s32[2048]{0:T(1024)S(1)} %copy-done.1, s32[16,128]{1,0:T(8,128)S(1)} %bitcast.1, bf16[256,512]{1,0:T(8,128)(2,1)S(1)} %copy-done, bf16[256,256]{1,0:T(8,128)(2,1)S(1)} %constant_dynamic-update-slice_fusion.rest_0_, ...), custom_call_target="tpu_custom_call" | custom-call | flops 1073741824 | bytes 1048576 | tf_op jit(solution)/shard_map/attention/pallas_call | solution.py:212
  44.9 5.3 %collective-permute-start.22 = (bf16[512,256]{1,0:T(8,128)(2,1)S(1)}, bf16[512,256]{1,0:T(8,128)(2,1)S(1)}, u32[]{:S(2)}, u32[]{:S(2)}) collective-permute-start(bf16[512,256]{1,0:T(8,128)(2,1)S(1)} %collective-permute-done.15.rest_8_), channel_id=1, source_target_pairs={{0,4},{8,0},{16,8},{24,16},{28,24},{20,28},{12,20},{4,12},{1,5},{9... | collective-permute-start | bytes 786440 | tf_op jit(solution)/shard_map/ppermute | solution.py:183
  50.6 1.7 %collective-permute-start.28 = (bf16[512,256]{1,0:T(8,128)(2,1)S(1)}, bf16[512,256]{1,0:T(8,128)(2,1)S(1)}, u32[]{:S(2)}, u32[]{:S(2)}) collective-permute-start(bf16[512,256]{1,0:T(8,128)(2,1)S(1)} %collective-permute-done.23.rest_3_), channel_id=1, source_target_pairs={{0,4},{8,0},{16,8},{24,16},{28,24},{20,28},{12,20},{4,12},{1,5},{9... | collective-permute-start | bytes 786440 | tf_op jit(solution)/shard_map/ppermute | solution.py:183
  52.4 2.1 %project.3 = (bf16[2,256,256]{2,1,0:T(8,128)(2,1)S(1)}, bf16[2,256,256]{2,1,0:T(8,128)(2,1)S(1)}, bf16[2,256,256]{2,1,0:T(8,128)(2,1)S(1)}, bf16[2,256,256]{2,1,0:T(8,128)(2,1)S(1)}) custom-call(bf16[256,512]{1,0:T(8,128)(2,1)S(1)} %attention.1.a_ref, bf16[256,512]{1,0:T(8,128)(2,1)S(1)} %collective-permute-done.7.b_ref, ...), custom_call_target="tpu_custom_call" | custom-call | flops 671088640 | bytes 2621440 | tf_op jit(solution)/shard_map/project/pallas_call | solution.py:238
  54.4 1.9 %collective-permute-start.17 = (bf16[2,256,256]{2,1,0:T(8,128)(2,1)S(1)}, bf16[2,256,256]{2,1,0:T(8,128)(2,1)S(1)}, u32[]{:S(2)}, u32[]{:S(2)}) collective-permute-start(bf16[2,256,256]{2,1,0:T(8,128)(2,1)S(1)} %get-tuple-element.20), channel_id=1, source_target_pairs={{0,1},{1,0},{3,2},{4,5},{5,4},{7,6},{8,9},{9,8},{10,11},{11,10},{1... | collective-permute-start | bytes 786440 | tf_op jit(solution)/shard_map/ppermute | solution.py:253
  56.9 3.4 %collective-permute-start.18 = (bf16[2,256,256]{2,1,0:T(8,128)(2,1)S(1)}, bf16[2,256,256]{2,1,0:T(8,128)(2,1)S(1)}, u32[]{:S(2)}, u32[]{:S(2)}) collective-permute-start(bf16[2,256,256]{2,1,0:T(8,128)(2,1)S(1)} %get-tuple-element.21), channel_id=1, source_target_pairs={{0,2},{2,0},{3,1},{4,6},{6,4},{7,5},{8,10},{9,11},{10,8},{11,9},{1... | collective-permute-start | bytes 786440 | tf_op jit(solution)/shard_map/ppermute | solution.py:253
  62.6 1.7 %collective-permute-done.27.rest_0_ = bf16[512,256]{1,0:T(8,128)(2,1)S(1)} collective-permute-done((bf16[512,256]{1,0:T(8,128)(2,1)S(1)}, bf16[512,256]{1,0:T(8,128)(2,1)S(1)}, u32[]{:S(2)}, u32[]{:S(2)}) %collective-permute-start.27) | collective-permute-done | bytes 262176 | tf_op jit(solution)/shard_map/ppermute | solution.py:183
  64.9 4.7 %collective-permute-start.25 = (bf16[1,256,256]{2,1,0:T(8,128)(2,1)S(1)}, bf16[1,256,256]{2,1,0:T(8,128)(2,1)S(1)}, u32[]{:S(2)}, u32[]{:S(2)}) collective-permute-start(bf16[1,256,256]{2,1,0:T(8,128)(2,1)S(1)} %get-tuple-element.25), channel_id=1, source_target_pairs={{0,2},{1,3},{4,6},{5,7},{9,11},{11,9},{13,15},{15,13},{16,18},{18,... | collective-permute-start | bytes 393224 | tf_op jit(solution)/shard_map/ppermute | solution.py:253
  70.0 1.4 %collective-permute-start.26 = (bf16[1,256,256]{2,1,0:T(8,128)(2,1)S(1)}, bf16[1,256,256]{2,1,0:T(8,128)(2,1)S(1)}, u32[]{:S(2)}, u32[]{:S(2)}) collective-permute-start(bf16[1,256,256]{2,1,0:T(8,128)(2,1)S(1)} %get-tuple-element.26), channel_id=1, source_target_pairs={{0,3},{1,2},{4,7},{5,6},{8,11},{10,9},{12,15},{14,13},{17,18},{19,... | collective-permute-start | bytes 393224 | tf_op jit(solution)/shard_map/ppermute | solution.py:253
  72.7 2.5 %collective-permute-start.31 = (bf16[1,256,256]{2,1,0:T(8,128)(2,1)S(1)}, bf16[1,256,256]{2,1,0:T(8,128)(2,1)S(1)}, u32[]{:S(2)}, u32[]{:S(2)}) collective-permute-start(bf16[1,256,256]{2,1,0:T(8,128)(2,1)S(1)} %get-tuple-element.30), channel_id=1, source_target_pairs={{0,3},{4,7},{9,10},{13,14},{18,17},{22,21},{27,24},{31,28}} | collective-permute-start | bytes 393224 | tf_op jit(solution)/shard_map/ppermute | solution.py:253
  76.3 2.3 %collective-permute-done.31.rest_11_ = bf16[1,256,256]{2,1,0:T(8,128)(2,1)S(1)} collective-permute-done((bf16[1,256,256]{2,1,0:T(8,128)(2,1)S(1)}, bf16[1,256,256]{2,1,0:T(8,128)(2,1)S(1)}, u32[]{:S(2)}, u32[]{:S(2)}) %collective-permute-start.31) | collective-permute-done | bytes 131104 | tf_op jit(solution)/shard_map/ppermute | solution.py:253
  (56 shorter events, 14.5 us)
Async XLA Ops:
  2.6 7.2 %collective-permute-start = (bf16[256,256]{1,0:T(8,128)(2,1)S(1)}, bf16[256,256]{1,0:T(8,128)(2,1)S(1)}, u32[]{:S(2)}, u32[]{:S(2)}) collective-permute-start(bf16[256,256]{1,0:T(8,128)(2,1)S(1)} %constant_dynamic-update-slice_fusion.rest_0_), channel_id=1, source_target_pairs={{0,8},{8,16},{16,24},{24,28},{28,20},{20,12},{12,4},{4,0},{1,9},{9... | collective-permute-start | bytes 393224 | tf_op jit(solution)/shard_map/ppermute | solution.py:183
  5.3 15.6 %collective-permute-start.9 = (bf16[512,256]{1,0:T(8,128)(2,1)S(1)}, bf16[512,256]{1,0:T(8,128)(2,1)S(1)}, u32[]{:S(2)}, u32[]{:S(2)}) collective-permute-start(bf16[512,256]{1,0:T(8,128)(2,1)S(1)} %get-tuple-element.32.rest_0_), channel_id=1, source_target_pairs={{0,8},{8,16},{16,24},{24,28},{28,20},{20,12},{12,4},{4,0},{1,9},{9... | collective-permute-start | bytes 786440 | tf_op jit(solution)/shard_map/ppermute | solution.py:183
  6.8 15.6 %collective-permute-start.12 = (bf16[512,256]{1,0:T(8,128)(2,1)S(1)}, bf16[512,256]{1,0:T(8,128)(2,1)S(1)}, u32[]{:S(2)}, u32[]{:S(2)}) collective-permute-start(bf16[512,256]{1,0:T(8,128)(2,1)S(1)} %collective-permute-done.8.rest_1_), channel_id=1, source_target_pairs={{0,4},{8,0},{16,8},{24,16},{28,24},{20,28},{12,20},{4,12},{1,5},{9... | collective-permute-start | bytes 786440 | tf_op jit(solution)/shard_map/ppermute | solution.py:183
  7.3 11.5 %collective-permute-start.1 = (bf16[256,256]{1,0:T(8,128)(2,1)S(1)}, bf16[256,256]{1,0:T(8,128)(2,1)S(1)}, u32[]{:S(2)}, u32[]{:S(2)}) collective-permute-start(bf16[256,256]{1,0:T(8,128)(2,1)S(1)} %constant_dynamic-update-slice_fusion.rest_0_), channel_id=1, source_target_pairs={{0,4},{8,0},{16,8},{24,16},{28,24},{20,28},{12,20},{4,12},{1,5},{9... | collective-permute-start | bytes 393224 | tf_op jit(solution)/shard_map/ppermute | solution.py:183
  8.2 20.6 %collective-permute-start.11 = (bf16[512,256]{1,0:T(8,128)(2,1)S(1)}, bf16[512,256]{1,0:T(8,128)(2,1)S(1)}, u32[]{:S(2)}, u32[]{:S(2)}) collective-permute-start(bf16[512,256]{1,0:T(8,128)(2,1)S(1)} %get-tuple-element.32.rest_0_), channel_id=1, source_target_pairs={{0,4},{8,0},{16,8},{24,16},{28,24},{20,28},{12,20},{4,12},{1,5},{9... | collective-permute-start | bytes 786440 | tf_op jit(solution)/shard_map/ppermute | solution.py:183
  9.8 9.5 %collective-permute-start.2 = (bf16[256,256]{1,0:T(8,128)(2,1)S(1)}, bf16[256,256]{1,0:T(8,128)(2,1)S(1)}, u32[]{:S(2)}, u32[]{:S(2)}) collective-permute-start(bf16[256,256]{1,0:T(8,128)(2,1)S(1)} %collective-permute-done.rest_1_), channel_id=1, source_target_pairs={{0,8},{8,16},{16,24},{24,28},{28,20},{20,12},{12,4},{4,0},{1,9},{9... | collective-permute-start | bytes 393224 | tf_op jit(solution)/shard_map/ppermute | solution.py:183
  18.8 8.4 %collective-permute-start.3 = (bf16[256,256]{1,0:T(8,128)(2,1)S(1)}, bf16[256,256]{1,0:T(8,128)(2,1)S(1)}, u32[]{:S(2)}, u32[]{:S(2)}) collective-permute-start(bf16[256,256]{1,0:T(8,128)(2,1)S(1)} %collective-permute-done.1.rest_2_), channel_id=1, source_target_pairs={{0,4},{8,0},{16,8},{24,16},{28,24},{20,28},{12,20},{4,12},{1,5},{9... | collective-permute-start | bytes 393224 | tf_op jit(solution)/shard_map/ppermute | solution.py:183
  19.3 17.0 %collective-permute-start.10 = (bf16[512,256]{1,0:T(8,128)(2,1)S(1)}, bf16[512,256]{1,0:T(8,128)(2,1)S(1)}, u32[]{:S(2)}, u32[]{:S(2)}) collective-permute-start(bf16[512,256]{1,0:T(8,128)(2,1)S(1)} %collective-permute-done.8.rest_1_), channel_id=1, source_target_pairs={{0,8},{8,16},{16,24},{24,28},{28,20},{20,12},{12,4},{4,0},{1,9},{9... | collective-permute-start | bytes 786440 | tf_op jit(solution)/shard_map/ppermute | solution.py:183
  20.9 16.9 %collective-permute-start.13 = (bf16[512,256]{1,0:T(8,128)(2,1)S(1)}, bf16[512,256]{1,0:T(8,128)(2,1)S(1)}, u32[]{:S(2)}, u32[]{:S(2)}) collective-permute-start(bf16[512,256]{1,0:T(8,128)(2,1)S(1)} %collective-permute-done.9.rest_2_), channel_id=1, source_target_pairs={{0,8},{8,16},{16,24},{24,28},{28,20},{20,12},{12,4},{4,0},{1,9},{9... | collective-permute-start | bytes 786440 | tf_op jit(solution)/shard_map/ppermute | solution.py:183
  22.4 16.9 %collective-permute-start.16 = (bf16[512,256]{1,0:T(8,128)(2,1)S(1)}, bf16[512,256]{1,0:T(8,128)(2,1)S(1)}, u32[]{:S(2)}, u32[]{:S(2)}) collective-permute-start(bf16[512,256]{1,0:T(8,128)(2,1)S(1)} %collective-permute-done.12.rest_5_), channel_id=1, source_target_pairs={{0,4},{8,0},{16,8},{24,16},{28,24},{20,28},{12,20},{4,12},{1,5},{9... | collective-permute-start | bytes 786440 | tf_op jit(solution)/shard_map/ppermute | solution.py:183
  35.8 9.2 %collective-permute-start.15 = (bf16[512,256]{1,0:T(8,128)(2,1)S(1)}, bf16[512,256]{1,0:T(8,128)(2,1)S(1)}, u32[]{:S(2)}, u32[]{:S(2)}) collective-permute-start(bf16[512,256]{1,0:T(8,128)(2,1)S(1)} %collective-permute-done.11.rest_4_), channel_id=1, source_target_pairs={{0,4},{8,0},{16,8},{24,16},{28,24},{20,28},{12,20},{4,12},{1,5},{9... | collective-permute-start | bytes 786440 | tf_op jit(solution)/shard_map/ppermute | solution.py:183
  36.2 14.0 %collective-permute-start.14 = (bf16[512,256]{1,0:T(8,128)(2,1)S(1)}, bf16[512,256]{1,0:T(8,128)(2,1)S(1)}, u32[]{:S(2)}, u32[]{:S(2)}) collective-permute-start(bf16[512,256]{1,0:T(8,128)(2,1)S(1)} %collective-permute-done.10.rest_3_), channel_id=1, source_target_pairs={{0,8},{8,16},{16,24},{24,28},{28,20},{20,12},{12,4},{4,0},{1,9},{9... | collective-permute-start | bytes 786440 | tf_op jit(solution)/shard_map/ppermute | solution.py:183
  37.8 12.5 %collective-permute-start.20 = (bf16[512,256]{1,0:T(8,128)(2,1)S(1)}, bf16[512,256]{1,0:T(8,128)(2,1)S(1)}, u32[]{:S(2)}, u32[]{:S(2)}) collective-permute-start(bf16[512,256]{1,0:T(8,128)(2,1)S(1)} %collective-permute-done.13.rest_6_), channel_id=1, source_target_pairs={{0,8},{8,16},{16,24},{24,28},{28,20},{20,12},{12,4},{4,0},{1,9},{9... | collective-permute-start | bytes 786440 | tf_op jit(solution)/shard_map/ppermute | solution.py:183
  39.4 11.2 %collective-permute-start.23 = (bf16[512,256]{1,0:T(8,128)(2,1)S(1)}, bf16[512,256]{1,0:T(8,128)(2,1)S(1)}, u32[]{:S(2)}, u32[]{:S(2)}) collective-permute-start(bf16[512,256]{1,0:T(8,128)(2,1)S(1)} %collective-permute-done.16.rest_9_), channel_id=1, source_target_pairs={{0,4},{8,0},{16,8},{24,16},{28,24},{20,28},{12,20},{4,12},{1,5},{9... | collective-permute-start | bytes 786440 | tf_op jit(solution)/shard_map/ppermute | solution.py:183
  44.9 7.5 %collective-permute-start.7 = (bf16[256,512]{1,0:T(8,128)(2,1)S(1)}, bf16[256,512]{1,0:T(8,128)(2,1)S(1)}, u32[]{:S(2)}, u32[]{:S(2)}) collective-permute-start(bf16[256,512]{1,0:T(8,128)(2,1)S(1)} %attention.1.a_ref), channel_id=1, source_target_pairs={{0,1},{1,0},{2,3},{3,2},{4,5},{5,4},{6,7},{7,6},{8,9},{9,8},{10,11... | collective-permute-start | bytes 786440 | tf_op jit(solution)/shard_map/ppermute | solution.py:231
  44.9 12.0 %collective-permute-start.22 = (bf16[512,256]{1,0:T(8,128)(2,1)S(1)}, bf16[512,256]{1,0:T(8,128)(2,1)S(1)}, u32[]{:S(2)}, u32[]{:S(2)}) collective-permute-start(bf16[512,256]{1,0:T(8,128)(2,1)S(1)} %collective-permute-done.15.rest_8_), channel_id=1, source_target_pairs={{0,4},{8,0},{16,8},{24,16},{28,24},{20,28},{12,20},{4,12},{1,5},{9... | collective-permute-start | bytes 786440 | tf_op jit(solution)/shard_map/ppermute | solution.py:183
  50.3 10.1 %collective-permute-start.21 = (bf16[512,256]{1,0:T(8,128)(2,1)S(1)}, bf16[512,256]{1,0:T(8,128)(2,1)S(1)}, u32[]{:S(2)}, u32[]{:S(2)}) collective-permute-start(bf16[512,256]{1,0:T(8,128)(2,1)S(1)} %collective-permute-done.14.rest_7_), channel_id=1, source_target_pairs={{0,8},{8,16},{16,24},{24,28},{28,20},{20,12},{12,4},{4,0},{1,9},{9... | collective-permute-start | bytes 786440 | tf_op jit(solution)/shard_map/ppermute | solution.py:183
  50.3 14.0 %collective-permute-start.27 = (bf16[512,256]{1,0:T(8,128)(2,1)S(1)}, bf16[512,256]{1,0:T(8,128)(2,1)S(1)}, u32[]{:S(2)}, u32[]{:S(2)}) collective-permute-start(bf16[512,256]{1,0:T(8,128)(2,1)S(1)} %collective-permute-done.20.rest_0_), channel_id=1, source_target_pairs={{0,8},{8,16},{16,24},{24,28},{28,20},{20,12},{12,4},{4,0},{1,9},{9... | collective-permute-start | bytes 786440 | tf_op jit(solution)/shard_map/ppermute | solution.py:183
  50.6 14.3 %collective-permute-start.28 = (bf16[512,256]{1,0:T(8,128)(2,1)S(1)}, bf16[512,256]{1,0:T(8,128)(2,1)S(1)}, u32[]{:S(2)}, u32[]{:S(2)}) collective-permute-start(bf16[512,256]{1,0:T(8,128)(2,1)S(1)} %collective-permute-done.23.rest_3_), channel_id=1, source_target_pairs={{0,4},{8,0},{16,8},{24,16},{28,24},{20,28},{12,20},{4,12},{1,5},{9... | collective-permute-start | bytes 786440 | tf_op jit(solution)/shard_map/ppermute | solution.py:183
  54.4 15.5 %collective-permute-start.17 = (bf16[2,256,256]{2,1,0:T(8,128)(2,1)S(1)}, bf16[2,256,256]{2,1,0:T(8,128)(2,1)S(1)}, u32[]{:S(2)}, u32[]{:S(2)}) collective-permute-start(bf16[2,256,256]{2,1,0:T(8,128)(2,1)S(1)} %get-tuple-element.20), channel_id=1, source_target_pairs={{0,1},{1,0},{3,2},{4,5},{5,4},{7,6},{8,9},{9,8},{10,11},{11,10},{1... | collective-permute-start | bytes 786440 | tf_op jit(solution)/shard_map/ppermute | solution.py:253
  56.9 14.4 %collective-permute-start.18 = (bf16[2,256,256]{2,1,0:T(8,128)(2,1)S(1)}, bf16[2,256,256]{2,1,0:T(8,128)(2,1)S(1)}, u32[]{:S(2)}, u32[]{:S(2)}) collective-permute-start(bf16[2,256,256]{2,1,0:T(8,128)(2,1)S(1)} %get-tuple-element.21), channel_id=1, source_target_pairs={{0,2},{2,0},{3,1},{4,6},{6,4},{7,5},{8,10},{9,11},{10,8},{11,9},{1... | collective-permute-start | bytes 786440 | tf_op jit(solution)/shard_map/ppermute | solution.py:253
  60.4 11.7 %collective-permute-start.19 = (bf16[2,256,256]{2,1,0:T(8,128)(2,1)S(1)}, bf16[2,256,256]{2,1,0:T(8,128)(2,1)S(1)}, u32[]{:S(2)}, u32[]{:S(2)}) collective-permute-start(bf16[2,256,256]{2,1,0:T(8,128)(2,1)S(1)} %get-tuple-element.22), channel_id=1, source_target_pairs={{1,2},{2,1},{3,0},{5,6},{6,5},{7,4},{8,11},{9,10},{10,9},{11,8},{1... | collective-permute-start | bytes 786440 | tf_op jit(solution)/shard_map/ppermute | solution.py:253
  64.2 8.5 %collective-permute-start.24 = (bf16[1,256,256]{2,1,0:T(8,128)(2,1)S(1)}, bf16[1,256,256]{2,1,0:T(8,128)(2,1)S(1)}, u32[]{:S(2)}, u32[]{:S(2)}) collective-permute-start(bf16[1,256,256]{2,1,0:T(8,128)(2,1)S(1)} %get-tuple-element.24), channel_id=1, source_target_pairs={{2,3},{3,2},{6,7},{7,6},{8,9},{10,11},{12,13},{14,15},{17,16},{19,... | collective-permute-start | bytes 393224 | tf_op jit(solution)/shard_map/ppermute | solution.py:253
  64.9 10.4 %collective-permute-start.25 = (bf16[1,256,256]{2,1,0:T(8,128)(2,1)S(1)}, bf16[1,256,256]{2,1,0:T(8,128)(2,1)S(1)}, u32[]{:S(2)}, u32[]{:S(2)}) collective-permute-start(bf16[1,256,256]{2,1,0:T(8,128)(2,1)S(1)} %get-tuple-element.25), channel_id=1, source_target_pairs={{0,2},{1,3},{4,6},{5,7},{9,11},{11,9},{13,15},{15,13},{16,18},{18,... | collective-permute-start | bytes 393224 | tf_op jit(solution)/shard_map/ppermute | solution.py:253
  (12 other events, 161.9 us)
where the time goes:
time: 79.9 us; the launch traced here: 79.6 us
  starting transfers between devices  45.9 us (57%)
  waiting for transfers between devices  22.9 us (29%)
  Pallas kernels  8.45 us (11%)
  other arithmetic  1.11 us (1%)
  local copies, waits for them, and re-layouts  0.92 us (1%)
    ppermute x21, starting transfers between devices, move(): return lax.ppermute(x, 'seq', pairs)  28.1 us
    ppermute x21, waiting for transfers between devices, move(): return lax.ppermute(x, 'seq', pairs)  19.6 us
    ppermute x9, starting transfers between devices, ring_device(): shares.append(lax.ppermute(made[k], ('seq', 'head'), pairs[k]))  17.2 us
    pallas_call x1, Pallas kernels, ring_device(): pl.pallas_call(functools.partial(attention_kernel, n, span, group, source...  4.27 us
    ppermute x9, waiting for transfers between devices, ring_device(): shares.append(lax.ppermute(made[k], ('seq', 'head'), pairs[k]))  3.33 us
    pallas_call x3, Pallas kernels, ring_device(): pl.pallas_call(functools.partial(project_kernel, codes, per), out_shape=(...  3.25 us
  transfers between devices with their start and end apart: 32, of which 8 were waited for; matrix products, arithmetic and copies ran while one was open for 0% of the time, Pallas kernels for 9%

commit v1 on v0

--- a/solution.py
+++ b/solution.py
@@ -14,7 +14,7 @@
 NONE = -1000
 VMEM = pl.BlockSpec(memory_space=pltpu.VMEM)
 SMEM = pl.BlockSpec(memory_space=pltpu.SMEM)
-NONE = 15
+NONE, KEEP = 15, 8
 
 
 def limit(mib):
@@ -36,13 +36,18 @@
     return list(range(0, n, 2)) + list(range(n - 1, 0, -2))
 
 
-def attention_kernel(n, span, group, sources, order_ref, docid_ref, docs_ref, q_ref, *rest):
-    kv_refs, (out_ref, s_ref, m_ref, l_ref, acc_ref) = rest[:n], rest[n:]
+def attention_kernel(span, group, sources, first, order_ref, docid_ref, docs_ref, q_ref, *rest):
+    many = len(sources[0])
+    kv_refs, rest = rest[:many], rest[many:]
+    if first:
+        top_ref, sum_ref, mix_ref, s_ref, m_ref = rest
+    else:
+        top_in, sum_in, mix_in, out_ref, s_ref, m_ref, sum_ref, mix_ref = rest
     base2 = math.log2(math.e) / math.sqrt(DH)
     mine = lax.axis_index("seq")
     dims = (((1,), (1,)), ((), ()))
     kposs = []
-    for i in range(n):
+    for i in range(many):
         source = lookup([row[i] for row in sources], mine)
         kposs += [order_ref[2 * source], order_ref[2 * source + 1]]
 
@@ -60,11 +65,9 @@
             jnp.int32, (span, span), 0
         )
         m_ref[...] = jnp.full_like(m_ref, -1e30)
-        l_ref[...] = jnp.zeros_like(l_ref)
-        acc_ref[...] = jnp.zeros_like(acc_ref)
         lives = [(k <= qpos) & (docid_ref[k * span + span - 1] >= qfirst) for k in kposs]
 
-        for j in range(2 * n):
+        for j in range(2 * many):
 
             @pl.when(lives[j])
             def _():
@@ -78,61 +81,85 @@
                 m_ref[...] = jnp.maximum(m_ref[...], s)
 
         largest = jnp.max(m_ref[...], axis=1, keepdims=True) * base2
-
-        for j in range(2 * n):
+        if first:
+            top_ref[part] = jnp.broadcast_to(largest, m_ref.shape)
+            sum_ref[part] = jnp.zeros_like(m_ref)
+            mix_ref[part] = jnp.zeros_like(m_ref)
+        else:
+            before = top_in[part]
+            largest = jnp.maximum(before, largest)
+            fade = jnp.exp2(before - largest)
+            sum_ref[part] = sum_in[part] * fade
+            mix_ref[part] = mix_in[part] * fade
+
+        for j in range(2 * many):
 
             @pl.when(lives[j])
             def _():
                 p = jnp.exp2(s_ref[:, j * span : (j + 1) * span] * base2 - largest)
-                l_ref[...] += p
+                sum_ref[part] += p
                 v = kv_refs[j // 2][(j % 2) * span : (j % 2 + 1) * span, DH:]
-                acc_ref[...] += jnp.dot(
+                mix_ref[part] += jnp.dot(
                     p.astype(jnp.bfloat16), v, preferred_element_type=jnp.float32
                 )
 
-        total = jnp.sum(l_ref[...], axis=1, keepdims=True)
-        attended = (acc_ref[...] / total).astype(jnp.bfloat16)
-        for h in range(group):
-            out_ref[rows, h * DH : (h + 1) * DH] = attended[h * span : (h + 1) * span]
+        if not first:
+            total = jnp.sum(sum_ref[part], axis=1, keepdims=True)
+            attended = (mix_ref[part] / total).astype(jnp.bfloat16)
+            for h in range(group):
+                out_ref[rows, h * DH : (h + 1) * DH] = attended[h * span : (h + 1) * span]
 
 
 def place():
     return lax.axis_index("seq") * lax.axis_size("head") + lax.axis_index("head")
 
 
-def project_kernel(codes, per, a_ref, b_ref, *rest):
-    w_refs, out_refs = rest[: 2 * len(codes)], rest[2 * len(codes) :]
+def project_kernel(codes, a_ref, b_ref, *rest):
+    w_refs, (send_ref, keep_ref) = rest[:-2], rest[-2:]
     me = place()
     for i, values in enumerate(codes):
         at = lookup(values, me)
         c = jnp.dot(a_ref[...], w_refs[2 * i][...], preferred_element_type=jnp.float32)
         c += jnp.dot(b_ref[...], w_refs[2 * i + 1][...], preferred_element_type=jnp.float32)
         c = c.astype(jnp.bfloat16)
-        for k, out_ref in enumerate(out_refs):
-
-            @pl.when((at >= k * per) & (at < (k + 1) * per))
+
+        @pl.when(at < KEEP)
+        def _():
+            send_ref[at] = c
+
+        @pl.when(at >= KEEP)
+        def _():
+            keep_ref[at - KEEP] = c
+
+
+def fold_kernel(codes, per, *rest):
+    kept, came, (own_ref, send_ref) = rest[: len(codes)], rest[len(codes) : -2], rest[-2:]
+    me = place()
+    for r, slots in enumerate(codes):
+        for i, values in enumerate(slots):
+            at = lookup(values, me)
+
+            @pl.when(at != NONE)
             def _():
-                out_ref[at - k * per] = c
-
-
-def finish_kernel(codes, heads, *rest):
-    out_ref = rest[-1]
-    me = place()
+                c = kept[r][i].astype(jnp.float32) + came[r][i].astype(jnp.float32)
+                c = c.astype(jnp.bfloat16)
+
+                @pl.when(at < per)
+                def _():
+                    own_ref[at] = c
+
+                @pl.when(at >= per)
+                def _():
+                    send_ref[at - per] = c
+
+
+def finish_kernel(own_ref, came_ref, out_ref):
     core = lax.axis_index("head") & 1
-    for r, slots in enumerate(codes):
-        shares = rest[heads * r : heads * (r + 1)]
-        for i, values in enumerate(slots):
-            part = lookup(values, me)
-
-            @pl.when(part != NONE)
-            def _():
-                width = shares[0].shape[2]
-                for side in range(2):
-                    c = shares[side][i].astype(jnp.float32)
-                    for k in range(2 + side, heads, 2):
-                        c += shares[k][i].astype(jnp.float32)
-                    start = pl.multiple_of((2 * part + (core ^ side)) * width, LANES)
-                    out_ref[:, pl.ds(start, width)] = c.astype(out_ref.dtype)
+    per, _, half = own_ref.shape
+    for part in range(per):
+        for ref, side in ((own_ref, core), (came_ref, 1 - core)):
+            start = pl.multiple_of((2 * part + side) * half, LANES)
+            out_ref[:, pl.ds(start, half)] = ref[part]
 
 
 def reduce_plan(n, heads, sources, rounds):
@@ -140,22 +167,23 @@
     devices = [(s, h) for s in range(n) for h in range(heads)]
     plan = []
     for places in rounds:
-        codes, pairs = [[] for _ in places], [[] for _ in range(heads)]
-        owned = {d: [] for d in devices}
+        codes, pairs = [[] for _ in places], []
+        kept = {d: [] for d in devices}
         for s, h in devices:
-            counts = [0] * heads
+            sent = 0
             for i, p in enumerate(places):
                 block = sources[s][p]
-                k = (block // per) ^ h
-                codes[i].append(k * per + counts[k])
-                counts[k] += 1
-                if not k:
-                    owned[s, h].append(block % per)
-            for k in range(heads):
-                if counts[k]:
-                    pairs[k].append((s * heads + h, s * heads + (h ^ k)))
-        count = max(len(v) for v in owned.values())
-        ends = [[v[i] if i < len(v) else NONE for v in owned.values()] for i in range(count)]
+                away = (block // per) ^ h
+                if away & 2:
+                    codes[i].append(sent)
+                    sent += 1
+                else:
+                    codes[i].append(KEEP + len(kept[s, h]))
+                    kept[s, h].append(block % per + per * (away & 1))
+            if sent:
+                pairs.append((s * heads + h, s * heads + (h ^ 2)))
+        count = max(len(v) for v in kept.values())
+        ends = [[v[i] if i < len(v) else NONE for v in kept.values()] for i in range(count)]
         plan.append((codes, pairs, count, ends))
     return plan
 
@@ -209,37 +237,49 @@
     other = lax.ppermute(other, "head", beside)
     w = gather([mine, other])
 
-    attended = pl.pallas_call(
-        functools.partial(attention_kernel, n, span, group, sources),
-        out_shape=jax.ShapeDtypeStruct((tok_rows, group * DH), jnp.bfloat16),
-        in_specs=[SMEM, SMEM] + [VMEM] * (2 + n),
-        out_specs=VMEM,
-        scratch_shapes=[
-            pltpu.VMEM((group * span, 2 * n * span), jnp.float32),
-            pltpu.VMEM((group * span, span), jnp.float32),
-            pltpu.VMEM((group * span, span), jnp.float32),
-            pltpu.VMEM((group * span, DH), jnp.float32),
-        ],
-        compiler_params=limit(16),
-        cost_estimate=pl.CostEstimate(
-            flops=4 * group * tok_rows * n * tok_rows * DH,
-            bytes_accessed=n * tok_rows * 4 * DH,
-            transcendentals=group * tok_rows * n * tok_rows,
-        ),
-        name="attention",
-    )(span_order, doc_ids, doc_ids.reshape(-1, span), queries, *kv)
+    def attend(stage, slots, state, out_shape):
+        first = stage == 0
+        block = pltpu.VMEM((group * span, span), jnp.float32)
+        states = pltpu.VMEM((2, group * span, span), jnp.float32)
+        share = 2 * len(slots) * group * tok_rows * tok_rows
+        args = [queries] + [kv[i] for i in slots] + state
+        return pl.pallas_call(
+            functools.partial(
+                attention_kernel, span, group, [[row[i] for i in slots] for row in sources], first
+            ),
+            out_shape=out_shape,
+            in_specs=[SMEM, SMEM] + [VMEM] * (1 + len(args)),
+            out_specs=jax.tree.map(lambda _: VMEM, out_shape),
+            scratch_shapes=[pltpu.VMEM((group * span, 2 * len(slots) * span), jnp.float32), block]
+            + ([] if first else [states, states]),
+            compiler_params=limit(16),
+            cost_estimate=pl.CostEstimate(
+                flops=2 * share * DH,
+                bytes_accessed=len(slots) * tok_rows * 4 * DH,
+                transcendentals=share,
+            ),
+            name="attend",
+        )(span_order, doc_ids, doc_ids.reshape(-1, span), *args)
+
+    memory = jax.ShapeDtypeStruct((2, group * span, span), jnp.float32)
+    state = attend(0, range(n - 1), [], (memory,) * 3)
+    attended = attend(
+        1, [n - 1], list(state), jax.ShapeDtypeStruct((tok_rows, group * DH), jnp.bfloat16)
+    )
     paired = lax.ppermute(attended, "head", beside)
 
+    def block(count):
+        return jax.ShapeDtypeStruct((count, tok_rows, half), jnp.bfloat16)
+
     rounds = [list(range(n - 3)), [n - 3, n - 2], [n - 1]]
-    shares, ends = [], []
+    kept, came, ends = [], [], []
     for r, (codes, pairs, count, end) in enumerate(reduce_plan(n, heads, sources, rounds)):
         pieces = [piece for p in rounds[r] for piece in w[p]]
-        block = jax.ShapeDtypeStruct((count, tok_rows, half), jnp.bfloat16)
-        made = pl.pallas_call(
-            functools.partial(project_kernel, codes, per),
-            out_shape=(block,) * heads,
+        send, keep = pl.pallas_call(
+            functools.partial(project_kernel, codes),
+            out_shape=(block(count), block(count)),
             in_specs=[VMEM] * (2 + len(pieces)),
-            out_specs=(VMEM,) * heads,
+            out_specs=(VMEM, VMEM),
             compiler_params=limit(8),
             cost_estimate=pl.CostEstimate(
                 flops=2 * tok_rows * group * DH * half * len(pieces),
@@ -248,19 +288,27 @@
             ),
             name="project",
         )(attended, paired, *pieces)
-        shares.append(made[0])
-        for k in range(1, heads):
-            shares.append(lax.ppermute(made[k], ("seq", "head"), pairs[k]))
+        came.append(lax.ppermute(send, ("seq", "head"), pairs))
+        kept.append(keep)
         ends.append(end)
 
+    own, send = pl.pallas_call(
+        functools.partial(fold_kernel, ends, per),
+        out_shape=(block(per), block(per)),
+        in_specs=[VMEM] * (2 * len(ends)),
+        out_specs=(VMEM, VMEM),
+        compiler_params=limit(8),
+        name="fold",
+    )(*kept, *came)
+    joined = lax.ppermute(send, "head", beside)
     return pl.pallas_call(
-        functools.partial(finish_kernel, ends, heads),
+        finish_kernel,
         out_shape=jax.ShapeDtypeStruct((tok_rows, per * width), jnp.bfloat16),
-        in_specs=[VMEM] * len(shares),
+        in_specs=[VMEM, VMEM],
         out_specs=VMEM,
         compiler_params=limit(8),
         name="finish",
-    )(*shares)
+    )(own, joined)
 
 
 def on_device(queries, keys, values, doc_ids, span_order, out_weight):
@@ -347,7 +395,7 @@
             4 <= n <= 16
             and n % 2 == 0
             and n % heads == 0
-            and heads & (heads - 1) == 0
+            and heads == 4
             and keys.shape[1] == DH
             and span % LANES == 0
             and out_weight.shape[1] % (2 * LANES) == 0

time: 79.9 us -> 72.2 us (0.904)
  starting transfers between devices: 45.9 us -> 33.9 us
  waiting for transfers between devices: 22.9 us -> 26.2 us
  Pallas kernels: 8.45 us -> 9.68 us
    ppermute x9 -> x4, starting transfers between devices: 17.2 us -> 8.23 us  [the longest x3 8.15 us: ring_device(): came.append(lax.ppermute(send, ('seq', 'head'), pairs))]
    ppermute x21, starting transfers between devices: 28.1 us -> 25 us  [move(): return lax.ppermute(x, 'seq', pairs)]
    ppermute x21, waiting for transfers between devices: 19.6 us -> 21.5 us  [move(): return lax.ppermute(x, 'seq', pairs)]
    ppermute x9 -> x4, waiting for transfers between devices: 3.33 us -> 4.68 us  [the longest x3 3.16 us: ring_device(): came.append(lax.ppermute(send, ('seq', 'head'), pairs))]
    pallas_call x5 -> x7, Pallas kernels: 8.45 us -> 9.68 us  [the longest x2 5.4 us: attend(): pl.pallas_call(functools.partial(attention_kernel, span, group, [[row[i]...]
  transfers between devices with their start and end apart: 32 -> 27, of which waited for: 8 -> 11; matrix products, arithmetic and copies ran while one was open for 0% -> 0% of each run, Pallas kernels for 9% -> 12%
where the time goes in v1:
time: 72.2 us; the launch traced here: 72 us
  starting transfers between devices  33.9 us (47%)
  waiting for transfers between devices  26.2 us (36%)
  Pallas kernels  9.68 us (13%)
  other arithmetic  1.11 us (2%)
  local copies, waits for them, and re-layouts  0.92 us (1%)
    ppermute x21, starting transfers between devices, move(): return lax.ppermute(x, 'seq', pairs)  25 us
    ppermute x21, waiting for transfers between devices, move(): return lax.ppermute(x, 'seq', pairs)  21.5 us
    ppermute x3, starting transfers between devices, ring_device(): came.append(lax.ppermute(send, ('seq', 'head'), pairs))  8.15 us
    pallas_call x2, Pallas kernels, attend(): pl.pallas_call(functools.partial(attention_kernel, span, group, [[row[i]...  5.4 us
    pallas_call x3, Pallas kernels, ring_device(): pl.pallas_call(functools.partial(project_kernel, codes), out_shape=(block...  3.19 us
    ppermute x3, waiting for transfers between devices, ring_device(): came.append(lax.ppermute(send, ('seq', 'head'), pairs))  3.16 us
    ppermute x1, waiting for transfers between devices, ring_device(): joined = lax.ppermute(send, 'head', beside)  1.52 us
  transfers between devices with their start and end apart: 27, of which 11 were waited for; matrix products, arithmetic and copies ran while one was open for 0% of the time, Pallas kernels for 12%

profile of v1, /device:TPU:0, one launch (start us, length us, event | category | flops | bytes accessed | tf_op | source)
XLA Modules:
  0.0 72.0 jit_solution(4108985103329934659)
XLA Ops:
  2.6 2.6 %collective-permute-start = (bf16[256,256]{1,0:T(8,128)(2,1)S(1)}, bf16[256,256]{1,0:T(8,128)(2,1)S(1)}, u32[]{:S(2)}, u32[]{:S(2)}) collective-permute-start(bf16[256,256]{1,0:T(8,128)(2,1)S(1)} %constant_dynamic-update-slice_fusion.rest_0_), channel_id=1, source_target_pairs={{0,8},{8,16},{16,24},{24,28},{28,20},{20,12},{12,4},{4,0},{1,9},{9... | collective-permute-start | bytes 393224 | tf_op jit(solution)/shard_map/ppermute | solution.py:211
  5.3 2.0 %collective-permute-start.9 = (bf16[512,256]{1,0:T(8,128)(2,1)S(1)}, bf16[512,256]{1,0:T(8,128)(2,1)S(1)}, u32[]{:S(2)}, u32[]{:S(2)}) collective-permute-start(bf16[512,256]{1,0:T(8,128)(2,1)S(1)} %get-tuple-element.30.rest_0_), channel_id=1, source_target_pairs={{0,8},{8,16},{16,24},{24,28},{28,20},{20,12},{12,4},{4,0},{1,9},{9... | collective-permute-start | bytes 786440 | tf_op jit(solution)/shard_map/ppermute | solution.py:211
  7.3 2.2 %collective-permute-done.rest_1_ = bf16[256,256]{1,0:T(8,128)(2,1)S(1)} collective-permute-done((bf16[256,256]{1,0:T(8,128)(2,1)S(1)}, bf16[256,256]{1,0:T(8,128)(2,1)S(1)}, u32[]{:S(2)}, u32[]{:S(2)}) %collective-permute-start) | collective-permute-done | bytes 131104 | tf_op jit(solution)/shard_map/ppermute | solution.py:211
  9.5 2.1 %collective-permute-start.1 = (bf16[256,256]{1,0:T(8,128)(2,1)S(1)}, bf16[256,256]{1,0:T(8,128)(2,1)S(1)}, u32[]{:S(2)}, u32[]{:S(2)}) collective-permute-start(bf16[256,256]{1,0:T(8,128)(2,1)S(1)} %collective-permute-done.rest_1_), channel_id=1, source_target_pairs={{0,8},{8,16},{16,24},{24,28},{28,20},{20,12},{12,4},{4,0},{1,9},{9... | collective-permute-start | bytes 393224 | tf_op jit(solution)/shard_map/ppermute | solution.py:211
  11.6 1.9 %collective-permute-start.11 = (bf16[512,256]{1,0:T(8,128)(2,1)S(1)}, bf16[512,256]{1,0:T(8,128)(2,1)S(1)}, u32[]{:S(2)}, u32[]{:S(2)}) collective-permute-start(bf16[512,256]{1,0:T(8,128)(2,1)S(1)} %get-tuple-element.30.rest_0_), channel_id=1, source_target_pairs={{0,4},{8,0},{16,8},{24,16},{28,24},{20,28},{12,20},{4,12},{1,5},{9... | collective-permute-start | bytes 786440 | tf_op jit(solution)/shard_map/ppermute | solution.py:211
  13.6 1.6 %collective-permute-start.12 = (bf16[512,256]{1,0:T(8,128)(2,1)S(1)}, bf16[512,256]{1,0:T(8,128)(2,1)S(1)}, u32[]{:S(2)}, u32[]{:S(2)}) collective-permute-start(bf16[512,256]{1,0:T(8,128)(2,1)S(1)} %collective-permute-done.8.rest_1_), channel_id=1, source_target_pairs={{0,4},{8,0},{16,8},{24,16},{28,24},{20,28},{12,20},{4,12},{1,5},{9... | collective-permute-start | bytes 786440 | tf_op jit(solution)/shard_map/ppermute | solution.py:211
  15.1 2.5 %collective-permute-done.1.rest_3_ = bf16[256,256]{1,0:T(8,128)(2,1)S(1)} collective-permute-done((bf16[256,256]{1,0:T(8,128)(2,1)S(1)}, bf16[256,256]{1,0:T(8,128)(2,1)S(1)}, u32[]{:S(2)}, u32[]{:S(2)}) %collective-permute-start.1) | collective-permute-done | bytes 131104 | tf_op jit(solution)/shard_map/ppermute | solution.py:211
  17.7 1.8 %collective-permute-start.10 = (bf16[512,256]{1,0:T(8,128)(2,1)S(1)}, bf16[512,256]{1,0:T(8,128)(2,1)S(1)}, u32[]{:S(2)}, u32[]{:S(2)}) collective-permute-start(bf16[512,256]{1,0:T(8,128)(2,1)S(1)} %collective-permute-done.8.rest_1_), channel_id=1, source_target_pairs={{0,8},{8,16},{16,24},{24,28},{28,20},{20,12},{12,4},{4,0},{1,9},{9... | collective-permute-start | bytes 786440 | tf_op jit(solution)/shard_map/ppermute | solution.py:211
  19.5 1.6 %collective-permute-start.2 = (bf16[256,256]{1,0:T(8,128)(2,1)S(1)}, bf16[256,256]{1,0:T(8,128)(2,1)S(1)}, u32[]{:S(2)}, u32[]{:S(2)}) collective-permute-start(bf16[256,256]{1,0:T(8,128)(2,1)S(1)} %collective-permute-done.1.rest_3_), channel_id=1, source_target_pairs={{0,8},{8,16},{16,24},{24,28},{28,20},{20,12},{12,4},{4,0},{1,9},{9... | collective-permute-start | bytes 393224 | tf_op jit(solution)/shard_map/ppermute | solution.py:211
  21.6 7.0 %collective-permute-done.2.rest_5_ = bf16[256,256]{1,0:T(8,128)(2,1)S(1)} collective-permute-done((bf16[256,256]{1,0:T(8,128)(2,1)S(1)}, bf16[256,256]{1,0:T(8,128)(2,1)S(1)}, u32[]{:S(2)}, u32[]{:S(2)}) %collective-permute-start.2) | collective-permute-done | bytes 131104 | tf_op jit(solution)/shard_map/ppermute | solution.py:211
  28.6 1.6 %collective-permute-start.3 = (bf16[256,256]{1,0:T(8,128)(2,1)S(1)}, bf16[256,256]{1,0:T(8,128)(2,1)S(1)}, u32[]{:S(2)}, u32[]{:S(2)}) collective-permute-start(bf16[256,256]{1,0:T(8,128)(2,1)S(1)} %collective-permute-done.2.rest_5_), channel_id=1, source_target_pairs={{0,8},{8,16},{16,24},{24,28},{28,20},{20,12},{12,4},{4,0},{1,9},{9... | collective-permute-start | bytes 393224 | tf_op jit(solution)/shard_map/ppermute | solution.py:211
  30.1 1.6 %collective-permute-start.13 = (bf16[512,256]{1,0:T(8,128)(2,1)S(1)}, bf16[512,256]{1,0:T(8,128)(2,1)S(1)}, u32[]{:S(2)}, u32[]{:S(2)}) collective-permute-start(bf16[512,256]{1,0:T(8,128)(2,1)S(1)} %collective-permute-done.9.rest_2_), channel_id=1, source_target_pairs={{0,8},{8,16},{16,24},{24,28},{28,20},{20,12},{12,4},{4,0},{1,9},{9... | collective-permute-start | bytes 786440 | tf_op jit(solution)/shard_map/ppermute | solution.py:211
  32.7 3.7 %attend.2 = (f32[2,512,128]{2,1,0:T(8,128)S(1)}, f32[2,512,128]{2,1,0:T(8,128)S(1)}, f32[2,512,128]{2,1,0:T(8,128)S(1)}) custom-call(s32[16]{0:T(128)S(1)} %copy-done.2, s32[2048]{0:T(1024)S(1)} %copy-done.1, s32[16,128]{1,0:T(8,128)S(1)} %bitcast.1, bf16[256,512]{1,0:T(8,128)(2,1)S(1)} %copy-done, ...), custom_call_target="tpu_custom_call" | custom-call | flops 939524096 | bytes 917504 | tf_op jit(solution)/shard_map/attend/pallas_call | solution.py:246
  36.3 2.4 %collective-permute-start.14 = (bf16[512,256]{1,0:T(8,128)(2,1)S(1)}, bf16[512,256]{1,0:T(8,128)(2,1)S(1)}, u32[]{:S(2)}, u32[]{:S(2)}) collective-permute-start(bf16[512,256]{1,0:T(8,128)(2,1)S(1)} %collective-permute-done.10.rest_3_), channel_id=1, source_target_pairs={{0,8},{8,16},{16,24},{24,28},{28,20},{20,12},{12,4},{4,0},{1,9},{9... | collective-permute-start | bytes 786440 | tf_op jit(solution)/shard_map/ppermute | solution.py:211
  38.7 1.7 %attend.3.a_ref = bf16[256,512]{1,0:T(8,128)(2,1)S(1)} custom-call(s32[16]{0:T(128)S(1)} %copy-done.2, s32[2048]{0:T(1024)S(1)} %copy-done.1, s32[16,128]{1,0:T(8,128)S(1)} %bitcast.2, bf16[256,512]{1,0:T(8,128)(2,1)S(1)} %copy-done, bf16[256,256]{1,0:T(8,128)(2,1)S(1)} %collective-permute-done.3.rest_0_, f32[2,512,128]{2,1,0:T(8,128)S(1)} %get-tuple-element.17.rest_1_, ...), custom_call_target="tpu_custom_call" | custom-call | flops 134217728 | bytes 131072 | tf_op jit(solution)/shard_map/attend/pallas_call | solution.py:246
  41.4 2.3 %collective-permute-done.16.rest_9_ = bf16[512,256]{1,0:T(8,128)(2,1)S(1)} collective-permute-done((bf16[512,256]{1,0:T(8,128)(2,1)S(1)}, bf16[512,256]{1,0:T(8,128)(2,1)S(1)}, u32[]{:S(2)}, u32[]{:S(2)}) %collective-permute-start.16) | collective-permute-done | bytes 262176 | tf_op jit(solution)/shard_map/ppermute | solution.py:211
  46.5 2.0 %project.3 = (bf16[4,256,256]{2,1,0:T(8,128)(2,1)S(1)}, bf16[4,256,256]{2,1,0:T(8,128)(2,1)S(1)}) custom-call(bf16[256,512]{1,0:T(8,128)(2,1)S(1)} %attend.3.a_ref, bf16[256,512]{1,0:T(8,128)(2,1)S(1)} %collective-permute-done.7.b_ref, bf16[512,256]{1,0:T(8,128)(2,1)S(1)} %get-tuple-element.30.rest_0_, bf16[512,256]{1,0:T(8,128)(2,1)S(1)} %collective-permute-done.8.rest_1_, ...), custom_call_target="tpu_custom_call" | custom-call | flops 671088640 | bytes 2621440 | tf_op jit(solution)/shard_map/project/pallas_call | solution.py:278
  48.6 1.6 %collective-permute-start.23 = (bf16[4,256,256]{2,1,0:T(8,128)(2,1)S(1)}, bf16[4,256,256]{2,1,0:T(8,128)(2,1)S(1)}, u32[]{:S(2)}, u32[]{:S(2)}) collective-permute-start(bf16[4,256,256]{2,1,0:T(8,128)(2,1)S(1)} %get-tuple-element.24), channel_id=1, source_target_pairs={{0,2},{1,3},{2,0},{3,1},{4,6},{5,7},{6,4},{7,5},{8,10},{9,11},{10,... | collective-permute-start | bytes 1572872 | tf_op jit(solution)/shard_map/ppermute | solution.py:291
  50.1 1.8 %collective-permute-done.17.rest_0_ = bf16[512,256]{1,0:T(8,128)(2,1)S(1)} collective-permute-done((bf16[512,256]{1,0:T(8,128)(2,1)S(1)}, bf16[512,256]{1,0:T(8,128)(2,1)S(1)}, u32[]{:S(2)}, u32[]{:S(2)}) %collective-permute-start.17) | collective-permute-done | bytes 262176 | tf_op jit(solution)/shard_map/ppermute | solution.py:211
  54.2 4.1 %collective-permute-done.19.rest_2_ = bf16[512,256]{1,0:T(8,128)(2,1)S(1)} collective-permute-done((bf16[512,256]{1,0:T(8,128)(2,1)S(1)}, bf16[512,256]{1,0:T(8,128)(2,1)S(1)}, u32[]{:S(2)}, u32[]{:S(2)}) %collective-permute-start.19) | collective-permute-done | bytes 262176 | tf_op jit(solution)/shard_map/ppermute | solution.py:211
  59.2 3.4 %collective-permute-start.24 = (bf16[2,256,256]{2,1,0:T(8,128)(2,1)S(1)}, bf16[2,256,256]{2,1,0:T(8,128)(2,1)S(1)}, u32[]{:S(2)}, u32[]{:S(2)}) collective-permute-start(bf16[2,256,256]{2,1,0:T(8,128)(2,1)S(1)} %get-tuple-element.25), channel_id=1, source_target_pairs={{0,2},{1,3},{4,6},{5,7},{8,10},{9,11},{10,8},{11,9},{12,14},{13,15... | collective-permute-start | bytes 786440 | tf_op jit(solution)/shard_map/ppermute | solution.py:291
  63.0 3.1 %collective-permute-start.25 = (bf16[1,256,256]{2,1,0:T(8,128)(2,1)S(1)}, bf16[1,256,256]{2,1,0:T(8,128)(2,1)S(1)}, u32[]{:S(2)}, u32[]{:S(2)}) collective-permute-start(bf16[1,256,256]{2,1,0:T(8,128)(2,1)S(1)} %get-tuple-element.26), channel_id=1, source_target_pairs={{0,2},{1,3},{4,6},{5,7},{8,10},{9,11},{12,14},{13,15},{18,16},{19,... | collective-permute-start | bytes 393224 | tf_op jit(solution)/shard_map/ppermute | solution.py:291
  67.4 1.9 %collective-permute-done.25.rest_5_ = bf16[1,256,256]{2,1,0:T(8,128)(2,1)S(1)} collective-permute-done((bf16[1,256,256]{2,1,0:T(8,128)(2,1)S(1)}, bf16[1,256,256]{2,1,0:T(8,128)(2,1)S(1)}, u32[]{:S(2)}, u32[]{:S(2)}) %collective-permute-start.25) | collective-permute-done | bytes 131104 | tf_op jit(solution)/shard_map/ppermute | solution.py:291
  69.6 1.5 %collective-permute-done.26.came_ref = bf16[2,256,256]{2,1,0:T(8,128)(2,1)S(1)} collective-permute-done((bf16[2,256,256]{2,1,0:T(8,128)(2,1)S(1)}, bf16[2,256,256]{2,1,0:T(8,128)(2,1)S(1)}, u32[]{:S(2)}, u32[]{:S(2)}) %collective-permute-start.26) | collective-permute-done | bytes 262176 | tf_op jit(solution)/shard_map/ppermute | solution.py:303
  (48 shorter events, 13.7 us)
Async XLA Ops:
  2.1 11.5 %collective-permute-start.8 = (bf16[512,256]{1,0:T(8,128)(2,1)S(1)}, bf16[512,256]{1,0:T(8,128)(2,1)S(1)}, u32[]{:S(2)}, u32[]{:S(2)}) collective-permute-start(bf16[512,256]{1,0:T(8,128)(2,1)S(1)} %get-tuple-element.29), channel_id=1, source_target_pairs={{0,1},{1,0},{2,3},{3,2},{4,5},{5,4},{6,7},{7,6},{8,9},{9,8},{10,11... | collective-permute-start | bytes 786440 | tf_op jit(solution)/shard_map/ppermute | solution.py:237
  2.6 6.9 %collective-permute-start = (bf16[256,256]{1,0:T(8,128)(2,1)S(1)}, bf16[256,256]{1,0:T(8,128)(2,1)S(1)}, u32[]{:S(2)}, u32[]{:S(2)}) collective-permute-start(bf16[256,256]{1,0:T(8,128)(2,1)S(1)} %constant_dynamic-update-slice_fusion.rest_0_), channel_id=1, source_target_pairs={{0,8},{8,16},{16,24},{24,28},{28,20},{20,12},{12,4},{4,0},{1,9},{9... | collective-permute-start | bytes 393224 | tf_op jit(solution)/shard_map/ppermute | solution.py:211
  5.3 6.4 %collective-permute-start.4 = (bf16[256,256]{1,0:T(8,128)(2,1)S(1)}, bf16[256,256]{1,0:T(8,128)(2,1)S(1)}, u32[]{:S(2)}, u32[]{:S(2)}) collective-permute-start(bf16[256,256]{1,0:T(8,128)(2,1)S(1)} %constant_dynamic-update-slice_fusion.rest_0_), channel_id=1, source_target_pairs={{0,4},{8,0},{16,8},{24,16},{28,24},{20,28},{12,20},{4,12},{1,5},{9... | collective-permute-start | bytes 393224 | tf_op jit(solution)/shard_map/ppermute | solution.py:211
  5.3 15.9 %collective-permute-start.9 = (bf16[512,256]{1,0:T(8,128)(2,1)S(1)}, bf16[512,256]{1,0:T(8,128)(2,1)S(1)}, u32[]{:S(2)}, u32[]{:S(2)}) collective-permute-start(bf16[512,256]{1,0:T(8,128)(2,1)S(1)} %get-tuple-element.30.rest_0_), channel_id=1, source_target_pairs={{0,8},{8,16},{16,24},{24,28},{28,20},{20,12},{12,4},{4,0},{1,9},{9... | collective-permute-start | bytes 786440 | tf_op jit(solution)/shard_map/ppermute | solution.py:211
  9.5 8.2 %collective-permute-start.1 = (bf16[256,256]{1,0:T(8,128)(2,1)S(1)}, bf16[256,256]{1,0:T(8,128)(2,1)S(1)}, u32[]{:S(2)}, u32[]{:S(2)}) collective-permute-start(bf16[256,256]{1,0:T(8,128)(2,1)S(1)} %collective-permute-done.rest_1_), channel_id=1, source_target_pairs={{0,8},{8,16},{16,24},{24,28},{28,20},{20,12},{12,4},{4,0},{1,9},{9... | collective-permute-start | bytes 393224 | tf_op jit(solution)/shard_map/ppermute | solution.py:211
  11.6 7.9 %collective-permute-start.5 = (bf16[256,256]{1,0:T(8,128)(2,1)S(1)}, bf16[256,256]{1,0:T(8,128)(2,1)S(1)}, u32[]{:S(2)}, u32[]{:S(2)}) collective-permute-start(bf16[256,256]{1,0:T(8,128)(2,1)S(1)} %collective-permute-done.4.rest_2_), channel_id=1, source_target_pairs={{0,4},{8,0},{16,8},{24,16},{28,24},{20,28},{12,20},{4,12},{1,5},{9... | collective-permute-start | bytes 393224 | tf_op jit(solution)/shard_map/ppermute | solution.py:211
  11.6 18.5 %collective-permute-start.11 = (bf16[512,256]{1,0:T(8,128)(2,1)S(1)}, bf16[512,256]{1,0:T(8,128)(2,1)S(1)}, u32[]{:S(2)}, u32[]{:S(2)}) collective-permute-start(bf16[512,256]{1,0:T(8,128)(2,1)S(1)} %get-tuple-element.30.rest_0_), channel_id=1, source_target_pairs={{0,4},{8,0},{16,8},{24,16},{28,24},{20,28},{12,20},{4,12},{1,5},{9... | collective-permute-start | bytes 786440 | tf_op jit(solution)/shard_map/ppermute | solution.py:211
  13.6 18.6 %collective-permute-start.12 = (bf16[512,256]{1,0:T(8,128)(2,1)S(1)}, bf16[512,256]{1,0:T(8,128)(2,1)S(1)}, u32[]{:S(2)}, u32[]{:S(2)}) collective-permute-start(bf16[512,256]{1,0:T(8,128)(2,1)S(1)} %collective-permute-done.8.rest_1_), channel_id=1, source_target_pairs={{0,4},{8,0},{16,8},{24,16},{28,24},{20,28},{12,20},{4,12},{1,5},{9... | collective-permute-start | bytes 786440 | tf_op jit(solution)/shard_map/ppermute | solution.py:211
  17.7 18.6 %collective-permute-start.10 = (bf16[512,256]{1,0:T(8,128)(2,1)S(1)}, bf16[512,256]{1,0:T(8,128)(2,1)S(1)}, u32[]{:S(2)}, u32[]{:S(2)}) collective-permute-start(bf16[512,256]{1,0:T(8,128)(2,1)S(1)} %collective-permute-done.8.rest_1_), channel_id=1, source_target_pairs={{0,8},{8,16},{16,24},{24,28},{28,20},{20,12},{12,4},{4,0},{1,9},{9... | collective-permute-start | bytes 786440 | tf_op jit(solution)/shard_map/ppermute | solution.py:211
  19.5 9.1 %collective-permute-start.2 = (bf16[256,256]{1,0:T(8,128)(2,1)S(1)}, bf16[256,256]{1,0:T(8,128)(2,1)S(1)}, u32[]{:S(2)}, u32[]{:S(2)}) collective-permute-start(bf16[256,256]{1,0:T(8,128)(2,1)S(1)} %collective-permute-done.1.rest_3_), channel_id=1, source_target_pairs={{0,8},{8,16},{16,24},{24,28},{28,20},{20,12},{12,4},{4,0},{1,9},{9... | collective-permute-start | bytes 393224 | tf_op jit(solution)/shard_map/ppermute | solution.py:211
  21.1 10.6 %collective-permute-start.6 = (bf16[256,256]{1,0:T(8,128)(2,1)S(1)}, bf16[256,256]{1,0:T(8,128)(2,1)S(1)}, u32[]{:S(2)}, u32[]{:S(2)}) collective-permute-start(bf16[256,256]{1,0:T(8,128)(2,1)S(1)} %collective-permute-done.5.rest_4_), channel_id=1, source_target_pairs={{0,4},{8,0},{16,8},{24,16},{28,24},{20,28},{12,20},{4,12},{1,5},{9... | collective-permute-start | bytes 393224 | tf_op jit(solution)/shard_map/ppermute | solution.py:211
  28.6 10.1 %collective-permute-start.3 = (bf16[256,256]{1,0:T(8,128)(2,1)S(1)}, bf16[256,256]{1,0:T(8,128)(2,1)S(1)}, u32[]{:S(2)}, u32[]{:S(2)}) collective-permute-start(bf16[256,256]{1,0:T(8,128)(2,1)S(1)} %collective-permute-done.2.rest_5_), channel_id=1, source_target_pairs={{0,8},{8,16},{16,24},{24,28},{28,20},{20,12},{12,4},{4,0},{1,9},{9... | collective-permute-start | bytes 393224 | tf_op jit(solution)/shard_map/ppermute | solution.py:211
  30.1 10.4 %collective-permute-start.13 = (bf16[512,256]{1,0:T(8,128)(2,1)S(1)}, bf16[512,256]{1,0:T(8,128)(2,1)S(1)}, u32[]{:S(2)}, u32[]{:S(2)}) collective-permute-start(bf16[512,256]{1,0:T(8,128)(2,1)S(1)} %collective-permute-done.9.rest_2_), channel_id=1, source_target_pairs={{0,8},{8,16},{16,24},{24,28},{28,20},{20,12},{12,4},{4,0},{1,9},{9... | collective-permute-start | bytes 786440 | tf_op jit(solution)/shard_map/ppermute | solution.py:211
  31.7 12.5 %collective-permute-start.15 = (bf16[512,256]{1,0:T(8,128)(2,1)S(1)}, bf16[512,256]{1,0:T(8,128)(2,1)S(1)}, u32[]{:S(2)}, u32[]{:S(2)}) collective-permute-start(bf16[512,256]{1,0:T(8,128)(2,1)S(1)} %collective-permute-done.11.rest_4_), channel_id=1, source_target_pairs={{0,4},{8,0},{16,8},{24,16},{28,24},{20,28},{12,20},{4,12},{1,5},{9... | collective-permute-start | bytes 786440 | tf_op jit(solution)/shard_map/ppermute | solution.py:211
  32.2 11.5 %collective-permute-start.16 = (bf16[512,256]{1,0:T(8,128)(2,1)S(1)}, bf16[512,256]{1,0:T(8,128)(2,1)S(1)}, u32[]{:S(2)}, u32[]{:S(2)}) collective-permute-start(bf16[512,256]{1,0:T(8,128)(2,1)S(1)} %collective-permute-done.12.rest_5_), channel_id=1, source_target_pairs={{0,4},{8,0},{16,8},{24,16},{28,24},{20,28},{12,20},{4,12},{1,5},{9... | collective-permute-start | bytes 786440 | tf_op jit(solution)/shard_map/ppermute | solution.py:211
  36.3 10.0 %collective-permute-start.14 = (bf16[512,256]{1,0:T(8,128)(2,1)S(1)}, bf16[512,256]{1,0:T(8,128)(2,1)S(1)}, u32[]{:S(2)}, u32[]{:S(2)}) collective-permute-start(bf16[512,256]{1,0:T(8,128)(2,1)S(1)} %collective-permute-done.10.rest_3_), channel_id=1, source_target_pairs={{0,8},{8,16},{16,24},{24,28},{28,20},{20,12},{12,4},{4,0},{1,9},{9... | collective-permute-start | bytes 786440 | tf_op jit(solution)/shard_map/ppermute | solution.py:211
  40.5 11.4 %collective-permute-start.17 = (bf16[512,256]{1,0:T(8,128)(2,1)S(1)}, bf16[512,256]{1,0:T(8,128)(2,1)S(1)}, u32[]{:S(2)}, u32[]{:S(2)}) collective-permute-start(bf16[512,256]{1,0:T(8,128)(2,1)S(1)} %collective-permute-done.13.rest_6_), channel_id=1, source_target_pairs={{0,8},{8,16},{16,24},{24,28},{28,20},{20,12},{12,4},{4,0},{1,9},{9... | collective-permute-start | bytes 786440 | tf_op jit(solution)/shard_map/ppermute | solution.py:211
  43.7 9.1 %collective-permute-start.20 = (bf16[512,256]{1,0:T(8,128)(2,1)S(1)}, bf16[512,256]{1,0:T(8,128)(2,1)S(1)}, u32[]{:S(2)}, u32[]{:S(2)}) collective-permute-start(bf16[512,256]{1,0:T(8,128)(2,1)S(1)} %collective-permute-done.16.rest_9_), channel_id=1, source_target_pairs={{0,4},{8,0},{16,8},{24,16},{28,24},{20,28},{12,20},{4,12},{1,5},{9... | collective-permute-start | bytes 786440 | tf_op jit(solution)/shard_map/ppermute | solution.py:211
  44.2 14.1 %collective-permute-start.19 = (bf16[512,256]{1,0:T(8,128)(2,1)S(1)}, bf16[512,256]{1,0:T(8,128)(2,1)S(1)}, u32[]{:S(2)}, u32[]{:S(2)}) collective-permute-start(bf16[512,256]{1,0:T(8,128)(2,1)S(1)} %collective-permute-done.15.rest_8_), channel_id=1, source_target_pairs={{0,4},{8,0},{16,8},{24,16},{28,24},{20,28},{12,20},{4,12},{1,5},{9... | collective-permute-start | bytes 786440 | tf_op jit(solution)/shard_map/ppermute | solution.py:211
  46.3 12.0 %collective-permute-start.18 = (bf16[512,256]{1,0:T(8,128)(2,1)S(1)}, bf16[512,256]{1,0:T(8,128)(2,1)S(1)}, u32[]{:S(2)}, u32[]{:S(2)}) collective-permute-start(bf16[512,256]{1,0:T(8,128)(2,1)S(1)} %collective-permute-done.14.rest_7_), channel_id=1, source_target_pairs={{0,8},{8,16},{16,24},{24,28},{28,20},{20,12},{12,4},{4,0},{1,9},{9... | collective-permute-start | bytes 786440 | tf_op jit(solution)/shard_map/ppermute | solution.py:211
  48.6 17.5 %collective-permute-start.23 = (bf16[4,256,256]{2,1,0:T(8,128)(2,1)S(1)}, bf16[4,256,256]{2,1,0:T(8,128)(2,1)S(1)}, u32[]{:S(2)}, u32[]{:S(2)}) collective-permute-start(bf16[4,256,256]{2,1,0:T(8,128)(2,1)S(1)} %get-tuple-element.24), channel_id=1, source_target_pairs={{0,2},{1,3},{2,0},{3,1},{4,6},{5,7},{6,4},{7,5},{8,10},{9,11},{10,... | collective-permute-start | bytes 1572872 | tf_op jit(solution)/shard_map/ppermute | solution.py:291
  51.9 10.7 %collective-permute-start.21 = (bf16[512,256]{1,0:T(8,128)(2,1)S(1)}, bf16[512,256]{1,0:T(8,128)(2,1)S(1)}, u32[]{:S(2)}, u32[]{:S(2)}) collective-permute-start(bf16[512,256]{1,0:T(8,128)(2,1)S(1)} %collective-permute-done.17.rest_0_), channel_id=1, source_target_pairs={{0,8},{8,16},{16,24},{24,28},{28,20},{20,12},{12,4},{4,0},{1,9},{9... | collective-permute-start | bytes 786440 | tf_op jit(solution)/shard_map/ppermute | solution.py:211
  52.9 9.8 %collective-permute-start.22 = (bf16[512,256]{1,0:T(8,128)(2,1)S(1)}, bf16[512,256]{1,0:T(8,128)(2,1)S(1)}, u32[]{:S(2)}, u32[]{:S(2)}) collective-permute-start(bf16[512,256]{1,0:T(8,128)(2,1)S(1)} %collective-permute-done.20.rest_3_), channel_id=1, source_target_pairs={{0,4},{8,0},{16,8},{24,16},{28,24},{20,28},{12,20},{4,12},{1,5},{9... | collective-permute-start | bytes 786440 | tf_op jit(solution)/shard_map/ppermute | solution.py:211
  59.2 8.2 %collective-permute-start.24 = (bf16[2,256,256]{2,1,0:T(8,128)(2,1)S(1)}, bf16[2,256,256]{2,1,0:T(8,128)(2,1)S(1)}, u32[]{:S(2)}, u32[]{:S(2)}) collective-permute-start(bf16[2,256,256]{2,1,0:T(8,128)(2,1)S(1)} %get-tuple-element.25), channel_id=1, source_target_pairs={{0,2},{1,3},{4,6},{5,7},{8,10},{9,11},{10,8},{11,9},{12,14},{13,15... | collective-permute-start | bytes 786440 | tf_op jit(solution)/shard_map/ppermute | solution.py:291
  (7 other events, 105.7 us)

commit v2 on v1

--- a/solution.py
+++ b/solution.py
@@ -14,7 +14,7 @@
 NONE = -1000
 VMEM = pl.BlockSpec(memory_space=pltpu.VMEM)
 SMEM = pl.BlockSpec(memory_space=pltpu.SMEM)
-NONE, KEEP = 15, 8
+SEND, KEEP, HOLD, NONE = 0, 5, 10, 15
 
 
 def limit(mib):
@@ -38,7 +38,9 @@
 
 def attention_kernel(span, group, sources, first, order_ref, docid_ref, docs_ref, q_ref, *rest):
     many = len(sources[0])
-    kv_refs, rest = rest[:many], rest[many:]
+    split = 1 if first else 2
+    kv_refs, rest = rest[: many * split], rest[many * split :]
+    spans = [(ref, at) for ref in kv_refs for at in range(0, ref.shape[0], span)]
     if first:
         top_ref, sum_ref, mix_ref, s_ref, m_ref = rest
     else:
@@ -71,7 +73,7 @@
 
             @pl.when(lives[j])
             def _():
-                k = kv_refs[j // 2][(j % 2) * span : (j % 2 + 1) * span, :DH]
+                k = spans[j][0][spans[j][1] : spans[j][1] + span, :DH]
                 s = lax.dot_general(q, k, dims, preferred_element_type=jnp.float32)
                 kdoc = docs_ref[pl.ds(kposs[j], 1), :].astype(jnp.float32)
                 visible = (qdoc == kdoc) & (ahead <= (qpos - kposs[j]) * span)
@@ -98,7 +100,7 @@
             def _():
                 p = jnp.exp2(s_ref[:, j * span : (j + 1) * span] * base2 - largest)
                 sum_ref[part] += p
-                v = kv_refs[j // 2][(j % 2) * span : (j % 2 + 1) * span, DH:]
+                v = spans[j][0][spans[j][1] : spans[j][1] + span, DH:]
                 mix_ref[part] += jnp.dot(
                     p.astype(jnp.bfloat16), v, preferred_element_type=jnp.float32
                 )
@@ -114,22 +116,25 @@
     return lax.axis_index("seq") * lax.axis_size("head") + lax.axis_index("head")
 
 
-def project_kernel(codes, a_ref, b_ref, *rest):
-    w_refs, (send_ref, keep_ref) = rest[:-2], rest[-2:]
+def project_kernel(codes, moved, a_ref, b_ref, *rest):
+    w_refs, rest = rest[: 2 * len(codes)], rest[2 * len(codes) :]
+    if moved:
+        held_ref, rest = rest[0], rest[1:]
     me = place()
+
+    def put(at, c):
+        for low, ref in zip((SEND, KEEP, HOLD), rest):
+
+            @pl.when((at >= low) & (at < low + ref.shape[0]))
+            def _():
+                ref[at - low] = c
+
+    for i, values in enumerate(moved):
+        put(lookup(values, me), held_ref[i])
     for i, values in enumerate(codes):
-        at = lookup(values, me)
         c = jnp.dot(a_ref[...], w_refs[2 * i][...], preferred_element_type=jnp.float32)
         c += jnp.dot(b_ref[...], w_refs[2 * i + 1][...], preferred_element_type=jnp.float32)
-        c = c.astype(jnp.bfloat16)
-
-        @pl.when(at < KEEP)
-        def _():
-            send_ref[at] = c
-
-        @pl.when(at >= KEEP)
-        def _():
-            keep_ref[at - KEEP] = c
+        put(lookup(values, me), c.astype(jnp.bfloat16))
 
 
 def fold_kernel(codes, per, *rest):
@@ -165,26 +170,44 @@
 def reduce_plan(n, heads, sources, rounds):
     per = n // heads
     devices = [(s, h) for s in range(n) for h in range(heads)]
+    first = n // 2 - sum(len(places) for places in rounds[1:])
+    caps = [max(1, first)] + [len(places) for places in rounds[1:]]
+    turns = {}
+    for s in range(n):
+        for owners in (0, 2):
+            room = list(caps)
+            for r, places in enumerate(rounds):
+                for p in places:
+                    if (sources[s][p] // per) & 2 == owners:
+                        at = next(k for k in range(r, len(caps)) if room[k])
+                        room[at] -= 1
+                        turns[s, p] = at
     plan = []
-    for places in rounds:
-        codes, pairs = [[] for _ in places], []
-        kept = {d: [] for d in devices}
+    held = {d: [] for d in devices}
+    for r, places in enumerate(rounds):
+        codes, moved = [[] for _ in places], [[] for _ in range(max(map(len, held.values())))]
+        kept, later = {d: [] for d in devices}, {d: [] for d in devices}
         for s, h in devices:
             sent = 0
-            for i, p in enumerate(places):
+            jobs = [(moved[i], p) for i, p in enumerate(held[s, h])]
+            jobs += [(codes[i], p) for i, p in enumerate(places)]
+            for row, p in jobs:
                 block = sources[s][p]
                 away = (block // per) ^ h
-                if away & 2:
-                    codes[i].append(sent)
+                if turns[s, p] > r:
+                    row.append(HOLD + len(later[s, h]))
+                    later[s, h].append(p)
+                elif away & 2:
+                    row.append(SEND + sent)
                     sent += 1
                 else:
-                    codes[i].append(KEEP + len(kept[s, h]))
+                    row.append(KEEP + len(kept[s, h]))
                     kept[s, h].append(block % per + per * (away & 1))
-            if sent:
-                pairs.append((s * heads + h, s * heads + (h ^ 2)))
-        count = max(len(v) for v in kept.values())
-        ends = [[v[i] if i < len(v) else NONE for v in kept.values()] for i in range(count)]
-        plan.append((codes, pairs, count, ends))
+            for row in moved[len(held[s, h]) :]:
+                row.append(NONE)
+        held = later
+        ends = [[v[i] if i < len(v) else NONE for v in kept.values()] for i in range(caps[r])]
+        plan.append((codes, moved, caps[r], max(map(len, held.values())), ends))
     return plan
 
 
@@ -211,24 +234,19 @@
             return lax.ppermute(x, "seq", pairs)
 
         ups, downs = list(pieces), list(pieces)
-        late = (len(pieces) + 1) // 2
         got = [list(pieces)]
-        for hop in range(1, hops + 1):
-            last = hop == hops
+        for _ in range(1, hops):
             for i in range(len(pieces)):
-                if not last or i < late:
-                    ups[i] = move("up", ups[i])
-                if not last or i >= late:
-                    downs[i] = move("dn", downs[i])
-            if last:
-                got.append(ups[:late] + downs[late:])
-            else:
-                got += [list(ups), list(downs)]
+                ups[i] = move("up", ups[i])
+                downs[i] = move("dn", downs[i])
+            got += [list(ups), list(downs)]
+        if len(pieces) == 1:
+            rows = pieces[0].shape[0] // 2
+            ups, downs = [ups[0][:rows], None], [None, downs[0][rows:]]
+        got.append([move("up", ups[0]), move("dn", downs[1])])
         return got
 
-    both = jnp.concatenate([keys, values], axis=1)
-    kv = [g[0] for g in gather([both])]
-    out_weight, both = lax.optimization_barrier((out_weight, both))
+    kv = gather([jnp.concatenate([keys, values], axis=1)])
     half = width // 2
     first = (lax.axis_index("head") & 1) == 0
     mine = jnp.where(first, out_weight[:, :half], out_weight[:, half:])
@@ -242,7 +260,7 @@
         block = pltpu.VMEM((group * span, span), jnp.float32)
         states = pltpu.VMEM((2, group * span, span), jnp.float32)
         share = 2 * len(slots) * group * tok_rows * tok_rows
-        args = [queries] + [kv[i] for i in slots] + state
+        args = [queries] + [piece for i in slots for piece in kv[i]] + state
         return pl.pallas_call(
             functools.partial(
                 attention_kernel, span, group, [[row[i] for i in slots] for row in sources], first
@@ -272,14 +290,18 @@
         return jax.ShapeDtypeStruct((count, tok_rows, half), jnp.bfloat16)
 
     rounds = [list(range(n - 3)), [n - 3, n - 2], [n - 1]]
-    kept, came, ends = [], [], []
-    for r, (codes, pairs, count, end) in enumerate(reduce_plan(n, heads, sources, rounds)):
+    across = [(h, h ^ 2) for h in range(heads)]
+    kept, came, ends, held = [], [], [], []
+    for r, (codes, moved, count, hold, end) in enumerate(
+        reduce_plan(n, heads, sources, rounds)
+    ):
         pieces = [piece for p in rounds[r] for piece in w[p]]
-        send, keep = pl.pallas_call(
-            functools.partial(project_kernel, codes),
-            out_shape=(block(count), block(count)),
-            in_specs=[VMEM] * (2 + len(pieces)),
-            out_specs=(VMEM, VMEM),
+        outs = (block(count), block(count)) + ((block(hold),) if hold else ())
+        send, keep, *rest = pl.pallas_call(
+            functools.partial(project_kernel, codes, moved),
+            out_shape=outs,
+            in_specs=[VMEM] * (2 + len(pieces) + len(held)),
+            out_specs=(VMEM,) * len(outs),
             compiler_params=limit(8),
             cost_estimate=pl.CostEstimate(
                 flops=2 * tok_rows * group * DH * half * len(pieces),
@@ -287,8 +309,9 @@
                 transcendentals=0,
             ),
             name="project",
-        )(attended, paired, *pieces)
-        came.append(lax.ppermute(send, ("seq", "head"), pairs))
+        )(attended, paired, *pieces, *held)
+        came.append(lax.ppermute(send, "head", across))
+        held = rest
         kept.append(keep)
         ends.append(end)
 

time: 72.2 us -> 82.1 us (1.14)
  waiting for transfers between devices: 26.2 us -> 37.2 us
    ppermute x21 -> x22, waiting for transfers between devices: 21.5 us -> 29.1 us  [move(): return lax.ppermute(x, 'seq', pairs)]
    ppermute x3, starting transfers between devices: 8.15 us -> 3.66 us  [ring_device(): came.append(lax.ppermute(send, 'head', across))]
    ppermute x21 -> x22, starting transfers between devices: 25 us -> 29 us  [move(): return lax.ppermute(x, 'seq', pairs)]
    ppermute x3, waiting for transfers between devices: 3.16 us -> 6.59 us  [ring_device(): came.append(lax.ppermute(send, 'head', across))]
  transfers between devices with their start and end apart: 27 -> 28, of which waited for: 11 -> 12; matrix products, arithmetic and copies ran while one was open for 0% -> 0% of each run, Pallas kernels for 12% -> 11%
where the time goes in v2:
time: 82.1 us; the launch traced here: 82 us
  waiting for transfers between devices  37.2 us (45%)
  starting transfers between devices  33.4 us (41%)
  Pallas kernels  9.78 us (12%)
  other arithmetic  1.1 us (1%)
    ppermute x22, waiting for transfers between devices, move(): return lax.ppermute(x, 'seq', pairs)  29.1 us
    ppermute x22, starting transfers between devices, move(): return lax.ppermute(x, 'seq', pairs)  29 us
    ppermute x3, waiting for transfers between devices, ring_device(): came.append(lax.ppermute(send, 'head', across))  6.59 us
    pallas_call x2, Pallas kernels, attend(): pl.pallas_call(functools.partial(attention_kernel, span, group, [[row[i]...  5.4 us
    ppermute x3, starting transfers between devices, ring_device(): came.append(lax.ppermute(send, 'head', across))  3.66 us
    pallas_call x3, Pallas kernels, ring_device(): pl.pallas_call(functools.partial(project_kernel, codes, moved), out_shape...  3.31 us
  transfers between devices with their start and end apart: 28, of which 12 were waited for; matrix products, arithmetic and copies ran while one was open for 0% of the time, Pallas kernels for 11%

profile of v2, /device:TPU:0, one launch (start us, length us, event | category | flops | bytes accessed | tf_op | source)
XLA Modules:
  0.0 82.0 jit_solution(12550869923463397717)
XLA Ops:
  2.0 3.1 %collective-permute-start = (bf16[256,256]{1,0:T(8,128)(2,1)S(1)}, bf16[256,256]{1,0:T(8,128)(2,1)S(1)}, u32[]{:S(2)}, u32[]{:S(2)}) collective-permute-start(bf16[256,256]{1,0:T(8,128)(2,1)S(1)} %constant_dynamic-update-slice_fusion.rest_0_), channel_id=1, source_target_pairs={{0,8},{8,16},{16,24},{24,28},{28,20},{20,12},{12,4},{4,0},{1,9},{9... | collective-permute-start | bytes 393224 | tf_op jit(solution)/shard_map/ppermute | solution.py:234
  5.1 1.6 %collective-permute-start.10 = (bf16[512,256]{1,0:T(8,128)(2,1)S(1)}, bf16[512,256]{1,0:T(8,128)(2,1)S(1)}, u32[]{:S(2)}, u32[]{:S(2)}) collective-permute-start(bf16[512,256]{1,0:T(8,128)(2,1)S(1)} %get-tuple-element.32.rest_0_), channel_id=1, source_target_pairs={{0,8},{8,16},{16,24},{24,28},{28,20},{20,12},{12,4},{4,0},{1,9},{9... | collective-permute-start | bytes 786440 | tf_op jit(solution)/shard_map/ppermute | solution.py:234
  7.3 2.1 %collective-permute-done.rest_1_ = bf16[256,256]{1,0:T(8,128)(2,1)S(1)} collective-permute-done((bf16[256,256]{1,0:T(8,128)(2,1)S(1)}, bf16[256,256]{1,0:T(8,128)(2,1)S(1)}, u32[]{:S(2)}, u32[]{:S(2)}) %collective-permute-start) | collective-permute-done | bytes 131104 | tf_op jit(solution)/shard_map/ppermute | solution.py:234
  9.3 2.1 %collective-permute-start.1 = (bf16[256,256]{1,0:T(8,128)(2,1)S(1)}, bf16[256,256]{1,0:T(8,128)(2,1)S(1)}, u32[]{:S(2)}, u32[]{:S(2)}) collective-permute-start(bf16[256,256]{1,0:T(8,128)(2,1)S(1)} %collective-permute-done.rest_1_), channel_id=1, source_target_pairs={{0,8},{8,16},{16,24},{24,28},{28,20},{20,12},{12,4},{4,0},{1,9},{9... | collective-permute-start | bytes 393224 | tf_op jit(solution)/shard_map/ppermute | solution.py:234
  11.4 7.2 %collective-permute-done.4.rest_2_ = bf16[256,256]{1,0:T(8,128)(2,1)S(1)} collective-permute-done((bf16[256,256]{1,0:T(8,128)(2,1)S(1)}, bf16[256,256]{1,0:T(8,128)(2,1)S(1)}, u32[]{:S(2)}, u32[]{:S(2)}) %collective-permute-start.4) | collective-permute-done | bytes 131104 | tf_op jit(solution)/shard_map/ppermute | solution.py:234
  19.1 1.6 %collective-permute-start.11 = (bf16[512,256]{1,0:T(8,128)(2,1)S(1)}, bf16[512,256]{1,0:T(8,128)(2,1)S(1)}, u32[]{:S(2)}, u32[]{:S(2)}) collective-permute-start(bf16[512,256]{1,0:T(8,128)(2,1)S(1)} %collective-permute-done.9.rest_1_), channel_id=1, source_target_pairs={{0,8},{8,16},{16,24},{24,28},{28,20},{20,12},{12,4},{4,0},{1,9},{9... | collective-permute-start | bytes 786440 | tf_op jit(solution)/shard_map/ppermute | solution.py:234
  20.7 1.6 %collective-permute-start.14 = (bf16[512,256]{1,0:T(8,128)(2,1)S(1)}, bf16[512,256]{1,0:T(8,128)(2,1)S(1)}, u32[]{:S(2)}, u32[]{:S(2)}) collective-permute-start(bf16[512,256]{1,0:T(8,128)(2,1)S(1)} %collective-permute-done.10.rest_2_), channel_id=1, source_target_pairs={{0,8},{8,16},{16,24},{24,28},{28,20},{20,12},{12,4},{4,0},{1,9},{9... | collective-permute-start | bytes 786440 | tf_op jit(solution)/shard_map/ppermute | solution.py:234
  22.7 4.4 %collective-permute-done.5.rest_4_ = bf16[256,256]{1,0:T(8,128)(2,1)S(1)} collective-permute-done((bf16[256,256]{1,0:T(8,128)(2,1)S(1)}, bf16[256,256]{1,0:T(8,128)(2,1)S(1)}, u32[]{:S(2)}, u32[]{:S(2)}) %collective-permute-start.5) | collective-permute-done | bytes 131104 | tf_op jit(solution)/shard_map/ppermute | solution.py:234
  27.1 1.6 %collective-permute-start.2 = (bf16[256,256]{1,0:T(8,128)(2,1)S(1)}, bf16[256,256]{1,0:T(8,128)(2,1)S(1)}, u32[]{:S(2)}, u32[]{:S(2)}) collective-permute-start(bf16[256,256]{1,0:T(8,128)(2,1)S(1)} %collective-permute-done.1.rest_3_), channel_id=1, source_target_pairs={{0,8},{8,16},{16,24},{24,28},{28,20},{20,12},{12,4},{4,0},{1,9},{9... | collective-permute-start | bytes 393224 | tf_op jit(solution)/shard_map/ppermute | solution.py:234
  29.1 3.7 %collective-permute-done.2.rest_5_ = bf16[256,256]{1,0:T(8,128)(2,1)S(1)} collective-permute-done((bf16[256,256]{1,0:T(8,128)(2,1)S(1)}, bf16[256,256]{1,0:T(8,128)(2,1)S(1)}, u32[]{:S(2)}, u32[]{:S(2)}) %collective-permute-start.2) | collective-permute-done | bytes 131104 | tf_op jit(solution)/shard_map/ppermute | solution.py:234
  35.5 1.6 %collective-permute-start.3 = (bf16[128,256]{1,0:T(8,128)(2,1)S(1)}, bf16[128,256]{1,0:T(8,128)(2,1)S(1)}, u32[]{:S(2)}, u32[]{:S(2)}) collective-permute-start(bf16[128,256]{1,0:T(8,128)(2,1)S(1)} %slice.18), channel_id=1, source_target_pairs={{0,8},{8,16},{16,24},{24,28},{28,20},{20,12},{12,4},{4,0},{1,9},{9... | collective-permute-start | bytes 196616 | tf_op jit(solution)/shard_map/ppermute | solution.py:234
  37.1 4.3 %collective-permute-done.3.rest_0_ = bf16[128,256]{1,0:T(8,128)(2,1)S(1)} collective-permute-done((bf16[128,256]{1,0:T(8,128)(2,1)S(1)}, bf16[128,256]{1,0:T(8,128)(2,1)S(1)}, u32[]{:S(2)}, u32[]{:S(2)}) %collective-permute-start.3) | collective-permute-done | bytes 65568 | tf_op jit(solution)/shard_map/ppermute | solution.py:234
  41.3 1.6 %collective-permute-start.7 = (bf16[128,256]{1,0:T(8,128)(2,1)S(1)}, bf16[128,256]{1,0:T(8,128)(2,1)S(1)}, u32[]{:S(2)}, u32[]{:S(2)}) collective-permute-start(bf16[128,256]{1,0:T(8,128)(2,1)S(1)} %slice.19), channel_id=1, source_target_pairs={{0,4},{8,0},{16,8},{24,16},{28,24},{20,28},{12,20},{4,12},{1,5},{9... | collective-permute-start | bytes 196616 | tf_op jit(solution)/shard_map/ppermute | solution.py:234
  43.4 1.6 %collective-permute-start.21 = (bf16[512,256]{1,0:T(8,128)(2,1)S(1)}, bf16[512,256]{1,0:T(8,128)(2,1)S(1)}, u32[]{:S(2)}, u32[]{:S(2)}) collective-permute-start(bf16[512,256]{1,0:T(8,128)(2,1)S(1)} %collective-permute-done.17.rest_9_), channel_id=1, source_target_pairs={{0,4},{8,0},{16,8},{24,16},{28,24},{20,28},{12,20},{4,12},{1,5},{9... | collective-permute-start | bytes 786440 | tf_op jit(solution)/shard_map/ppermute | solution.py:234
  45.0 3.7 %attend.2 = (f32[2,512,128]{2,1,0:T(8,128)S(1)}, f32[2,512,128]{2,1,0:T(8,128)S(1)}, f32[2,512,128]{2,1,0:T(8,128)S(1)}) custom-call(s32[16]{0:T(128)S(1)} %copy-done.2, s32[2048]{0:T(1024)S(1)} %copy-done.1, s32[16,128]{1,0:T(8,128)S(1)} %bitcast.1, bf16[256,512]{1,0:T(8,128)(2,1)S(1)} %copy-done, ...), custom_call_target="tpu_custom_call" | custom-call | flops 939524096 | bytes 917504 | tf_op jit(solution)/shard_map/attend/pallas_call | solution.py:264
  48.6 1.8 %attend.3.a_ref = bf16[256,512]{1,0:T(8,128)(2,1)S(1)} custom-call(s32[16]{0:T(128)S(1)} %copy-done.2, s32[2048]{0:T(1024)S(1)} %copy-done.1, s32[16,128]{1,0:T(8,128)S(1)} %bitcast.2, bf16[256,512]{1,0:T(8,128)(2,1)S(1)} %copy-done, bf16[128,256]{1,0:T(8,128)(2,1)S(1)} %collective-permute-done.3.rest_0_, ...), custom_call_target="tpu_custom_call" | custom-call | flops 134217728 | bytes 131072 | tf_op jit(solution)/shard_map/attend/pallas_call | solution.py:264
  50.5 6.3 %collective-permute-start.20 = (bf16[512,256]{1,0:T(8,128)(2,1)S(1)}, bf16[512,256]{1,0:T(8,128)(2,1)S(1)}, u32[]{:S(2)}, u32[]{:S(2)}) collective-permute-start(bf16[512,256]{1,0:T(8,128)(2,1)S(1)} %collective-permute-done.16.rest_8_), channel_id=1, source_target_pairs={{0,4},{8,0},{16,8},{24,16},{28,24},{20,28},{12,20},{4,12},{1,5},{9... | collective-permute-start | bytes 786440 | tf_op jit(solution)/shard_map/ppermute | solution.py:234
  56.9 2.0 %collective-permute-start.23 = (bf16[512,256]{1,0:T(8,128)(2,1)S(1)}, bf16[512,256]{1,0:T(8,128)(2,1)S(1)}, u32[]{:S(2)}, u32[]{:S(2)}) collective-permute-start(bf16[512,256]{1,0:T(8,128)(2,1)S(1)} %collective-permute-done.21.rest_3_), channel_id=1, source_target_pairs={{0,4},{8,0},{16,8},{24,16},{28,24},{20,28},{12,20},{4,12},{1,5},{9... | collective-permute-start | bytes 786440 | tf_op jit(solution)/shard_map/ppermute | solution.py:234
  58.9 2.0 %project.3 = (bf16[1,256,256]{2,1,0:T(8,128)(2,1)S(1)}, bf16[1,256,256]{2,1,0:T(8,128)(2,1)S(1)}, bf16[3,256,256]{2,1,0:T(8,128)(2,1)S(1)}) custom-call(bf16[256,512]{1,0:T(8,128)(2,1)S(1)} %attend.3.a_ref, bf16[256,512]{1,0:T(8,128)(2,1)S(1)} %collective-permute-done.8.b_ref, bf16[512,256]{1,0:T(8,128)(2,1)S(1)} %get-tuple-element.32.rest_0_, ...), custom_call_target="tpu_custom_call" | custom-call | flops 671088640 | bytes 2621440 | tf_op jit(solution)/shard_map/project/pallas_call | solution.py:300
  60.9 2.6 %collective-permute-done.20.rest_2_ = bf16[512,256]{1,0:T(8,128)(2,1)S(1)} collective-permute-done((bf16[512,256]{1,0:T(8,128)(2,1)S(1)}, bf16[512,256]{1,0:T(8,128)(2,1)S(1)}, u32[]{:S(2)}, u32[]{:S(2)}) %collective-permute-start.20) | collective-permute-done | bytes 262176 | tf_op jit(solution)/shard_map/ppermute | solution.py:234
  63.5 2.5 %collective-permute-done.19.rest_1_ = bf16[512,256]{1,0:T(8,128)(2,1)S(1)} collective-permute-done((bf16[512,256]{1,0:T(8,128)(2,1)S(1)}, bf16[512,256]{1,0:T(8,128)(2,1)S(1)}, u32[]{:S(2)}, u32[]{:S(2)}) %collective-permute-start.19) | collective-permute-done | bytes 262176 | tf_op jit(solution)/shard_map/ppermute | solution.py:234
  66.9 1.6 %collective-permute-start.25 = (bf16[2,256,256]{2,1,0:T(8,128)(2,1)S(1)}, bf16[2,256,256]{2,1,0:T(8,128)(2,1)S(1)}, u32[]{:S(2)}, u32[]{:S(2)}) collective-permute-start(bf16[2,256,256]{2,1,0:T(8,128)(2,1)S(1)} %get-tuple-element.27), channel_id=1, source_target_pairs={{0,2},{1,3},{2,0},{3,1},{4,6},{5,7},{6,4},{7,5},{8,10},{9,11},{10,... | collective-permute-start | bytes 786440 | tf_op jit(solution)/shard_map/ppermute | solution.py:313
  69.0 1.8 %collective-permute-done.22.rest_0_ = bf16[512,256]{1,0:T(8,128)(2,1)S(1)} collective-permute-done((bf16[512,256]{1,0:T(8,128)(2,1)S(1)}, bf16[512,256]{1,0:T(8,128)(2,1)S(1)}, u32[]{:S(2)}, u32[]{:S(2)}) %collective-permute-start.22) | collective-permute-done | bytes 262176 | tf_op jit(solution)/shard_map/ppermute | solution.py:234
  72.7 5.2 %collective-permute-done.24.rest_3_ = bf16[1,256,256]{2,1,0:T(8,128)(2,1)S(1)} collective-permute-done((bf16[1,256,256]{2,1,0:T(8,128)(2,1)S(1)}, bf16[1,256,256]{2,1,0:T(8,128)(2,1)S(1)}, u32[]{:S(2)}, u32[]{:S(2)}) %collective-permute-start.24) | collective-permute-done | bytes 131104 | tf_op jit(solution)/shard_map/ppermute | solution.py:313
  (54 shorter events, 14.7 us)
Async XLA Ops:
  2.0 7.4 %collective-permute-start = (bf16[256,256]{1,0:T(8,128)(2,1)S(1)}, bf16[256,256]{1,0:T(8,128)(2,1)S(1)}, u32[]{:S(2)}, u32[]{:S(2)}) collective-permute-start(bf16[256,256]{1,0:T(8,128)(2,1)S(1)} %constant_dynamic-update-slice_fusion.rest_0_), channel_id=1, source_target_pairs={{0,8},{8,16},{16,24},{24,28},{28,20},{20,12},{12,4},{4,0},{1,9},{9... | collective-permute-start | bytes 393224 | tf_op jit(solution)/shard_map/ppermute | solution.py:234
  5.1 15.6 %collective-permute-start.10 = (bf16[512,256]{1,0:T(8,128)(2,1)S(1)}, bf16[512,256]{1,0:T(8,128)(2,1)S(1)}, u32[]{:S(2)}, u32[]{:S(2)}) collective-permute-start(bf16[512,256]{1,0:T(8,128)(2,1)S(1)} %get-tuple-element.32.rest_0_), channel_id=1, source_target_pairs={{0,8},{8,16},{16,24},{24,28},{28,20},{20,12},{12,4},{4,0},{1,9},{9... | collective-permute-start | bytes 786440 | tf_op jit(solution)/shard_map/ppermute | solution.py:234
  6.7 15.6 %collective-permute-start.13 = (bf16[512,256]{1,0:T(8,128)(2,1)S(1)}, bf16[512,256]{1,0:T(8,128)(2,1)S(1)}, u32[]{:S(2)}, u32[]{:S(2)}) collective-permute-start(bf16[512,256]{1,0:T(8,128)(2,1)S(1)} %collective-permute-done.9.rest_1_), channel_id=1, source_target_pairs={{0,4},{8,0},{16,8},{24,16},{28,24},{20,28},{12,20},{4,12},{1,5},{9... | collective-permute-start | bytes 786440 | tf_op jit(solution)/shard_map/ppermute | solution.py:234
  7.1 11.5 %collective-permute-start.4 = (bf16[256,256]{1,0:T(8,128)(2,1)S(1)}, bf16[256,256]{1,0:T(8,128)(2,1)S(1)}, u32[]{:S(2)}, u32[]{:S(2)}) collective-permute-start(bf16[256,256]{1,0:T(8,128)(2,1)S(1)} %constant_dynamic-update-slice_fusion.rest_0_), channel_id=1, source_target_pairs={{0,4},{8,0},{16,8},{24,16},{28,24},{20,28},{12,20},{4,12},{1,5},{9... | collective-permute-start | bytes 393224 | tf_op jit(solution)/shard_map/ppermute | solution.py:234
  9.3 9.8 %collective-permute-start.1 = (bf16[256,256]{1,0:T(8,128)(2,1)S(1)}, bf16[256,256]{1,0:T(8,128)(2,1)S(1)}, u32[]{:S(2)}, u32[]{:S(2)}) collective-permute-start(bf16[256,256]{1,0:T(8,128)(2,1)S(1)} %collective-permute-done.rest_1_), channel_id=1, source_target_pairs={{0,8},{8,16},{16,24},{24,28},{28,20},{20,12},{12,4},{4,0},{1,9},{9... | collective-permute-start | bytes 393224 | tf_op jit(solution)/shard_map/ppermute | solution.py:234
  11.4 17.2 %collective-permute-start.12 = (bf16[512,256]{1,0:T(8,128)(2,1)S(1)}, bf16[512,256]{1,0:T(8,128)(2,1)S(1)}, u32[]{:S(2)}, u32[]{:S(2)}) collective-permute-start(bf16[512,256]{1,0:T(8,128)(2,1)S(1)} %get-tuple-element.32.rest_0_), channel_id=1, source_target_pairs={{0,4},{8,0},{16,8},{24,16},{28,24},{20,28},{12,20},{4,12},{1,5},{9... | collective-permute-start | bytes 786440 | tf_op jit(solution)/shard_map/ppermute | solution.py:234
  18.6 8.4 %collective-permute-start.5 = (bf16[256,256]{1,0:T(8,128)(2,1)S(1)}, bf16[256,256]{1,0:T(8,128)(2,1)S(1)}, u32[]{:S(2)}, u32[]{:S(2)}) collective-permute-start(bf16[256,256]{1,0:T(8,128)(2,1)S(1)} %collective-permute-done.4.rest_2_), channel_id=1, source_target_pairs={{0,4},{8,0},{16,8},{24,16},{28,24},{20,28},{12,20},{4,12},{1,5},{9... | collective-permute-start | bytes 393224 | tf_op jit(solution)/shard_map/ppermute | solution.py:234
  19.1 15.2 %collective-permute-start.11 = (bf16[512,256]{1,0:T(8,128)(2,1)S(1)}, bf16[512,256]{1,0:T(8,128)(2,1)S(1)}, u32[]{:S(2)}, u32[]{:S(2)}) collective-permute-start(bf16[512,256]{1,0:T(8,128)(2,1)S(1)} %collective-permute-done.9.rest_1_), channel_id=1, source_target_pairs={{0,8},{8,16},{16,24},{24,28},{28,20},{20,12},{12,4},{4,0},{1,9},{9... | collective-permute-start | bytes 786440 | tf_op jit(solution)/shard_map/ppermute | solution.py:234
  20.7 22.2 %collective-permute-start.14 = (bf16[512,256]{1,0:T(8,128)(2,1)S(1)}, bf16[512,256]{1,0:T(8,128)(2,1)S(1)}, u32[]{:S(2)}, u32[]{:S(2)}) collective-permute-start(bf16[512,256]{1,0:T(8,128)(2,1)S(1)} %collective-permute-done.10.rest_2_), channel_id=1, source_target_pairs={{0,8},{8,16},{16,24},{24,28},{28,20},{20,12},{12,4},{4,0},{1,9},{9... | collective-permute-start | bytes 786440 | tf_op jit(solution)/shard_map/ppermute | solution.py:234
  22.3 21.1 %collective-permute-start.17 = (bf16[512,256]{1,0:T(8,128)(2,1)S(1)}, bf16[512,256]{1,0:T(8,128)(2,1)S(1)}, u32[]{:S(2)}, u32[]{:S(2)}) collective-permute-start(bf16[512,256]{1,0:T(8,128)(2,1)S(1)} %collective-permute-done.13.rest_5_), channel_id=1, source_target_pairs={{0,4},{8,0},{16,8},{24,16},{28,24},{20,28},{12,20},{4,12},{1,5},{9... | collective-permute-start | bytes 786440 | tf_op jit(solution)/shard_map/ppermute | solution.py:234
  28.7 6.8 %collective-permute-start.6 = (bf16[256,256]{1,0:T(8,128)(2,1)S(1)}, bf16[256,256]{1,0:T(8,128)(2,1)S(1)}, u32[]{:S(2)}, u32[]{:S(2)}) collective-permute-start(bf16[256,256]{1,0:T(8,128)(2,1)S(1)} %collective-permute-done.5.rest_4_), channel_id=1, source_target_pairs={{0,4},{8,0},{16,8},{24,16},{28,24},{20,28},{12,20},{4,12},{1,5},{9... | collective-permute-start | bytes 393224 | tf_op jit(solution)/shard_map/ppermute | solution.py:234
  32.8 17.7 %collective-permute-start.16 = (bf16[512,256]{1,0:T(8,128)(2,1)S(1)}, bf16[512,256]{1,0:T(8,128)(2,1)S(1)}, u32[]{:S(2)}, u32[]{:S(2)}) collective-permute-start(bf16[512,256]{1,0:T(8,128)(2,1)S(1)} %collective-permute-done.12.rest_4_), channel_id=1, source_target_pairs={{0,4},{8,0},{16,8},{24,16},{28,24},{20,28},{12,20},{4,12},{1,5},{9... | collective-permute-start | bytes 786440 | tf_op jit(solution)/shard_map/ppermute | solution.py:234
  34.3 22.5 %collective-permute-start.15 = (bf16[512,256]{1,0:T(8,128)(2,1)S(1)}, bf16[512,256]{1,0:T(8,128)(2,1)S(1)}, u32[]{:S(2)}, u32[]{:S(2)}) collective-permute-start(bf16[512,256]{1,0:T(8,128)(2,1)S(1)} %collective-permute-done.11.rest_3_), channel_id=1, source_target_pairs={{0,8},{8,16},{16,24},{24,28},{28,20},{20,12},{12,4},{4,0},{1,9},{9... | collective-permute-start | bytes 786440 | tf_op jit(solution)/shard_map/ppermute | solution.py:234
  41.3 7.3 %collective-permute-start.7 = (bf16[128,256]{1,0:T(8,128)(2,1)S(1)}, bf16[128,256]{1,0:T(8,128)(2,1)S(1)}, u32[]{:S(2)}, u32[]{:S(2)}) collective-permute-start(bf16[128,256]{1,0:T(8,128)(2,1)S(1)} %slice.19), channel_id=1, source_target_pairs={{0,4},{8,0},{16,8},{24,16},{28,24},{20,28},{12,20},{4,12},{1,5},{9... | collective-permute-start | bytes 196616 | tf_op jit(solution)/shard_map/ppermute | solution.py:234
  42.9 13.9 %collective-permute-start.18 = (bf16[512,256]{1,0:T(8,128)(2,1)S(1)}, bf16[512,256]{1,0:T(8,128)(2,1)S(1)}, u32[]{:S(2)}, u32[]{:S(2)}) collective-permute-start(bf16[512,256]{1,0:T(8,128)(2,1)S(1)} %collective-permute-done.14.rest_6_), channel_id=1, source_target_pairs={{0,8},{8,16},{16,24},{24,28},{28,20},{20,12},{12,4},{4,0},{1,9},{9... | collective-permute-start | bytes 786440 | tf_op jit(solution)/shard_map/ppermute | solution.py:234
  43.4 13.5 %collective-permute-start.21 = (bf16[512,256]{1,0:T(8,128)(2,1)S(1)}, bf16[512,256]{1,0:T(8,128)(2,1)S(1)}, u32[]{:S(2)}, u32[]{:S(2)}) collective-permute-start(bf16[512,256]{1,0:T(8,128)(2,1)S(1)} %collective-permute-done.17.rest_9_), channel_id=1, source_target_pairs={{0,4},{8,0},{16,8},{24,16},{28,24},{20,28},{12,20},{4,12},{1,5},{9... | collective-permute-start | bytes 786440 | tf_op jit(solution)/shard_map/ppermute | solution.py:234
  50.4 8.5 %collective-permute-start.8 = (bf16[256,512]{1,0:T(8,128)(2,1)S(1)}, bf16[256,512]{1,0:T(8,128)(2,1)S(1)}, u32[]{:S(2)}, u32[]{:S(2)}) collective-permute-start(bf16[256,512]{1,0:T(8,128)(2,1)S(1)} %attend.3.a_ref), channel_id=1, source_target_pairs={{0,1},{1,0},{2,3},{3,2},{4,5},{5,4},{6,7},{7,6},{8,9},{9,8},{10,11... | collective-permute-start | bytes 786440 | tf_op jit(solution)/shard_map/ppermute | solution.py:287
  50.5 13.0 %collective-permute-start.20 = (bf16[512,256]{1,0:T(8,128)(2,1)S(1)}, bf16[512,256]{1,0:T(8,128)(2,1)S(1)}, u32[]{:S(2)}, u32[]{:S(2)}) collective-permute-start(bf16[512,256]{1,0:T(8,128)(2,1)S(1)} %collective-permute-done.16.rest_8_), channel_id=1, source_target_pairs={{0,4},{8,0},{16,8},{24,16},{28,24},{20,28},{12,20},{4,12},{1,5},{9... | collective-permute-start | bytes 786440 | tf_op jit(solution)/shard_map/ppermute | solution.py:234
  56.8 9.2 %collective-permute-start.19 = (bf16[512,256]{1,0:T(8,128)(2,1)S(1)}, bf16[512,256]{1,0:T(8,128)(2,1)S(1)}, u32[]{:S(2)}, u32[]{:S(2)}) collective-permute-start(bf16[512,256]{1,0:T(8,128)(2,1)S(1)} %collective-permute-done.15.rest_7_), channel_id=1, source_target_pairs={{0,8},{8,16},{16,24},{24,28},{28,20},{20,12},{12,4},{4,0},{1,9},{9... | collective-permute-start | bytes 786440 | tf_op jit(solution)/shard_map/ppermute | solution.py:234
  56.8 14.0 %collective-permute-start.22 = (bf16[512,256]{1,0:T(8,128)(2,1)S(1)}, bf16[512,256]{1,0:T(8,128)(2,1)S(1)}, u32[]{:S(2)}, u32[]{:S(2)}) collective-permute-start(bf16[512,256]{1,0:T(8,128)(2,1)S(1)} %collective-permute-done.18.rest_0_), channel_id=1, source_target_pairs={{0,8},{8,16},{16,24},{24,28},{28,20},{20,12},{12,4},{4,0},{1,9},{9... | collective-permute-start | bytes 786440 | tf_op jit(solution)/shard_map/ppermute | solution.py:234
  56.9 13.9 %collective-permute-start.23 = (bf16[512,256]{1,0:T(8,128)(2,1)S(1)}, bf16[512,256]{1,0:T(8,128)(2,1)S(1)}, u32[]{:S(2)}, u32[]{:S(2)}) collective-permute-start(bf16[512,256]{1,0:T(8,128)(2,1)S(1)} %collective-permute-done.21.rest_3_), channel_id=1, source_target_pairs={{0,4},{8,0},{16,8},{24,16},{28,24},{20,28},{12,20},{4,12},{1,5},{9... | collective-permute-start | bytes 786440 | tf_op jit(solution)/shard_map/ppermute | solution.py:234
  66.9 11.0 %collective-permute-start.25 = (bf16[2,256,256]{2,1,0:T(8,128)(2,1)S(1)}, bf16[2,256,256]{2,1,0:T(8,128)(2,1)S(1)}, u32[]{:S(2)}, u32[]{:S(2)}) collective-permute-start(bf16[2,256,256]{2,1,0:T(8,128)(2,1)S(1)} %get-tuple-element.27), channel_id=1, source_target_pairs={{0,2},{1,3},{2,0},{3,1},{4,6},{5,7},{6,4},{7,5},{8,10},{9,11},{10,... | collective-permute-start | bytes 786440 | tf_op jit(solution)/shard_map/ppermute | solution.py:313
  68.5 9.4 %collective-permute-start.24 = (bf16[1,256,256]{2,1,0:T(8,128)(2,1)S(1)}, bf16[1,256,256]{2,1,0:T(8,128)(2,1)S(1)}, u32[]{:S(2)}, u32[]{:S(2)}) collective-permute-start(bf16[1,256,256]{2,1,0:T(8,128)(2,1)S(1)} %get-tuple-element.26), channel_id=1, source_target_pairs={{0,2},{1,3},{2,0},{3,1},{4,6},{5,7},{6,4},{7,5},{8,10},{9,11},{10,... | collective-permute-start | bytes 393224 | tf_op jit(solution)/shard_map/ppermute | solution.py:313
  71.1 8.2 %collective-permute-start.26 = (bf16[1,256,256]{2,1,0:T(8,128)(2,1)S(1)}, bf16[1,256,256]{2,1,0:T(8,128)(2,1)S(1)}, u32[]{:S(2)}, u32[]{:S(2)}) collective-permute-start(bf16[1,256,256]{2,1,0:T(8,128)(2,1)S(1)} %get-tuple-element.28), channel_id=1, source_target_pairs={{0,2},{1,3},{2,0},{3,1},{4,6},{5,7},{6,4},{7,5},{8,10},{9,11},{10,... | collective-permute-start | bytes 393224 | tf_op jit(solution)/shard_map/ppermute | solution.py:313
  (9 other events, 83.1 us)

commit v3 on v2

--- a/solution.py
+++ b/solution.py
@@ -36,15 +36,15 @@
     return list(range(0, n, 2)) + list(range(n - 1, 0, -2))
 
 
-def attention_kernel(span, group, sources, first, order_ref, docid_ref, docs_ref, q_ref, *rest):
+def attention_kernel(n, span, group, sources, first, order_ref, docid_ref, docs_ref, q_ref, *rest):
     many = len(sources[0])
     split = 1 if first else 2
     kv_refs, rest = rest[: many * split], rest[many * split :]
-    spans = [(ref, at) for ref in kv_refs for at in range(0, ref.shape[0], span)]
     if first:
-        top_ref, sum_ref, mix_ref, s_ref, m_ref = rest
+        top_ref, sum_ref, mix_ref, s_ref, m_ref, kv_ref, slot_ref, pos_ref = rest
     else:
-        top_in, sum_in, mix_in, out_ref, s_ref, m_ref, sum_ref, mix_ref = rest
+        top_in, sum_in, mix_in, out_ref, s_ref, m_ref, kv_ref, slot_ref, pos_ref, *rest = rest
+        sum_ref, mix_ref = rest
     base2 = math.log2(math.e) / math.sqrt(DH)
     mine = lax.axis_index("seq")
     dims = (((1,), (1,)), ((), ()))
@@ -52,58 +52,79 @@
     for i in range(many):
         source = lookup([row[i] for row in sources], mine)
         kposs += [order_ref[2 * source], order_ref[2 * source + 1]]
+    j = 0
+    for ref in kv_refs:
+        for at in range(0, ref.shape[0], span):
+            kv_ref[j] = ref[at : at + span, :]
+            j += 1
+    ahead = lax.broadcasted_iota(jnp.int32, (span, span), 1) - lax.broadcasted_iota(
+        jnp.int32, (span, span), 0
+    )
 
     for part in range(2):
         rows = pl.ds(part * span, span)
         qpos = order_ref[2 * mine + part]
-        q = jnp.concatenate(
-            [q_ref[rows, h * DH : (h + 1) * DH] for h in range(group)], axis=0
-        )
         qdoc = jnp.transpose(
             jnp.broadcast_to(docs_ref[pl.ds(qpos, 1), :], (span, span)).astype(jnp.float32)
         )
         qfirst = docid_ref[qpos * span]
-        ahead = lax.broadcasted_iota(jnp.int32, (span, span), 1) - lax.broadcasted_iota(
-            jnp.int32, (span, span), 0
-        )
+        count = jnp.int32(0)
+        for j, k in enumerate(kposs):
+            slot_ref[count] = j
+            pos_ref[count] = k
+            live = (k <= qpos) & (docid_ref[k * span + span - 1] >= qfirst)
+            count += live.astype(jnp.int32)
+        slot_ref[count] = 0
+        pos_ref[count] = qpos + 2 * n
+        pairs = (count + 1) // 2
         m_ref[...] = jnp.full_like(m_ref, -1e30)
-        lives = [(k <= qpos) & (docid_ref[k * span + span - 1] >= qfirst) for k in kposs]
-
-        for j in range(2 * many):
-
-            @pl.when(lives[j])
-            def _():
-                k = spans[j][0][spans[j][1] : spans[j][1] + span, :DH]
-                s = lax.dot_general(q, k, dims, preferred_element_type=jnp.float32)
-                kdoc = docs_ref[pl.ds(kposs[j], 1), :].astype(jnp.float32)
-                visible = (qdoc == kdoc) & (ahead <= (qpos - kposs[j]) * span)
-                s = jnp.where(visible[None], s.reshape(group, span, span), -1e30)
-                s = s.reshape(group * span, span)
-                s_ref[:, j * span : (j + 1) * span] = s
-                m_ref[...] = jnp.maximum(m_ref[...], s)
-
+
+        def score(i, carry):
+            bias, k = [], []
+            for e in range(2):
+                slot, kpos = slot_ref[2 * i + e], pos_ref[2 * i + e]
+                kdoc = docs_ref[pl.ds(jnp.minimum(kpos, 2 * n - 1), 1), :].astype(jnp.float32)
+                visible = (qdoc == kdoc) & (ahead <= (qpos - kpos) * span)
+                bias.append(jnp.where(visible, 0.0, -1e30))
+                k.append(kv_ref[slot, :, :DH])
+            bias, k = jnp.concatenate(bias, axis=1), jnp.concatenate(k, axis=0)
+            for h in range(group):
+                q = q_ref[rows, h * DH : (h + 1) * DH]
+                s = lax.dot_general(q, k, dims, preferred_element_type=jnp.float32) + bias
+                at = slice(h * span, (h + 1) * span)
+                s_ref[i, at, :] = s
+                m_ref[at, :] = jnp.maximum(m_ref[at, :], jnp.maximum(s[:, :span], s[:, span:]))
+            return carry
+
+        lax.fori_loop(0, pairs, score, 0)
         largest = jnp.max(m_ref[...], axis=1, keepdims=True) * base2
         if first:
-            top_ref[part] = jnp.broadcast_to(largest, m_ref.shape)
+            m_ref[...] = jnp.broadcast_to(largest, m_ref.shape)
+            top_ref[part] = m_ref[...]
             sum_ref[part] = jnp.zeros_like(m_ref)
             mix_ref[part] = jnp.zeros_like(m_ref)
         else:
             before = top_in[part]
             largest = jnp.maximum(before, largest)
             fade = jnp.exp2(before - largest)
+            m_ref[...] = largest
             sum_ref[part] = sum_in[part] * fade
             mix_ref[part] = mix_in[part] * fade
 
-        for j in range(2 * many):
-
-            @pl.when(lives[j])
-            def _():
-                p = jnp.exp2(s_ref[:, j * span : (j + 1) * span] * base2 - largest)
-                sum_ref[part] += p
-                v = spans[j][0][spans[j][1] : spans[j][1] + span, DH:]
-                mix_ref[part] += jnp.dot(
-                    p.astype(jnp.bfloat16), v, preferred_element_type=jnp.float32
-                )
+        def mix(i, carry):
+            v = jnp.concatenate([kv_ref[slot_ref[2 * i + e], :, DH:] for e in range(2)], axis=0)
+            for h in range(group):
+                at = slice(h * span, (h + 1) * span)
+                top = m_ref[at, :]
+                s = s_ref[i, at, :]
+                p0 = jnp.exp2(s[:, :span] * base2 - top)
+                p1 = jnp.exp2(s[:, span:] * base2 - top)
+                sum_ref[part, at, :] += p0 + p1
+                p = jnp.concatenate([p0.astype(jnp.bfloat16), p1.astype(jnp.bfloat16)], axis=1)
+                mix_ref[part, at, :] += jnp.dot(p, v, preferred_element_type=jnp.float32)
+            return carry
+
+        lax.fori_loop(0, pairs, mix, 0)
 
         if not first:
             total = jnp.sum(sum_ref[part], axis=1, keepdims=True)
@@ -246,11 +267,14 @@
         got.append([move("up", ups[0]), move("dn", downs[1])])
         return got
 
-    kv = gather([jnp.concatenate([keys, values], axis=1)])
     half = width // 2
+    both = jnp.concatenate([keys, values], axis=1)
+    left, right, both = lax.optimization_barrier(
+        (out_weight[:, :half], out_weight[:, half:], both)
+    )
+    kv = gather([both])
     first = (lax.axis_index("head") & 1) == 0
-    mine = jnp.where(first, out_weight[:, :half], out_weight[:, half:])
-    other = jnp.where(first, out_weight[:, half:], out_weight[:, :half])
+    mine, other = jnp.where(first, left, right), jnp.where(first, right, left)
     beside = [(h, h ^ 1) for h in range(heads)]
     other = lax.ppermute(other, "head", beside)
     w = gather([mine, other])
@@ -263,12 +287,23 @@
         args = [queries] + [piece for i in slots for piece in kv[i]] + state
         return pl.pallas_call(
             functools.partial(
-                attention_kernel, span, group, [[row[i] for i in slots] for row in sources], first
+                attention_kernel,
+                n,
+                span,
+                group,
+                [[row[i] for i in slots] for row in sources],
+                first,
             ),
             out_shape=out_shape,
             in_specs=[SMEM, SMEM] + [VMEM] * (1 + len(args)),
             out_specs=jax.tree.map(lambda _: VMEM, out_shape),
-            scratch_shapes=[pltpu.VMEM((group * span, 2 * len(slots) * span), jnp.float32), block]
+            scratch_shapes=[
+                pltpu.VMEM((len(slots), group * span, 2 * span), jnp.float32),
+                block,
+                pltpu.VMEM((2 * len(slots), span, 2 * DH), jnp.bfloat16),
+                pltpu.SMEM((2 * len(slots) + 1,), jnp.int32),
+                pltpu.SMEM((2 * len(slots) + 1,), jnp.int32),
+            ]
             + ([] if first else [states, states]),
             compiler_params=limit(16),
             cost_estimate=pl.CostEstimate(

time: 82.1 us -> 80.6 us (0.982)
  starting transfers between devices: 33.4 us -> 32.3 us
  other arithmetic: 1.1 us -> 0.06 us
  Pallas kernels: 9.78 us -> 8.91 us
  local copies, waits for them, and re-layouts: 0.3 us -> 1.13 us
    slice x0 -> x1, local copies, waits for them, and re-layouts: none -> 1.1 us  [ring_device(): out_weight[:, half:]]
    ppermute x22, starting transfers between devices: 29 us -> 27.9 us  [move(): return lax.ppermute(x, 'seq', pairs)]
    select_n x1, other arithmetic: 1.1 us -> 0.04 us  [ring_device(): mine, other = (jnp.where(first, left, right), jnp.where(first, right, left))]
    pallas_call x2, Pallas kernels: 5.4 us -> 4.54 us  [attend(): pl.pallas_call(functools.partial(attention_kernel, n, span, group, [[row[...]
  transfers between devices with their start and end apart: 28 -> 28, of which waited for: 12 -> 11; matrix products, arithmetic and copies ran while one was open for 0% -> 0% of each run, Pallas kernels for 11% -> 10%
where the time goes in v3:
time: 80.6 us; the launch traced here: 80.5 us
  waiting for transfers between devices  37.9 us (47%)
  starting transfers between devices  32.3 us (40%)
  Pallas kernels  8.91 us (11%)
  local copies, waits for them, and re-layouts  1.13 us (1%)
    ppermute x22, waiting for transfers between devices, move(): return lax.ppermute(x, 'seq', pairs)  29.8 us
    ppermute x22, starting transfers between devices, move(): return lax.ppermute(x, 'seq', pairs)  27.9 us
    ppermute x3, waiting for transfers between devices, ring_device(): came.append(lax.ppermute(send, 'head', across))  6.59 us
    pallas_call x2, Pallas kernels, attend(): pl.pallas_call(functools.partial(attention_kernel, n, span, group, [[row[...  4.54 us
    ppermute x3, starting transfers between devices, ring_device(): came.append(lax.ppermute(send, 'head', across))  3.66 us
    pallas_call x3, Pallas kernels, ring_device(): pl.pallas_call(functools.partial(project_kernel, codes, moved), out_shape...  3.31 us
  transfers between devices with their start and end apart: 28, of which 11 were waited for; matrix products, arithmetic and copies ran while one was open for 0% of the time, Pallas kernels for 10%

profile of v3, /device:TPU:0, one launch (start us, length us, event | category | flops | bytes accessed | tf_op | source)
XLA Modules:
  0.0 80.5 jit_solution(14037056830060758471)
XLA Ops:
  1.8 2.6 %collective-permute-start = (bf16[256,256]{1,0:T(8,128)(2,1)S(1)}, bf16[256,256]{1,0:T(8,128)(2,1)S(1)}, u32[]{:S(2)}, u32[]{:S(2)}) collective-permute-start(bf16[256,256]{1,0:T(8,128)(2,1)S(1)} %pad_maximum_fusion.rest_0_), channel_id=1, source_target_pairs={{0,8},{8,16},{16,24},{24,28},{28,20},{20,12},{12,4},{4,0},{1,9},{9... | collective-permute-start | bytes 393224 | tf_op jit(solution)/shard_map/ppermute | solution.py:255
  4.4 1.6 %collective-permute-start.10 = (bf16[512,256]{1,0:T(8,128)(2,1)S(1)}, bf16[512,256]{1,0:T(8,128)(2,1)S(1)}, u32[]{:S(2)}, u32[]{:S(2)}) collective-permute-start(bf16[512,256]{1,0:T(8,128)(2,1)S(1)} %get-tuple-element.38.rest_0_), channel_id=1, source_target_pairs={{0,8},{8,16},{16,24},{24,28},{28,20},{20,12},{12,4},{4,0},{1,9},{9... | collective-permute-start | bytes 786440 | tf_op jit(solution)/shard_map/ppermute | solution.py:255
  8.7 2.1 %collective-permute-start.1 = (bf16[256,256]{1,0:T(8,128)(2,1)S(1)}, bf16[256,256]{1,0:T(8,128)(2,1)S(1)}, u32[]{:S(2)}, u32[]{:S(2)}) collective-permute-start(bf16[256,256]{1,0:T(8,128)(2,1)S(1)} %collective-permute-done.rest_1_), channel_id=1, source_target_pairs={{0,8},{8,16},{16,24},{24,28},{28,20},{20,12},{12,4},{4,0},{1,9},{9... | collective-permute-start | bytes 393224 | tf_op jit(solution)/shard_map/ppermute | solution.py:255
  10.8 7.2 %collective-permute-done.4.rest_2_ = bf16[256,256]{1,0:T(8,128)(2,1)S(1)} collective-permute-done((bf16[256,256]{1,0:T(8,128)(2,1)S(1)}, bf16[256,256]{1,0:T(8,128)(2,1)S(1)}, u32[]{:S(2)}, u32[]{:S(2)}) %collective-permute-start.4) | collective-permute-done | bytes 131104 | tf_op jit(solution)/shard_map/ppermute | solution.py:255
  18.4 1.6 %collective-permute-start.11 = (bf16[512,256]{1,0:T(8,128)(2,1)S(1)}, bf16[512,256]{1,0:T(8,128)(2,1)S(1)}, u32[]{:S(2)}, u32[]{:S(2)}) collective-permute-start(bf16[512,256]{1,0:T(8,128)(2,1)S(1)} %collective-permute-done.9.rest_1_), channel_id=1, source_target_pairs={{0,8},{8,16},{16,24},{24,28},{28,20},{20,12},{12,4},{4,0},{1,9},{9... | collective-permute-start | bytes 786440 | tf_op jit(solution)/shard_map/ppermute | solution.py:255
  20.0 1.6 %collective-permute-start.14 = (bf16[512,256]{1,0:T(8,128)(2,1)S(1)}, bf16[512,256]{1,0:T(8,128)(2,1)S(1)}, u32[]{:S(2)}, u32[]{:S(2)}) collective-permute-start(bf16[512,256]{1,0:T(8,128)(2,1)S(1)} %collective-permute-done.10.rest_2_), channel_id=1, source_target_pairs={{0,8},{8,16},{16,24},{24,28},{28,20},{20,12},{12,4},{4,0},{1,9},{9... | collective-permute-start | bytes 786440 | tf_op jit(solution)/shard_map/ppermute | solution.py:255
  22.0 4.4 %collective-permute-done.5.rest_4_ = bf16[256,256]{1,0:T(8,128)(2,1)S(1)} collective-permute-done((bf16[256,256]{1,0:T(8,128)(2,1)S(1)}, bf16[256,256]{1,0:T(8,128)(2,1)S(1)}, u32[]{:S(2)}, u32[]{:S(2)}) %collective-permute-start.5) | collective-permute-done | bytes 131104 | tf_op jit(solution)/shard_map/ppermute | solution.py:255
  26.4 1.6 %collective-permute-start.2 = (bf16[256,256]{1,0:T(8,128)(2,1)S(1)}, bf16[256,256]{1,0:T(8,128)(2,1)S(1)}, u32[]{:S(2)}, u32[]{:S(2)}) collective-permute-start(bf16[256,256]{1,0:T(8,128)(2,1)S(1)} %collective-permute-done.1.rest_3_), channel_id=1, source_target_pairs={{0,8},{8,16},{16,24},{24,28},{28,20},{20,12},{12,4},{4,0},{1,9},{9... | collective-permute-start | bytes 393224 | tf_op jit(solution)/shard_map/ppermute | solution.py:255
  28.4 4.9 %collective-permute-done.2.rest_5_ = bf16[256,256]{1,0:T(8,128)(2,1)S(1)} collective-permute-done((bf16[256,256]{1,0:T(8,128)(2,1)S(1)}, bf16[256,256]{1,0:T(8,128)(2,1)S(1)}, u32[]{:S(2)}, u32[]{:S(2)}) %collective-permute-start.2) | collective-permute-done | bytes 131104 | tf_op jit(solution)/shard_map/ppermute | solution.py:255
  35.4 1.6 %collective-permute-start.3 = (bf16[128,256]{1,0:T(8,128)(2,1)S(1)}, bf16[128,256]{1,0:T(8,128)(2,1)S(1)}, u32[]{:S(2)}, u32[]{:S(2)}) collective-permute-start(bf16[128,256]{1,0:T(8,128)(2,1)S(1)} %slice.16), channel_id=1, source_target_pairs={{0,8},{8,16},{16,24},{24,28},{28,20},{20,12},{12,4},{4,0},{1,9},{9... | collective-permute-start | bytes 196616 | tf_op jit(solution)/shard_map/ppermute | solution.py:255
  37.0 5.1 %collective-permute-done.3.rest_0_ = bf16[128,256]{1,0:T(8,128)(2,1)S(1)} collective-permute-done((bf16[128,256]{1,0:T(8,128)(2,1)S(1)}, bf16[128,256]{1,0:T(8,128)(2,1)S(1)}, u32[]{:S(2)}, u32[]{:S(2)}) %collective-permute-start.3) | collective-permute-done | bytes 65568 | tf_op jit(solution)/shard_map/ppermute | solution.py:255
  42.1 1.6 %collective-permute-start.7 = (bf16[128,256]{1,0:T(8,128)(2,1)S(1)}, bf16[128,256]{1,0:T(8,128)(2,1)S(1)}, u32[]{:S(2)}, u32[]{:S(2)}) collective-permute-start(bf16[128,256]{1,0:T(8,128)(2,1)S(1)} %slice.17), channel_id=1, source_target_pairs={{0,4},{8,0},{16,8},{24,16},{28,24},{20,28},{12,20},{4,12},{1,5},{9... | collective-permute-start | bytes 196616 | tf_op jit(solution)/shard_map/ppermute | solution.py:255
  44.2 1.6 %collective-permute-start.21 = (bf16[512,256]{1,0:T(8,128)(2,1)S(1)}, bf16[512,256]{1,0:T(8,128)(2,1)S(1)}, u32[]{:S(2)}, u32[]{:S(2)}) collective-permute-start(bf16[512,256]{1,0:T(8,128)(2,1)S(1)} %collective-permute-done.17.rest_9_), channel_id=1, source_target_pairs={{0,4},{8,0},{16,8},{24,16},{28,24},{20,28},{12,20},{4,12},{1,5},{9... | collective-permute-start | bytes 786440 | tf_op jit(solution)/shard_map/ppermute | solution.py:255
  45.8 2.6 %attend.2 = (f32[2,512,128]{2,1,0:T(8,128)S(1)}, f32[2,512,128]{2,1,0:T(8,128)S(1)}, f32[2,512,128]{2,1,0:T(8,128)S(1)}) custom-call(s32[16]{0:T(128)S(1)} %copy-done.2, s32[2048]{0:T(1024)S(1)} %copy-done.1, s32[16,128]{1,0:T(8,128)S(1)} %bitcast.1, bf16[256,512]{1,0:T(8,128)(2,1)S(1)} %copy-done, bf16[256,256]{1,0:T(8,128)(2,1)S(1)} %pad_maximum_fusion.rest_0_, ...), custom_call_target="tpu_custom_call" | custom-call | flops 939524096 | bytes 917504 | tf_op jit(solution)/shard_map/attend/pallas_call | solution.py:288
  48.4 1.9 %attend.3.a_ref = bf16[256,512]{1,0:T(8,128)(2,1)S(1)} custom-call(s32[16]{0:T(128)S(1)} %copy-done.2, s32[2048]{0:T(1024)S(1)} %copy-done.1, s32[16,128]{1,0:T(8,128)S(1)} %bitcast.2, bf16[256,512]{1,0:T(8,128)(2,1)S(1)} %copy-done, bf16[128,256]{1,0:T(8,128)(2,1)S(1)} %collective-permute-done.3.rest_0_, ...), custom_call_target="tpu_custom_call" | custom-call | flops 134217728 | bytes 131072 | tf_op jit(solution)/shard_map/attend/pallas_call | solution.py:288
  50.4 4.9 %collective-permute-start.20 = (bf16[512,256]{1,0:T(8,128)(2,1)S(1)}, bf16[512,256]{1,0:T(8,128)(2,1)S(1)}, u32[]{:S(2)}, u32[]{:S(2)}) collective-permute-start(bf16[512,256]{1,0:T(8,128)(2,1)S(1)} %collective-permute-done.16.rest_8_), channel_id=1, source_target_pairs={{0,4},{8,0},{16,8},{24,16},{28,24},{20,28},{12,20},{4,12},{1,5},{9... | collective-permute-start | bytes 786440 | tf_op jit(solution)/shard_map/ppermute | solution.py:255
  55.4 2.0 %collective-permute-start.23 = (bf16[512,256]{1,0:T(8,128)(2,1)S(1)}, bf16[512,256]{1,0:T(8,128)(2,1)S(1)}, u32[]{:S(2)}, u32[]{:S(2)}) collective-permute-start(bf16[512,256]{1,0:T(8,128)(2,1)S(1)} %collective-permute-done.21.rest_3_), channel_id=1, source_target_pairs={{0,4},{8,0},{16,8},{24,16},{28,24},{20,28},{12,20},{4,12},{1,5},{9... | collective-permute-start | bytes 786440 | tf_op jit(solution)/shard_map/ppermute | solution.py:255
  57.4 2.0 %project.3 = (bf16[1,256,256]{2,1,0:T(8,128)(2,1)S(1)}, bf16[1,256,256]{2,1,0:T(8,128)(2,1)S(1)}, bf16[3,256,256]{2,1,0:T(8,128)(2,1)S(1)}) custom-call(bf16[256,512]{1,0:T(8,128)(2,1)S(1)} %attend.3.a_ref, bf16[256,512]{1,0:T(8,128)(2,1)S(1)} %collective-permute-done.8.b_ref, bf16[512,256]{1,0:T(8,128)(2,1)S(1)} %get-tuple-element.38.rest_0_, ...), custom_call_target="tpu_custom_call" | custom-call | flops 671088640 | bytes 2621440 | tf_op jit(solution)/shard_map/project/pallas_call | solution.py:335
  59.4 2.6 %collective-permute-done.20.rest_2_ = bf16[512,256]{1,0:T(8,128)(2,1)S(1)} collective-permute-done((bf16[512,256]{1,0:T(8,128)(2,1)S(1)}, bf16[512,256]{1,0:T(8,128)(2,1)S(1)}, u32[]{:S(2)}, u32[]{:S(2)}) %collective-permute-start.20) | collective-permute-done | bytes 262176 | tf_op jit(solution)/shard_map/ppermute | solution.py:255
  62.0 2.5 %collective-permute-done.19.rest_1_ = bf16[512,256]{1,0:T(8,128)(2,1)S(1)} collective-permute-done((bf16[512,256]{1,0:T(8,128)(2,1)S(1)}, bf16[512,256]{1,0:T(8,128)(2,1)S(1)}, u32[]{:S(2)}, u32[]{:S(2)}) %collective-permute-start.19) | collective-permute-done | bytes 262176 | tf_op jit(solution)/shard_map/ppermute | solution.py:255
  65.4 1.6 %collective-permute-start.25 = (bf16[2,256,256]{2,1,0:T(8,128)(2,1)S(1)}, bf16[2,256,256]{2,1,0:T(8,128)(2,1)S(1)}, u32[]{:S(2)}, u32[]{:S(2)}) collective-permute-start(bf16[2,256,256]{2,1,0:T(8,128)(2,1)S(1)} %get-tuple-element.33), channel_id=1, source_target_pairs={{0,2},{1,3},{2,0},{3,1},{4,6},{5,7},{6,4},{7,5},{8,10},{9,11},{10,... | collective-permute-start | bytes 786440 | tf_op jit(solution)/shard_map/ppermute | solution.py:348
  67.5 1.8 %collective-permute-done.22.rest_0_ = bf16[512,256]{1,0:T(8,128)(2,1)S(1)} collective-permute-done((bf16[512,256]{1,0:T(8,128)(2,1)S(1)}, bf16[512,256]{1,0:T(8,128)(2,1)S(1)}, u32[]{:S(2)}, u32[]{:S(2)}) %collective-permute-start.22) | collective-permute-done | bytes 262176 | tf_op jit(solution)/shard_map/ppermute | solution.py:255
  69.6 1.6 %collective-permute-start.26 = (bf16[1,256,256]{2,1,0:T(8,128)(2,1)S(1)}, bf16[1,256,256]{2,1,0:T(8,128)(2,1)S(1)}, u32[]{:S(2)}, u32[]{:S(2)}) collective-permute-start(bf16[1,256,256]{2,1,0:T(8,128)(2,1)S(1)} %get-tuple-element.34), channel_id=1, source_target_pairs={{0,2},{1,3},{2,0},{3,1},{4,6},{5,7},{6,4},{7,5},{8,10},{9,11},{10,... | collective-permute-start | bytes 393224 | tf_op jit(solution)/shard_map/ppermute | solution.py:348
  71.2 5.2 %collective-permute-done.24.rest_3_ = bf16[1,256,256]{2,1,0:T(8,128)(2,1)S(1)} collective-permute-done((bf16[1,256,256]{2,1,0:T(8,128)(2,1)S(1)}, bf16[1,256,256]{2,1,0:T(8,128)(2,1)S(1)}, u32[]{:S(2)}, u32[]{:S(2)}) %collective-permute-start.24) | collective-permute-done | bytes 131104 | tf_op jit(solution)/shard_map/ppermute | solution.py:348
  (54 shorter events, 14.3 us)
Async XLA Ops:
  1.8 6.9 %collective-permute-start = (bf16[256,256]{1,0:T(8,128)(2,1)S(1)}, bf16[256,256]{1,0:T(8,128)(2,1)S(1)}, u32[]{:S(2)}, u32[]{:S(2)}) collective-permute-start(bf16[256,256]{1,0:T(8,128)(2,1)S(1)} %pad_maximum_fusion.rest_0_), channel_id=1, source_target_pairs={{0,8},{8,16},{16,24},{24,28},{28,20},{20,12},{12,4},{4,0},{1,9},{9... | collective-permute-start | bytes 393224 | tf_op jit(solution)/shard_map/ppermute | solution.py:255
  4.4 15.6 %collective-permute-start.10 = (bf16[512,256]{1,0:T(8,128)(2,1)S(1)}, bf16[512,256]{1,0:T(8,128)(2,1)S(1)}, u32[]{:S(2)}, u32[]{:S(2)}) collective-permute-start(bf16[512,256]{1,0:T(8,128)(2,1)S(1)} %get-tuple-element.38.rest_0_), channel_id=1, source_target_pairs={{0,8},{8,16},{16,24},{24,28},{28,20},{20,12},{12,4},{4,0},{1,9},{9... | collective-permute-start | bytes 786440 | tf_op jit(solution)/shard_map/ppermute | solution.py:255
  6.0 15.6 %collective-permute-start.13 = (bf16[512,256]{1,0:T(8,128)(2,1)S(1)}, bf16[512,256]{1,0:T(8,128)(2,1)S(1)}, u32[]{:S(2)}, u32[]{:S(2)}) collective-permute-start(bf16[512,256]{1,0:T(8,128)(2,1)S(1)} %collective-permute-done.9.rest_1_), channel_id=1, source_target_pairs={{0,4},{8,0},{16,8},{24,16},{28,24},{20,28},{12,20},{4,12},{1,5},{9... | collective-permute-start | bytes 786440 | tf_op jit(solution)/shard_map/ppermute | solution.py:255
  6.4 11.5 %collective-permute-start.4 = (bf16[256,256]{1,0:T(8,128)(2,1)S(1)}, bf16[256,256]{1,0:T(8,128)(2,1)S(1)}, u32[]{:S(2)}, u32[]{:S(2)}) collective-permute-start(bf16[256,256]{1,0:T(8,128)(2,1)S(1)} %pad_maximum_fusion.rest_0_), channel_id=1, source_target_pairs={{0,4},{8,0},{16,8},{24,16},{28,24},{20,28},{12,20},{4,12},{1,5},{9... | collective-permute-start | bytes 393224 | tf_op jit(solution)/shard_map/ppermute | solution.py:255
  8.7 9.8 %collective-permute-start.1 = (bf16[256,256]{1,0:T(8,128)(2,1)S(1)}, bf16[256,256]{1,0:T(8,128)(2,1)S(1)}, u32[]{:S(2)}, u32[]{:S(2)}) collective-permute-start(bf16[256,256]{1,0:T(8,128)(2,1)S(1)} %collective-permute-done.rest_1_), channel_id=1, source_target_pairs={{0,8},{8,16},{16,24},{24,28},{28,20},{20,12},{12,4},{4,0},{1,9},{9... | collective-permute-start | bytes 393224 | tf_op jit(solution)/shard_map/ppermute | solution.py:255
  10.8 17.2 %collective-permute-start.12 = (bf16[512,256]{1,0:T(8,128)(2,1)S(1)}, bf16[512,256]{1,0:T(8,128)(2,1)S(1)}, u32[]{:S(2)}, u32[]{:S(2)}) collective-permute-start(bf16[512,256]{1,0:T(8,128)(2,1)S(1)} %get-tuple-element.38.rest_0_), channel_id=1, source_target_pairs={{0,4},{8,0},{16,8},{24,16},{28,24},{20,28},{12,20},{4,12},{1,5},{9... | collective-permute-start | bytes 786440 | tf_op jit(solution)/shard_map/ppermute | solution.py:255
  18.0 8.4 %collective-permute-start.5 = (bf16[256,256]{1,0:T(8,128)(2,1)S(1)}, bf16[256,256]{1,0:T(8,128)(2,1)S(1)}, u32[]{:S(2)}, u32[]{:S(2)}) collective-permute-start(bf16[256,256]{1,0:T(8,128)(2,1)S(1)} %collective-permute-done.4.rest_2_), channel_id=1, source_target_pairs={{0,4},{8,0},{16,8},{24,16},{28,24},{20,28},{12,20},{4,12},{1,5},{9... | collective-permute-start | bytes 393224 | tf_op jit(solution)/shard_map/ppermute | solution.py:255
  18.4 16.4 %collective-permute-start.11 = (bf16[512,256]{1,0:T(8,128)(2,1)S(1)}, bf16[512,256]{1,0:T(8,128)(2,1)S(1)}, u32[]{:S(2)}, u32[]{:S(2)}) collective-permute-start(bf16[512,256]{1,0:T(8,128)(2,1)S(1)} %collective-permute-done.9.rest_1_), channel_id=1, source_target_pairs={{0,8},{8,16},{16,24},{24,28},{28,20},{20,12},{12,4},{4,0},{1,9},{9... | collective-permute-start | bytes 786440 | tf_op jit(solution)/shard_map/ppermute | solution.py:255
  20.0 23.7 %collective-permute-start.14 = (bf16[512,256]{1,0:T(8,128)(2,1)S(1)}, bf16[512,256]{1,0:T(8,128)(2,1)S(1)}, u32[]{:S(2)}, u32[]{:S(2)}) collective-permute-start(bf16[512,256]{1,0:T(8,128)(2,1)S(1)} %collective-permute-done.10.rest_2_), channel_id=1, source_target_pairs={{0,8},{8,16},{16,24},{24,28},{28,20},{20,12},{12,4},{4,0},{1,9},{9... | collective-permute-start | bytes 786440 | tf_op jit(solution)/shard_map/ppermute | solution.py:255
  21.6 22.6 %collective-permute-start.17 = (bf16[512,256]{1,0:T(8,128)(2,1)S(1)}, bf16[512,256]{1,0:T(8,128)(2,1)S(1)}, u32[]{:S(2)}, u32[]{:S(2)}) collective-permute-start(bf16[512,256]{1,0:T(8,128)(2,1)S(1)} %collective-permute-done.13.rest_5_), channel_id=1, source_target_pairs={{0,4},{8,0},{16,8},{24,16},{28,24},{20,28},{12,20},{4,12},{1,5},{9... | collective-permute-start | bytes 786440 | tf_op jit(solution)/shard_map/ppermute | solution.py:255
  26.4 7.0 %collective-permute-start.2 = (bf16[256,256]{1,0:T(8,128)(2,1)S(1)}, bf16[256,256]{1,0:T(8,128)(2,1)S(1)}, u32[]{:S(2)}, u32[]{:S(2)}) collective-permute-start(bf16[256,256]{1,0:T(8,128)(2,1)S(1)} %collective-permute-done.1.rest_3_), channel_id=1, source_target_pairs={{0,8},{8,16},{16,24},{24,28},{28,20},{20,12},{12,4},{4,0},{1,9},{9... | collective-permute-start | bytes 393224 | tf_op jit(solution)/shard_map/ppermute | solution.py:255
  28.0 7.4 %collective-permute-start.6 = (bf16[256,256]{1,0:T(8,128)(2,1)S(1)}, bf16[256,256]{1,0:T(8,128)(2,1)S(1)}, u32[]{:S(2)}, u32[]{:S(2)}) collective-permute-start(bf16[256,256]{1,0:T(8,128)(2,1)S(1)} %collective-permute-done.5.rest_4_), channel_id=1, source_target_pairs={{0,4},{8,0},{16,8},{24,16},{28,24},{20,28},{12,20},{4,12},{1,5},{9... | collective-permute-start | bytes 393224 | tf_op jit(solution)/shard_map/ppermute | solution.py:255
  33.4 17.0 %collective-permute-start.16 = (bf16[512,256]{1,0:T(8,128)(2,1)S(1)}, bf16[512,256]{1,0:T(8,128)(2,1)S(1)}, u32[]{:S(2)}, u32[]{:S(2)}) collective-permute-start(bf16[512,256]{1,0:T(8,128)(2,1)S(1)} %collective-permute-done.12.rest_4_), channel_id=1, source_target_pairs={{0,4},{8,0},{16,8},{24,16},{28,24},{20,28},{12,20},{4,12},{1,5},{9... | collective-permute-start | bytes 786440 | tf_op jit(solution)/shard_map/ppermute | solution.py:255
  34.8 20.5 %collective-permute-start.15 = (bf16[512,256]{1,0:T(8,128)(2,1)S(1)}, bf16[512,256]{1,0:T(8,128)(2,1)S(1)}, u32[]{:S(2)}, u32[]{:S(2)}) collective-permute-start(bf16[512,256]{1,0:T(8,128)(2,1)S(1)} %collective-permute-done.11.rest_3_), channel_id=1, source_target_pairs={{0,8},{8,16},{16,24},{24,28},{28,20},{20,12},{12,4},{4,0},{1,9},{9... | collective-permute-start | bytes 786440 | tf_op jit(solution)/shard_map/ppermute | solution.py:255
  43.7 11.6 %collective-permute-start.18 = (bf16[512,256]{1,0:T(8,128)(2,1)S(1)}, bf16[512,256]{1,0:T(8,128)(2,1)S(1)}, u32[]{:S(2)}, u32[]{:S(2)}) collective-permute-start(bf16[512,256]{1,0:T(8,128)(2,1)S(1)} %collective-permute-done.14.rest_6_), channel_id=1, source_target_pairs={{0,8},{8,16},{16,24},{24,28},{28,20},{20,12},{12,4},{4,0},{1,9},{9... | collective-permute-start | bytes 786440 | tf_op jit(solution)/shard_map/ppermute | solution.py:255
  44.2 11.2 %collective-permute-start.21 = (bf16[512,256]{1,0:T(8,128)(2,1)S(1)}, bf16[512,256]{1,0:T(8,128)(2,1)S(1)}, u32[]{:S(2)}, u32[]{:S(2)}) collective-permute-start(bf16[512,256]{1,0:T(8,128)(2,1)S(1)} %collective-permute-done.17.rest_9_), channel_id=1, source_target_pairs={{0,4},{8,0},{16,8},{24,16},{28,24},{20,28},{12,20},{4,12},{1,5},{9... | collective-permute-start | bytes 786440 | tf_op jit(solution)/shard_map/ppermute | solution.py:255
  50.3 7.1 %collective-permute-start.8 = (bf16[256,512]{1,0:T(8,128)(2,1)S(1)}, bf16[256,512]{1,0:T(8,128)(2,1)S(1)}, u32[]{:S(2)}, u32[]{:S(2)}) collective-permute-start(bf16[256,512]{1,0:T(8,128)(2,1)S(1)} %attend.3.a_ref), channel_id=1, source_target_pairs={{0,1},{1,0},{2,3},{3,2},{4,5},{5,4},{6,7},{7,6},{8,9},{9,8},{10,11... | collective-permute-start | bytes 786440 | tf_op jit(solution)/shard_map/ppermute | solution.py:322
  50.4 11.6 %collective-permute-start.20 = (bf16[512,256]{1,0:T(8,128)(2,1)S(1)}, bf16[512,256]{1,0:T(8,128)(2,1)S(1)}, u32[]{:S(2)}, u32[]{:S(2)}) collective-permute-start(bf16[512,256]{1,0:T(8,128)(2,1)S(1)} %collective-permute-done.16.rest_8_), channel_id=1, source_target_pairs={{0,4},{8,0},{16,8},{24,16},{28,24},{20,28},{12,20},{4,12},{1,5},{9... | collective-permute-start | bytes 786440 | tf_op jit(solution)/shard_map/ppermute | solution.py:255
  55.3 9.2 %collective-permute-start.19 = (bf16[512,256]{1,0:T(8,128)(2,1)S(1)}, bf16[512,256]{1,0:T(8,128)(2,1)S(1)}, u32[]{:S(2)}, u32[]{:S(2)}) collective-permute-start(bf16[512,256]{1,0:T(8,128)(2,1)S(1)} %collective-permute-done.15.rest_7_), channel_id=1, source_target_pairs={{0,8},{8,16},{16,24},{24,28},{28,20},{20,12},{12,4},{4,0},{1,9},{9... | collective-permute-start | bytes 786440 | tf_op jit(solution)/shard_map/ppermute | solution.py:255
  55.3 14.0 %collective-permute-start.22 = (bf16[512,256]{1,0:T(8,128)(2,1)S(1)}, bf16[512,256]{1,0:T(8,128)(2,1)S(1)}, u32[]{:S(2)}, u32[]{:S(2)}) collective-permute-start(bf16[512,256]{1,0:T(8,128)(2,1)S(1)} %collective-permute-done.18.rest_0_), channel_id=1, source_target_pairs={{0,8},{8,16},{16,24},{24,28},{28,20},{20,12},{12,4},{4,0},{1,9},{9... | collective-permute-start | bytes 786440 | tf_op jit(solution)/shard_map/ppermute | solution.py:255
  55.4 13.9 %collective-permute-start.23 = (bf16[512,256]{1,0:T(8,128)(2,1)S(1)}, bf16[512,256]{1,0:T(8,128)(2,1)S(1)}, u32[]{:S(2)}, u32[]{:S(2)}) collective-permute-start(bf16[512,256]{1,0:T(8,128)(2,1)S(1)} %collective-permute-done.21.rest_3_), channel_id=1, source_target_pairs={{0,4},{8,0},{16,8},{24,16},{28,24},{20,28},{12,20},{4,12},{1,5},{9... | collective-permute-start | bytes 786440 | tf_op jit(solution)/shard_map/ppermute | solution.py:255
  65.4 11.0 %collective-permute-start.25 = (bf16[2,256,256]{2,1,0:T(8,128)(2,1)S(1)}, bf16[2,256,256]{2,1,0:T(8,128)(2,1)S(1)}, u32[]{:S(2)}, u32[]{:S(2)}) collective-permute-start(bf16[2,256,256]{2,1,0:T(8,128)(2,1)S(1)} %get-tuple-element.33), channel_id=1, source_target_pairs={{0,2},{1,3},{2,0},{3,1},{4,6},{5,7},{6,4},{7,5},{8,10},{9,11},{10,... | collective-permute-start | bytes 786440 | tf_op jit(solution)/shard_map/ppermute | solution.py:348
  67.0 9.4 %collective-permute-start.24 = (bf16[1,256,256]{2,1,0:T(8,128)(2,1)S(1)}, bf16[1,256,256]{2,1,0:T(8,128)(2,1)S(1)}, u32[]{:S(2)}, u32[]{:S(2)}) collective-permute-start(bf16[1,256,256]{2,1,0:T(8,128)(2,1)S(1)} %get-tuple-element.32), channel_id=1, source_target_pairs={{0,2},{1,3},{2,0},{3,1},{4,6},{5,7},{6,4},{7,5},{8,10},{9,11},{10,... | collective-permute-start | bytes 393224 | tf_op jit(solution)/shard_map/ppermute | solution.py:348
  69.6 8.2 %collective-permute-start.26 = (bf16[1,256,256]{2,1,0:T(8,128)(2,1)S(1)}, bf16[1,256,256]{2,1,0:T(8,128)(2,1)S(1)}, u32[]{:S(2)}, u32[]{:S(2)}) collective-permute-start(bf16[1,256,256]{2,1,0:T(8,128)(2,1)S(1)} %get-tuple-element.34), channel_id=1, source_target_pairs={{0,2},{1,3},{2,0},{3,1},{4,6},{5,7},{6,4},{7,5},{8,10},{9,11},{10,... | collective-permute-start | bytes 393224 | tf_op jit(solution)/shard_map/ppermute | solution.py:348
  (9 other events, 119.5 us)

commit v4 on v3

--- a/solution.py
+++ b/solution.py
@@ -14,6 +14,7 @@
 NONE = -1000
 VMEM = pl.BlockSpec(memory_space=pltpu.VMEM)
 SMEM = pl.BlockSpec(memory_space=pltpu.SMEM)
+HBM = pl.BlockSpec(memory_space=pltpu.HBM)
 SEND, KEEP, HOLD, NONE = 0, 5, 10, 15
 
 
@@ -158,10 +159,11 @@
         put(lookup(values, me), c.astype(jnp.bfloat16))
 
 
-def fold_kernel(codes, per, *rest):
+def fold_kernel(codes, spans, per, *rest):
     kept, came, (own_ref, send_ref) = rest[: len(codes)], rest[len(codes) : -2], rest[-2:]
     me = place()
     for r, slots in enumerate(codes):
+        cols = slice(*spans[r])
         for i, values in enumerate(slots):
             at = lookup(values, me)
 
@@ -172,27 +174,32 @@
 
                 @pl.when(at < per)
                 def _():
-                    own_ref[at] = c
+                    own_ref[at, :, cols] = c
 
                 @pl.when(at >= per)
                 def _():
-                    send_ref[at - per] = c
-
-
-def finish_kernel(own_ref, came_ref, out_ref):
-    core = lax.axis_index("head") & 1
-    per, _, half = own_ref.shape
+                    send_ref[at - per, :, cols] = c
+
+
+def finish_kernel(side, part_ref, *rest):
+    out_ref, sem = rest[-2:]
+    per, _, half = part_ref.shape
+    core = (lax.axis_index("head") & 1) ^ side
+    copies = []
     for part in range(per):
-        for ref, side in ((own_ref, core), (came_ref, 1 - core)):
-            start = pl.multiple_of((2 * part + side) * half, LANES)
-            out_ref[:, pl.ds(start, half)] = ref[part]
+        start = pl.multiple_of((2 * part + core) * half, LANES)
+        columns = out_ref.at[:, pl.ds(start, half)]
+        copies.append(pltpu.make_async_copy(part_ref.at[part], columns, sem.at[part]))
+        copies[-1].start()
+    for copy in copies:
+        copy.wait()
 
 
 def reduce_plan(n, heads, sources, rounds):
     per = n // heads
     devices = [(s, h) for s in range(n) for h in range(heads)]
-    first = n // 2 - sum(len(places) for places in rounds[1:])
-    caps = [max(1, first)] + [len(places) for places in rounds[1:]]
+    caps = [max(1, n // 2 - len(rounds[1]))] + [len(places) for places in rounds[1:]]
+    sources = [row + row[-1:] for row in sources]
     turns = {}
     for s in range(n):
         for owners in (0, 2):
@@ -200,7 +207,7 @@
             for r, places in enumerate(rounds):
                 for p in places:
                     if (sources[s][p] // per) & 2 == owners:
-                        at = next(k for k in range(r, len(caps)) if room[k])
+                        at = next(k for k in (r, *range(r + 1, 2)) if room[k])
                         room[at] -= 1
                         turns[s, p] = at
     plan = []
@@ -263,8 +270,12 @@
             got += [list(ups), list(downs)]
         if len(pieces) == 1:
             rows = pieces[0].shape[0] // 2
-            ups, downs = [ups[0][:rows], None], [None, downs[0][rows:]]
-        got.append([move("up", ups[0]), move("dn", downs[1])])
+            parts = [(ups[0][:rows], downs[0][rows:])]
+        else:
+            cols = pieces[0].shape[1] // 2
+            parts = [(ups[0][:, :cols], downs[1][:, :cols]), (ups[0][:, cols:], downs[1][:, cols:])]
+        for up, down in parts:
+            got.append([move("up", up), move("dn", down)])
         return got
 
     half = width // 2
@@ -321,17 +332,20 @@
     )
     paired = lax.ppermute(attended, "head", beside)
 
-    def block(count):
-        return jax.ShapeDtypeStruct((count, tok_rows, half), jnp.bfloat16)
-
-    rounds = [list(range(n - 3)), [n - 3, n - 2], [n - 1]]
+    def block(count, cols):
+        return jax.ShapeDtypeStruct((count, tok_rows, cols), jnp.bfloat16)
+
+    rounds = [list(range(n - 3)), [n - 3, n - 2], [n - 1], [n]]
+    quarter = half // 2
+    spans = [(0, half), (0, half), (0, quarter), (quarter, half)]
     across = [(h, h ^ 2) for h in range(heads)]
     kept, came, ends, held = [], [], [], []
     for r, (codes, moved, count, hold, end) in enumerate(
         reduce_plan(n, heads, sources, rounds)
     ):
         pieces = [piece for p in rounds[r] for piece in w[p]]
-        outs = (block(count), block(count)) + ((block(hold),) if hold else ())
+        cols = spans[r][1] - spans[r][0]
+        outs = (block(count, cols),) * 2 + ((block(hold, cols),) if hold else ())
         send, keep, *rest = pl.pallas_call(
             functools.partial(project_kernel, codes, moved),
             out_shape=outs,
@@ -339,8 +353,8 @@
             out_specs=(VMEM,) * len(outs),
             compiler_params=limit(8),
             cost_estimate=pl.CostEstimate(
-                flops=2 * tok_rows * group * DH * half * len(pieces),
-                bytes_accessed=2 * group * DH * half * len(pieces),
+                flops=2 * tok_rows * group * DH * cols * len(pieces),
+                bytes_accessed=2 * group * DH * cols * len(pieces),
                 transcendentals=0,
             ),
             name="project",
@@ -351,22 +365,28 @@
         ends.append(end)
 
     own, send = pl.pallas_call(
-        functools.partial(fold_kernel, ends, per),
-        out_shape=(block(per), block(per)),
+        functools.partial(fold_kernel, ends, spans, per),
+        out_shape=(block(per, half),) * 2,
         in_specs=[VMEM] * (2 * len(ends)),
         out_specs=(VMEM, VMEM),
         compiler_params=limit(8),
         name="fold",
     )(*kept, *came)
     joined = lax.ppermute(send, "head", beside)
-    return pl.pallas_call(
-        finish_kernel,
-        out_shape=jax.ShapeDtypeStruct((tok_rows, per * width), jnp.bfloat16),
-        in_specs=[VMEM, VMEM],
-        out_specs=VMEM,
-        compiler_params=limit(8),
-        name="finish",
-    )(own, joined)
+
+    def finish(side, part, *out):
+        return pl.pallas_call(
+            functools.partial(finish_kernel, side),
+            out_shape=jax.ShapeDtypeStruct((tok_rows, per * width), jnp.bfloat16),
+            in_specs=[VMEM] + [HBM] * len(out),
+            out_specs=HBM,
+            input_output_aliases={1: 0} if out else {},
+            scratch_shapes=[pltpu.SemaphoreType.DMA((per,))],
+            compiler_params=limit(4),
+            name="finish",
+        )(part, *out)
+
+    return finish(1, joined, finish(0, own))
 
 
 def on_device(queries, keys, values, doc_ids, span_order, out_weight):
@@ -456,7 +476,7 @@
             and heads == 4
             and keys.shape[1] == DH
             and span % LANES == 0
-            and out_weight.shape[1] % (2 * LANES) == 0
+            and out_weight.shape[1] % (4 * LANES) == 0
         )
         args = (queries, keys, values, doc_ids, span_order, out_weight)
         if not ring:

time: 80.6 us -> 87.3 us (1.083)
  starting transfers between devices: 32.3 us -> 36.9 us
  waiting for transfers between devices: 37.9 us -> 39.2 us
    ppermute x22 -> x24, waiting for transfers between devices: 29.8 us -> 34.9 us  [move(): return lax.ppermute(x, 'seq', pairs)]
    ppermute x22 -> x24, starting transfers between devices: 27.9 us -> 31.6 us  [move(): return lax.ppermute(x, 'seq', pairs)]
    ppermute x3 -> x4, waiting for transfers between devices: 6.59 us -> 3.47 us  [ring_device(): came.append(lax.ppermute(send, 'head', across))]
    ppermute x3 -> x4, starting transfers between devices: 3.66 us -> 4.61 us  [ring_device(): came.append(lax.ppermute(send, 'head', across))]
    pallas_call x3 -> x4, Pallas kernels: 3.31 us -> 3.5 us  [ring_device(): pl.pallas_call(functools.partial(project_kernel, codes, moved), out_shape...]
  transfers between devices with their start and end apart: 28 -> 31, of which waited for: 11 -> 15; matrix products, arithmetic and copies ran while one was open for 0% -> 0% of each run, Pallas kernels for 10% -> 10%
where the time goes in v4:
time: 87.3 us; the launch traced here: 87.2 us
  waiting for transfers between devices  39.2 us (45%)
  starting transfers between devices  36.9 us (42%)
  Pallas kernels  9.7 us (11%)
  local copies, waits for them, and re-layouts  1.17 us (1%)
    ppermute x24, waiting for transfers between devices, move(): return lax.ppermute(x, 'seq', pairs)  34.9 us
    ppermute x24, starting transfers between devices, move(): return lax.ppermute(x, 'seq', pairs)  31.6 us
    ppermute x4, starting transfers between devices, ring_device(): came.append(lax.ppermute(send, 'head', across))  4.61 us
    pallas_call x2, Pallas kernels, attend(): pl.pallas_call(functools.partial(attention_kernel, n, span, group, [[row[...  4.55 us
    pallas_call x4, Pallas kernels, ring_device(): pl.pallas_call(functools.partial(project_kernel, codes, moved), out_shape...  3.5 us
    ppermute x4, waiting for transfers between devices, ring_device(): came.append(lax.ppermute(send, 'head', across))  3.47 us
  transfers between devices with their start and end apart: 31, of which 15 were waited for; matrix products, arithmetic and copies ran while one was open for 0% of the time, Pallas kernels for 10%

profile of v4, /device:TPU:0, one launch (start us, length us, event | category | flops | bytes accessed | tf_op | source)
XLA Modules:
  0.0 87.2 jit_solution(2332173893646668256)
XLA Ops:
  1.8 2.6 %collective-permute-start = (bf16[256,256]{1,0:T(8,128)(2,1)S(1)}, bf16[256,256]{1,0:T(8,128)(2,1)S(1)}, u32[]{:S(2)}, u32[]{:S(2)}) collective-permute-start(bf16[256,256]{1,0:T(8,128)(2,1)S(1)} %pad_maximum_fusion.rest_0_), channel_id=1, source_target_pairs={{0,8},{8,16},{16,24},{24,28},{28,20},{20,12},{12,4},{4,0},{1,9},{9... | collective-permute-start | bytes 393224 | tf_op jit(solution)/shard_map/ppermute | solution.py:262
  6.4 2.2 %collective-permute-done.rest_1_ = bf16[256,256]{1,0:T(8,128)(2,1)S(1)} collective-permute-done((bf16[256,256]{1,0:T(8,128)(2,1)S(1)}, bf16[256,256]{1,0:T(8,128)(2,1)S(1)}, u32[]{:S(2)}, u32[]{:S(2)}) %collective-permute-start) | collective-permute-done | bytes 131104 | tf_op jit(solution)/shard_map/ppermute | solution.py:262
  8.7 2.1 %collective-permute-start.1 = (bf16[256,256]{1,0:T(8,128)(2,1)S(1)}, bf16[256,256]{1,0:T(8,128)(2,1)S(1)}, u32[]{:S(2)}, u32[]{:S(2)}) collective-permute-start(bf16[256,256]{1,0:T(8,128)(2,1)S(1)} %collective-permute-done.rest_1_), channel_id=1, source_target_pairs={{0,8},{8,16},{16,24},{24,28},{28,20},{20,12},{12,4},{4,0},{1,9},{9... | collective-permute-start | bytes 393224 | tf_op jit(solution)/shard_map/ppermute | solution.py:262
  13.3 3.8 %collective-permute-done.1.rest_3_ = bf16[256,256]{1,0:T(8,128)(2,1)S(1)} collective-permute-done((bf16[256,256]{1,0:T(8,128)(2,1)S(1)}, bf16[256,256]{1,0:T(8,128)(2,1)S(1)}, u32[]{:S(2)}, u32[]{:S(2)}) %collective-permute-start.1) | collective-permute-done | bytes 131104 | tf_op jit(solution)/shard_map/ppermute | solution.py:262
  17.1 2.0 %collective-permute-start.13 = (bf16[512,256]{1,0:T(8,128)(2,1)S(1)}, bf16[512,256]{1,0:T(8,128)(2,1)S(1)}, u32[]{:S(2)}, u32[]{:S(2)}) collective-permute-start(bf16[512,256]{1,0:T(8,128)(2,1)S(1)} %collective-permute-done.9.rest_1_), channel_id=1, source_target_pairs={{0,4},{8,0},{16,8},{24,16},{28,24},{20,28},{12,20},{4,12},{1,5},{9... | collective-permute-start | bytes 786440 | tf_op jit(solution)/shard_map/ppermute | solution.py:262
  19.2 2.6 %collective-permute-done.5.rest_4_ = bf16[256,256]{1,0:T(8,128)(2,1)S(1)} collective-permute-done((bf16[256,256]{1,0:T(8,128)(2,1)S(1)}, bf16[256,256]{1,0:T(8,128)(2,1)S(1)}, u32[]{:S(2)}, u32[]{:S(2)}) %collective-permute-start.5) | collective-permute-done | bytes 131104 | tf_op jit(solution)/shard_map/ppermute | solution.py:262
  21.9 1.6 %collective-permute-start.2 = (bf16[256,256]{1,0:T(8,128)(2,1)S(1)}, bf16[256,256]{1,0:T(8,128)(2,1)S(1)}, u32[]{:S(2)}, u32[]{:S(2)}) collective-permute-start(bf16[256,256]{1,0:T(8,128)(2,1)S(1)} %collective-permute-done.1.rest_3_), channel_id=1, source_target_pairs={{0,8},{8,16},{16,24},{24,28},{28,20},{20,12},{12,4},{4,0},{1,9},{9... | collective-permute-start | bytes 393224 | tf_op jit(solution)/shard_map/ppermute | solution.py:262
  23.9 7.0 %collective-permute-done.2.rest_5_ = bf16[256,256]{1,0:T(8,128)(2,1)S(1)} collective-permute-done((bf16[256,256]{1,0:T(8,128)(2,1)S(1)}, bf16[256,256]{1,0:T(8,128)(2,1)S(1)}, u32[]{:S(2)}, u32[]{:S(2)}) %collective-permute-start.2) | collective-permute-done | bytes 131104 | tf_op jit(solution)/shard_map/ppermute | solution.py:262
  30.9 1.7 %collective-permute-start.16 = (bf16[512,256]{1,0:T(8,128)(2,1)S(1)}, bf16[512,256]{1,0:T(8,128)(2,1)S(1)}, u32[]{:S(2)}, u32[]{:S(2)}) collective-permute-start(bf16[512,256]{1,0:T(8,128)(2,1)S(1)} %collective-permute-done.12.rest_4_), channel_id=1, source_target_pairs={{0,4},{8,0},{16,8},{24,16},{28,24},{20,28},{12,20},{4,12},{1,5},{9... | collective-permute-start | bytes 786440 | tf_op jit(solution)/shard_map/ppermute | solution.py:262
  32.9 1.7 %collective-permute-start.17 = (bf16[512,256]{1,0:T(8,128)(2,1)S(1)}, bf16[512,256]{1,0:T(8,128)(2,1)S(1)}, u32[]{:S(2)}, u32[]{:S(2)}) collective-permute-start(bf16[512,256]{1,0:T(8,128)(2,1)S(1)} %collective-permute-done.13.rest_5_), channel_id=1, source_target_pairs={{0,4},{8,0},{16,8},{24,16},{28,24},{20,28},{12,20},{4,12},{1,5},{9... | collective-permute-start | bytes 786440 | tf_op jit(solution)/shard_map/ppermute | solution.py:262
  35.0 1.9 %collective-permute-start.3 = (bf16[128,256]{1,0:T(8,128)(2,1)S(1)}, bf16[128,256]{1,0:T(8,128)(2,1)S(1)}, u32[]{:S(2)}, u32[]{:S(2)}) collective-permute-start(bf16[128,256]{1,0:T(8,128)(2,1)S(1)} %slice.32), channel_id=1, source_target_pairs={{0,8},{8,16},{16,24},{24,28},{28,20},{20,12},{12,4},{4,0},{1,9},{9... | collective-permute-start | bytes 196616 | tf_op jit(solution)/shard_map/ppermute | solution.py:262
  36.9 10.3 %collective-permute-done.3.rest_0_ = bf16[128,256]{1,0:T(8,128)(2,1)S(1)} collective-permute-done((bf16[128,256]{1,0:T(8,128)(2,1)S(1)}, bf16[128,256]{1,0:T(8,128)(2,1)S(1)}, u32[]{:S(2)}, u32[]{:S(2)}) %collective-permute-start.3) | collective-permute-done | bytes 65568 | tf_op jit(solution)/shard_map/ppermute | solution.py:262
  48.8 2.7 %attend.2 = (f32[2,512,128]{2,1,0:T(8,128)S(1)}, f32[2,512,128]{2,1,0:T(8,128)S(1)}, f32[2,512,128]{2,1,0:T(8,128)S(1)}) custom-call(s32[16]{0:T(128)S(1)} %copy-done.2, s32[2048]{0:T(1024)S(1)} %copy-done.1, s32[16,128]{1,0:T(8,128)S(1)} %bitcast.1, bf16[256,512]{1,0:T(8,128)(2,1)S(1)} %copy-done, bf16[256,256]{1,0:T(8,128)(2,1)S(1)} %pad_maximum_fusion.rest_0_, ...), custom_call_target="tpu_custom_call" | custom-call | flops 939524096 | bytes 917504 | tf_op jit(solution)/shard_map/attend/pallas_call | solution.py:299
  51.5 1.9 %attend.3.a_ref = bf16[256,512]{1,0:T(8,128)(2,1)S(1)} custom-call(s32[16]{0:T(128)S(1)} %copy-done.2, s32[2048]{0:T(1024)S(1)} %copy-done.1, s32[16,128]{1,0:T(8,128)S(1)} %bitcast.2, bf16[256,512]{1,0:T(8,128)(2,1)S(1)} %copy-done, bf16[128,256]{1,0:T(8,128)(2,1)S(1)} %collective-permute-done.3.rest_0_, ...), custom_call_target="tpu_custom_call" | custom-call | flops 134217728 | bytes 131072 | tf_op jit(solution)/shard_map/attend/pallas_call | solution.py:299
  53.5 4.4 %collective-permute-start.20 = (bf16[512,256]{1,0:T(8,128)(2,1)S(1)}, bf16[512,256]{1,0:T(8,128)(2,1)S(1)}, u32[]{:S(2)}, u32[]{:S(2)}) collective-permute-start(bf16[512,256]{1,0:T(8,128)(2,1)S(1)} %collective-permute-done.16.rest_8_), channel_id=1, source_target_pairs={{0,4},{8,0},{16,8},{24,16},{28,24},{20,28},{12,20},{4,12},{1,5},{9... | collective-permute-start | bytes 786440 | tf_op jit(solution)/shard_map/ppermute | solution.py:262
  57.9 2.0 %collective-permute-start.21 = (bf16[512,256]{1,0:T(8,128)(2,1)S(1)}, bf16[512,256]{1,0:T(8,128)(2,1)S(1)}, u32[]{:S(2)}, u32[]{:S(2)}) collective-permute-start(bf16[512,256]{1,0:T(8,128)(2,1)S(1)} %collective-permute-done.17.rest_9_), channel_id=1, source_target_pairs={{0,4},{8,0},{16,8},{24,16},{28,24},{20,28},{12,20},{4,12},{1,5},{9... | collective-permute-start | bytes 786440 | tf_op jit(solution)/shard_map/ppermute | solution.py:262
  60.1 2.0 %project.4 = (bf16[2,256,256]{2,1,0:T(8,128)(2,1)S(1)}, bf16[2,256,256]{2,1,0:T(8,128)(2,1)S(1)}, bf16[2,256,256]{2,1,0:T(8,128)(2,1)S(1)}) custom-call(bf16[256,512]{1,0:T(8,128)(2,1)S(1)} %attend.3.a_ref, bf16[256,512]{1,0:T(8,128)(2,1)S(1)} %collective-permute-done.8.b_ref, bf16[512,256]{1,0:T(8,128)(2,1)S(1)} %get-tuple-element.40.rest_0_, ...), custom_call_target="tpu_custom_call" | custom-call | flops 671088640 | bytes 2621440 | tf_op jit(solution)/shard_map/project/pallas_call | solution.py:349
  64.6 2.5 %collective-permute-done.19.rest_1_ = bf16[512,256]{1,0:T(8,128)(2,1)S(1)} collective-permute-done((bf16[512,256]{1,0:T(8,128)(2,1)S(1)}, bf16[512,256]{1,0:T(8,128)(2,1)S(1)}, u32[]{:S(2)}, u32[]{:S(2)}) %collective-permute-start.19) | collective-permute-done | bytes 262176 | tf_op jit(solution)/shard_map/ppermute | solution.py:262
  67.1 2.6 %collective-permute-done.21.rest_3_ = bf16[512,256]{1,0:T(8,128)(2,1)S(1)} collective-permute-done((bf16[512,256]{1,0:T(8,128)(2,1)S(1)}, bf16[512,256]{1,0:T(8,128)(2,1)S(1)}, u32[]{:S(2)}, u32[]{:S(2)}) %collective-permute-start.21) | collective-permute-done | bytes 262176 | tf_op jit(solution)/shard_map/ppermute | solution.py:262
  70.6 1.6 %collective-permute-start.27 = (bf16[2,256,256]{2,1,0:T(8,128)(2,1)S(1)}, bf16[2,256,256]{2,1,0:T(8,128)(2,1)S(1)}, u32[]{:S(2)}, u32[]{:S(2)}) collective-permute-start(bf16[2,256,256]{2,1,0:T(8,128)(2,1)S(1)} %get-tuple-element.34), channel_id=1, source_target_pairs={{0,2},{1,3},{2,0},{3,1},{4,6},{5,7},{6,4},{7,5},{8,10},{9,11},{10,... | collective-permute-start | bytes 786440 | tf_op jit(solution)/shard_map/ppermute | solution.py:362
  72.2 2.5 %collective-permute-start.23 = (bf16[512,128]{1,0:T(8,128)(2,1)S(1)}, bf16[512,128]{1,0:T(8,128)(2,1)S(1)}, u32[]{:S(2)}, u32[]{:S(2)}) collective-permute-start(bf16[512,128]{1,0:T(8,128)(2,1)S(1)} %get-tuple-element.44), channel_id=1, source_target_pairs={{0,4},{8,0},{16,8},{24,16},{28,24},{20,28},{12,20},{4,12},{1,5},{9... | collective-permute-start | bytes 393224 | tf_op jit(solution)/shard_map/ppermute | solution.py:262
  74.7 2.0 %collective-permute-start.25 = (bf16[512,128]{1,0:T(8,128)(2,1)S(1)}, bf16[512,128]{1,0:T(8,128)(2,1)S(1)}, u32[]{:S(2)}, u32[]{:S(2)}) collective-permute-start(bf16[512,128]{1,0:T(8,128)(2,1)S(1)} %get-tuple-element.43), channel_id=1, source_target_pairs={{0,4},{8,0},{16,8},{24,16},{28,24},{20,28},{12,20},{4,12},{1,5},{9... | collective-permute-start | bytes 393224 | tf_op jit(solution)/shard_map/ppermute | solution.py:262
  76.7 1.7 %collective-permute-done.23.rest_1_ = bf16[512,128]{1,0:T(8,128)(2,1)S(1)} collective-permute-done((bf16[512,128]{1,0:T(8,128)(2,1)S(1)}, bf16[512,128]{1,0:T(8,128)(2,1)S(1)}, u32[]{:S(2)}, u32[]{:S(2)}) %collective-permute-start.23) | collective-permute-done | bytes 131104 | tf_op jit(solution)/shard_map/ppermute | solution.py:262
  81.2 2.2 %collective-permute-done.28.rest_6_ = bf16[1,256,128]{2,1,0:T(8,128)(2,1)S(1)} collective-permute-done((bf16[1,256,128]{2,1,0:T(8,128)(2,1)S(1)}, bf16[1,256,128]{2,1,0:T(8,128)(2,1)S(1)}, u32[]{:S(2)}, u32[]{:S(2)}) %collective-permute-start.28) | collective-permute-done | bytes 65568 | tf_op jit(solution)/shard_map/ppermute | solution.py:362
  (64 shorter events, 19.1 us)
Async XLA Ops:
  1.2 11.5 %collective-permute-start.9 = (bf16[512,256]{1,0:T(8,128)(2,1)S(1)}, bf16[512,256]{1,0:T(8,128)(2,1)S(1)}, u32[]{:S(2)}, u32[]{:S(2)}) collective-permute-start(bf16[512,256]{1,0:T(8,128)(2,1)S(1)} %get-tuple-element.39), channel_id=1, source_target_pairs={{0,1},{1,0},{2,3},{3,2},{4,5},{5,4},{6,7},{7,6},{8,9},{9,8},{10,11... | collective-permute-start | bytes 786440 | tf_op jit(solution)/shard_map/ppermute | solution.py:290
  1.8 6.9 %collective-permute-start = (bf16[256,256]{1,0:T(8,128)(2,1)S(1)}, bf16[256,256]{1,0:T(8,128)(2,1)S(1)}, u32[]{:S(2)}, u32[]{:S(2)}) collective-permute-start(bf16[256,256]{1,0:T(8,128)(2,1)S(1)} %pad_maximum_fusion.rest_0_), channel_id=1, source_target_pairs={{0,8},{8,16},{16,24},{24,28},{28,20},{20,12},{12,4},{4,0},{1,9},{9... | collective-permute-start | bytes 393224 | tf_op jit(solution)/shard_map/ppermute | solution.py:262
  4.4 14.7 %collective-permute-start.10 = (bf16[512,256]{1,0:T(8,128)(2,1)S(1)}, bf16[512,256]{1,0:T(8,128)(2,1)S(1)}, u32[]{:S(2)}, u32[]{:S(2)}) collective-permute-start(bf16[512,256]{1,0:T(8,128)(2,1)S(1)} %get-tuple-element.40.rest_0_), channel_id=1, source_target_pairs={{0,8},{8,16},{16,24},{24,28},{28,20},{20,12},{12,4},{4,0},{1,9},{9... | collective-permute-start | bytes 786440 | tf_op jit(solution)/shard_map/ppermute | solution.py:262
  8.7 8.4 %collective-permute-start.1 = (bf16[256,256]{1,0:T(8,128)(2,1)S(1)}, bf16[256,256]{1,0:T(8,128)(2,1)S(1)}, u32[]{:S(2)}, u32[]{:S(2)}) collective-permute-start(bf16[256,256]{1,0:T(8,128)(2,1)S(1)} %collective-permute-done.rest_1_), channel_id=1, source_target_pairs={{0,8},{8,16},{16,24},{24,28},{28,20},{20,12},{12,4},{4,0},{1,9},{9... | collective-permute-start | bytes 393224 | tf_op jit(solution)/shard_map/ppermute | solution.py:262
  10.8 12.7 %collective-permute-start.12 = (bf16[512,256]{1,0:T(8,128)(2,1)S(1)}, bf16[512,256]{1,0:T(8,128)(2,1)S(1)}, u32[]{:S(2)}, u32[]{:S(2)}) collective-permute-start(bf16[512,256]{1,0:T(8,128)(2,1)S(1)} %get-tuple-element.40.rest_0_), channel_id=1, source_target_pairs={{0,4},{8,0},{16,8},{24,16},{28,24},{20,28},{12,20},{4,12},{1,5},{9... | collective-permute-start | bytes 786440 | tf_op jit(solution)/shard_map/ppermute | solution.py:262
  11.3 10.6 %collective-permute-start.5 = (bf16[256,256]{1,0:T(8,128)(2,1)S(1)}, bf16[256,256]{1,0:T(8,128)(2,1)S(1)}, u32[]{:S(2)}, u32[]{:S(2)}) collective-permute-start(bf16[256,256]{1,0:T(8,128)(2,1)S(1)} %collective-permute-done.4.rest_2_), channel_id=1, source_target_pairs={{0,4},{8,0},{16,8},{24,16},{28,24},{20,28},{12,20},{4,12},{1,5},{9... | collective-permute-start | bytes 393224 | tf_op jit(solution)/shard_map/ppermute | solution.py:262
  12.7 19.9 %collective-permute-start.11 = (bf16[512,256]{1,0:T(8,128)(2,1)S(1)}, bf16[512,256]{1,0:T(8,128)(2,1)S(1)}, u32[]{:S(2)}, u32[]{:S(2)}) collective-permute-start(bf16[512,256]{1,0:T(8,128)(2,1)S(1)} %collective-permute-done.9.rest_1_), channel_id=1, source_target_pairs={{0,8},{8,16},{16,24},{24,28},{28,20},{20,12},{12,4},{4,0},{1,9},{9... | collective-permute-start | bytes 786440 | tf_op jit(solution)/shard_map/ppermute | solution.py:262
  17.1 15.8 %collective-permute-start.13 = (bf16[512,256]{1,0:T(8,128)(2,1)S(1)}, bf16[512,256]{1,0:T(8,128)(2,1)S(1)}, u32[]{:S(2)}, u32[]{:S(2)}) collective-permute-start(bf16[512,256]{1,0:T(8,128)(2,1)S(1)} %collective-permute-done.9.rest_1_), channel_id=1, source_target_pairs={{0,4},{8,0},{16,8},{24,16},{28,24},{20,28},{12,20},{4,12},{1,5},{9... | collective-permute-start | bytes 786440 | tf_op jit(solution)/shard_map/ppermute | solution.py:262
  19.1 15.6 %collective-permute-start.14 = (bf16[512,256]{1,0:T(8,128)(2,1)S(1)}, bf16[512,256]{1,0:T(8,128)(2,1)S(1)}, u32[]{:S(2)}, u32[]{:S(2)}) collective-permute-start(bf16[512,256]{1,0:T(8,128)(2,1)S(1)} %collective-permute-done.10.rest_2_), channel_id=1, source_target_pairs={{0,8},{8,16},{16,24},{24,28},{28,20},{20,12},{12,4},{4,0},{1,9},{9... | collective-permute-start | bytes 786440 | tf_op jit(solution)/shard_map/ppermute | solution.py:262
  21.9 9.0 %collective-permute-start.2 = (bf16[256,256]{1,0:T(8,128)(2,1)S(1)}, bf16[256,256]{1,0:T(8,128)(2,1)S(1)}, u32[]{:S(2)}, u32[]{:S(2)}) collective-permute-start(bf16[256,256]{1,0:T(8,128)(2,1)S(1)} %collective-permute-done.1.rest_3_), channel_id=1, source_target_pairs={{0,8},{8,16},{16,24},{24,28},{28,20},{20,12},{12,4},{4,0},{1,9},{9... | collective-permute-start | bytes 393224 | tf_op jit(solution)/shard_map/ppermute | solution.py:262
  23.5 11.5 %collective-permute-start.6 = (bf16[256,256]{1,0:T(8,128)(2,1)S(1)}, bf16[256,256]{1,0:T(8,128)(2,1)S(1)}, u32[]{:S(2)}, u32[]{:S(2)}) collective-permute-start(bf16[256,256]{1,0:T(8,128)(2,1)S(1)} %collective-permute-done.5.rest_4_), channel_id=1, source_target_pairs={{0,4},{8,0},{16,8},{24,16},{28,24},{20,28},{12,20},{4,12},{1,5},{9... | collective-permute-start | bytes 393224 | tf_op jit(solution)/shard_map/ppermute | solution.py:262
  30.9 22.5 %collective-permute-start.16 = (bf16[512,256]{1,0:T(8,128)(2,1)S(1)}, bf16[512,256]{1,0:T(8,128)(2,1)S(1)}, u32[]{:S(2)}, u32[]{:S(2)}) collective-permute-start(bf16[512,256]{1,0:T(8,128)(2,1)S(1)} %collective-permute-done.12.rest_4_), channel_id=1, source_target_pairs={{0,4},{8,0},{16,8},{24,16},{28,24},{20,28},{12,20},{4,12},{1,5},{9... | collective-permute-start | bytes 786440 | tf_op jit(solution)/shard_map/ppermute | solution.py:262
  32.7 25.2 %collective-permute-start.15 = (bf16[512,256]{1,0:T(8,128)(2,1)S(1)}, bf16[512,256]{1,0:T(8,128)(2,1)S(1)}, u32[]{:S(2)}, u32[]{:S(2)}) collective-permute-start(bf16[512,256]{1,0:T(8,128)(2,1)S(1)} %collective-permute-done.11.rest_3_), channel_id=1, source_target_pairs={{0,8},{8,16},{16,24},{24,28},{28,20},{20,12},{12,4},{4,0},{1,9},{9... | collective-permute-start | bytes 786440 | tf_op jit(solution)/shard_map/ppermute | solution.py:262
  32.9 25.0 %collective-permute-start.17 = (bf16[512,256]{1,0:T(8,128)(2,1)S(1)}, bf16[512,256]{1,0:T(8,128)(2,1)S(1)}, u32[]{:S(2)}, u32[]{:S(2)}) collective-permute-start(bf16[512,256]{1,0:T(8,128)(2,1)S(1)} %collective-permute-done.13.rest_5_), channel_id=1, source_target_pairs={{0,4},{8,0},{16,8},{24,16},{28,24},{20,28},{12,20},{4,12},{1,5},{9... | collective-permute-start | bytes 786440 | tf_op jit(solution)/shard_map/ppermute | solution.py:262
  34.7 25.2 %collective-permute-start.18 = (bf16[512,256]{1,0:T(8,128)(2,1)S(1)}, bf16[512,256]{1,0:T(8,128)(2,1)S(1)}, u32[]{:S(2)}, u32[]{:S(2)}) collective-permute-start(bf16[512,256]{1,0:T(8,128)(2,1)S(1)} %collective-permute-done.14.rest_6_), channel_id=1, source_target_pairs={{0,8},{8,16},{16,24},{24,28},{28,20},{20,12},{12,4},{4,0},{1,9},{9... | collective-permute-start | bytes 786440 | tf_op jit(solution)/shard_map/ppermute | solution.py:262
  35.0 12.2 %collective-permute-start.3 = (bf16[128,256]{1,0:T(8,128)(2,1)S(1)}, bf16[128,256]{1,0:T(8,128)(2,1)S(1)}, u32[]{:S(2)}, u32[]{:S(2)}) collective-permute-start(bf16[128,256]{1,0:T(8,128)(2,1)S(1)} %slice.32), channel_id=1, source_target_pairs={{0,8},{8,16},{16,24},{24,28},{28,20},{20,12},{12,4},{4,0},{1,9},{9... | collective-permute-start | bytes 196616 | tf_op jit(solution)/shard_map/ppermute | solution.py:262
  53.4 6.7 %collective-permute-start.8 = (bf16[256,512]{1,0:T(8,128)(2,1)S(1)}, bf16[256,512]{1,0:T(8,128)(2,1)S(1)}, u32[]{:S(2)}, u32[]{:S(2)}) collective-permute-start(bf16[256,512]{1,0:T(8,128)(2,1)S(1)} %attend.3.a_ref), channel_id=1, source_target_pairs={{0,1},{1,0},{2,3},{3,2},{4,5},{5,4},{6,7},{7,6},{8,9},{9,8},{10,11... | collective-permute-start | bytes 786440 | tf_op jit(solution)/shard_map/ppermute | solution.py:333
  53.5 11.1 %collective-permute-start.20 = (bf16[512,256]{1,0:T(8,128)(2,1)S(1)}, bf16[512,256]{1,0:T(8,128)(2,1)S(1)}, u32[]{:S(2)}, u32[]{:S(2)}) collective-permute-start(bf16[512,256]{1,0:T(8,128)(2,1)S(1)} %collective-permute-done.16.rest_8_), channel_id=1, source_target_pairs={{0,4},{8,0},{16,8},{24,16},{28,24},{20,28},{12,20},{4,12},{1,5},{9... | collective-permute-start | bytes 786440 | tf_op jit(solution)/shard_map/ppermute | solution.py:262
  57.9 9.2 %collective-permute-start.19 = (bf16[512,256]{1,0:T(8,128)(2,1)S(1)}, bf16[512,256]{1,0:T(8,128)(2,1)S(1)}, u32[]{:S(2)}, u32[]{:S(2)}) collective-permute-start(bf16[512,256]{1,0:T(8,128)(2,1)S(1)} %collective-permute-done.15.rest_7_), channel_id=1, source_target_pairs={{0,8},{8,16},{16,24},{24,28},{28,20},{20,12},{12,4},{4,0},{1,9},{9... | collective-permute-start | bytes 786440 | tf_op jit(solution)/shard_map/ppermute | solution.py:262
  57.9 11.8 %collective-permute-start.21 = (bf16[512,256]{1,0:T(8,128)(2,1)S(1)}, bf16[512,256]{1,0:T(8,128)(2,1)S(1)}, u32[]{:S(2)}, u32[]{:S(2)}) collective-permute-start(bf16[512,256]{1,0:T(8,128)(2,1)S(1)} %collective-permute-done.17.rest_9_), channel_id=1, source_target_pairs={{0,4},{8,0},{16,8},{24,16},{28,24},{20,28},{12,20},{4,12},{1,5},{9... | collective-permute-start | bytes 786440 | tf_op jit(solution)/shard_map/ppermute | solution.py:262
  59.9 14.8 %collective-permute-start.22 = (bf16[512,128]{1,0:T(8,128)(2,1)S(1)}, bf16[512,128]{1,0:T(8,128)(2,1)S(1)}, u32[]{:S(2)}, u32[]{:S(2)}) collective-permute-start(bf16[512,128]{1,0:T(8,128)(2,1)S(1)} %get-tuple-element.46), channel_id=1, source_target_pairs={{0,8},{8,16},{16,24},{24,28},{28,20},{20,12},{12,4},{4,0},{1,9},{9... | collective-permute-start | bytes 393224 | tf_op jit(solution)/shard_map/ppermute | solution.py:262
  62.1 19.1 %collective-permute-start.26 = (bf16[2,256,256]{2,1,0:T(8,128)(2,1)S(1)}, bf16[2,256,256]{2,1,0:T(8,128)(2,1)S(1)}, u32[]{:S(2)}, u32[]{:S(2)}) collective-permute-start(bf16[2,256,256]{2,1,0:T(8,128)(2,1)S(1)} %get-tuple-element.33), channel_id=1, source_target_pairs={{0,2},{1,3},{2,0},{3,1},{4,6},{5,7},{6,4},{7,5},{8,10},{9,11},{10,... | collective-permute-start | bytes 786440 | tf_op jit(solution)/shard_map/ppermute | solution.py:362
  70.6 14.1 %collective-permute-start.27 = (bf16[2,256,256]{2,1,0:T(8,128)(2,1)S(1)}, bf16[2,256,256]{2,1,0:T(8,128)(2,1)S(1)}, u32[]{:S(2)}, u32[]{:S(2)}) collective-permute-start(bf16[2,256,256]{2,1,0:T(8,128)(2,1)S(1)} %get-tuple-element.34), channel_id=1, source_target_pairs={{0,2},{1,3},{2,0},{3,1},{4,6},{5,7},{6,4},{7,5},{8,10},{9,11},{10,... | collective-permute-start | bytes 786440 | tf_op jit(solution)/shard_map/ppermute | solution.py:362
  72.2 6.2 %collective-permute-start.23 = (bf16[512,128]{1,0:T(8,128)(2,1)S(1)}, bf16[512,128]{1,0:T(8,128)(2,1)S(1)}, u32[]{:S(2)}, u32[]{:S(2)}) collective-permute-start(bf16[512,128]{1,0:T(8,128)(2,1)S(1)} %get-tuple-element.44), channel_id=1, source_target_pairs={{0,4},{8,0},{16,8},{24,16},{28,24},{20,28},{12,20},{4,12},{1,5},{9... | collective-permute-start | bytes 393224 | tf_op jit(solution)/shard_map/ppermute | solution.py:262
  (12 other events, 139.7 us)

commit v5 on v4

--- a/solution.py
+++ b/solution.py
@@ -138,8 +138,16 @@
     return lax.axis_index("seq") * lax.axis_size("head") + lax.axis_index("head")
 
 
-def project_kernel(codes, moved, a_ref, b_ref, *rest):
-    w_refs, rest = rest[: 2 * len(codes)], rest[2 * len(codes) :]
+def early_kernel(a_ref, b_ref, up_ref, down_ref, out_ref):
+    out_ref[0] = jnp.dot(a_ref[...], up_ref[...], preferred_element_type=jnp.float32)
+    out_ref[1] = jnp.dot(b_ref[...], down_ref[...], preferred_element_type=jnp.float32)
+
+
+def project_kernel(codes, moved, early, a_ref, b_ref, *rest):
+    if early:
+        early_ref, rest = rest[0], rest[1:]
+    number = (1 if early else 2) * len(codes)
+    w_refs, rest = rest[:number], rest[number:]
     if moved:
         held_ref, rest = rest[0], rest[1:]
     me = place()
@@ -154,8 +162,13 @@
     for i, values in enumerate(moved):
         put(lookup(values, me), held_ref[i])
     for i, values in enumerate(codes):
-        c = jnp.dot(a_ref[...], w_refs[2 * i][...], preferred_element_type=jnp.float32)
-        c += jnp.dot(b_ref[...], w_refs[2 * i + 1][...], preferred_element_type=jnp.float32)
+        if early:
+            x_ref = a_ref if i % 2 else b_ref
+            c = early_ref[i]
+            c += jnp.dot(x_ref[...], w_refs[i][...], preferred_element_type=jnp.float32)
+        else:
+            c = jnp.dot(a_ref[...], w_refs[2 * i][...], preferred_element_type=jnp.float32)
+            c += jnp.dot(b_ref[...], w_refs[2 * i + 1][...], preferred_element_type=jnp.float32)
         put(lookup(values, me), c.astype(jnp.bfloat16))
 
 
@@ -344,12 +357,26 @@
         reduce_plan(n, heads, sources, rounds)
     ):
         pieces = [piece for p in rounds[r] for piece in w[p]]
+        begun = []
+        if r == 1:
+            (first_up, last_up), (last_down, first_down) = w[n - 3], w[n - 2]
+            pieces = [last_up, last_down]
+            begun = [
+                pl.pallas_call(
+                    early_kernel,
+                    out_shape=jax.ShapeDtypeStruct((2, tok_rows, half), jnp.float32),
+                    in_specs=[VMEM] * 4,
+                    out_specs=VMEM,
+                    compiler_params=limit(8),
+                    name="early",
+                )(attended, paired, first_up, first_down)
+            ]
         cols = spans[r][1] - spans[r][0]
         outs = (block(count, cols),) * 2 + ((block(hold, cols),) if hold else ())
         send, keep, *rest = pl.pallas_call(
-            functools.partial(project_kernel, codes, moved),
+            functools.partial(project_kernel, codes, moved, r == 1),
             out_shape=outs,
-            in_specs=[VMEM] * (2 + len(pieces) + len(held)),
+            in_specs=[VMEM] * (2 + len(begun) + len(pieces) + len(held)),
             out_specs=(VMEM,) * len(outs),
             compiler_params=limit(8),
             cost_estimate=pl.CostEstimate(
@@ -358,7 +385,7 @@
                 transcendentals=0,
             ),
             name="project",
-        )(attended, paired, *pieces, *held)
+        )(attended, paired, *begun, *pieces, *held)
         came.append(lax.ppermute(send, "head", across))
         held = rest
         kept.append(keep)

time: 87.3 us -> 90 us (1.031)
  starting transfers between devices: 36.9 us -> 38.8 us
    ppermute x24, starting transfers between devices: 31.6 us -> 33.5 us  [move(): return lax.ppermute(x, 'seq', pairs)]
    pallas_call x4 -> x5, Pallas kernels: 3.5 us -> 3.57 us  [the longest x4 3.27 us: ring_device(): pl.pallas_call(functools.partial(project_kernel, codes, moved, r == 1), o...]
  transfers between devices with their start and end apart: 31 -> 31, of which waited for: 15 -> 13; matrix products, arithmetic and copies ran while one was open for 0% -> 0% of each run, Pallas kernels for 10% -> 10%
where the time goes in v5:
time: 90 us; the launch traced here: 89.9 us
  waiting for transfers between devices  39.8 us (44%)
  starting transfers between devices  38.8 us (43%)
  Pallas kernels  9.77 us (11%)
  local copies, waits for them, and re-layouts  1.17 us (1%)
    ppermute x24, waiting for transfers between devices, move(): return lax.ppermute(x, 'seq', pairs)  35.6 us
    ppermute x24, starting transfers between devices, move(): return lax.ppermute(x, 'seq', pairs)  33.5 us
    ppermute x4, starting transfers between devices, ring_device(): came.append(lax.ppermute(send, 'head', across))  4.61 us
    pallas_call x2, Pallas kernels, attend(): pl.pallas_call(functools.partial(attention_kernel, n, span, group, [[row[...  4.55 us
    ppermute x4, waiting for transfers between devices, ring_device(): came.append(lax.ppermute(send, 'head', across))  3.46 us
    pallas_call x4, Pallas kernels, ring_device(): pl.pallas_call(functools.partial(project_kernel, codes, moved, r == 1), o...  3.27 us
  transfers between devices with their start and end apart: 31, of which 13 were waited for; matrix products, arithmetic and copies ran while one was open for 0% of the time, Pallas kernels for 10%

profile of v5, /device:TPU:0, one launch (start us, length us, event | category | flops | bytes accessed | tf_op | source)
XLA Modules:
  0.0 89.9 jit_solution(15234765033630433393)
XLA Ops:
  1.8 2.6 %collective-permute-start = (bf16[256,256]{1,0:T(8,128)(2,1)S(1)}, bf16[256,256]{1,0:T(8,128)(2,1)S(1)}, u32[]{:S(2)}, u32[]{:S(2)}) collective-permute-start(bf16[256,256]{1,0:T(8,128)(2,1)S(1)} %pad_maximum_fusion.rest_0_), channel_id=1, source_target_pairs={{0,8},{8,16},{16,24},{24,28},{28,20},{20,12},{12,4},{4,0},{1,9},{9... | collective-permute-start | bytes 393224 | tf_op jit(solution)/shard_map/ppermute | solution.py:275
  4.4 1.6 %collective-permute-start.10 = (bf16[512,256]{1,0:T(8,128)(2,1)S(1)}, bf16[512,256]{1,0:T(8,128)(2,1)S(1)}, u32[]{:S(2)}, u32[]{:S(2)}) collective-permute-start(bf16[512,256]{1,0:T(8,128)(2,1)S(1)} %get-tuple-element.40.rest_0_), channel_id=1, source_target_pairs={{0,8},{8,16},{16,24},{24,28},{28,20},{20,12},{12,4},{4,0},{1,9},{9... | collective-permute-start | bytes 786440 | tf_op jit(solution)/shard_map/ppermute | solution.py:275
  6.4 2.2 %collective-permute-done.rest_1_ = bf16[256,256]{1,0:T(8,128)(2,1)S(1)} collective-permute-done((bf16[256,256]{1,0:T(8,128)(2,1)S(1)}, bf16[256,256]{1,0:T(8,128)(2,1)S(1)}, u32[]{:S(2)}, u32[]{:S(2)}) %collective-permute-start) | collective-permute-done | bytes 131104 | tf_op jit(solution)/shard_map/ppermute | solution.py:275
  8.7 2.1 %collective-permute-start.1 = (bf16[256,256]{1,0:T(8,128)(2,1)S(1)}, bf16[256,256]{1,0:T(8,128)(2,1)S(1)}, u32[]{:S(2)}, u32[]{:S(2)}) collective-permute-start(bf16[256,256]{1,0:T(8,128)(2,1)S(1)} %collective-permute-done.rest_1_), channel_id=1, source_target_pairs={{0,8},{8,16},{16,24},{24,28},{28,20},{20,12},{12,4},{4,0},{1,9},{9... | collective-permute-start | bytes 393224 | tf_op jit(solution)/shard_map/ppermute | solution.py:275
  12.7 1.6 %collective-permute-start.13 = (bf16[512,256]{1,0:T(8,128)(2,1)S(1)}, bf16[512,256]{1,0:T(8,128)(2,1)S(1)}, u32[]{:S(2)}, u32[]{:S(2)}) collective-permute-start(bf16[512,256]{1,0:T(8,128)(2,1)S(1)} %collective-permute-done.9.rest_1_), channel_id=1, source_target_pairs={{0,4},{8,0},{16,8},{24,16},{28,24},{20,28},{12,20},{4,12},{1,5},{9... | collective-permute-start | bytes 786440 | tf_op jit(solution)/shard_map/ppermute | solution.py:275
  14.3 2.5 %collective-permute-done.1.rest_3_ = bf16[256,256]{1,0:T(8,128)(2,1)S(1)} collective-permute-done((bf16[256,256]{1,0:T(8,128)(2,1)S(1)}, bf16[256,256]{1,0:T(8,128)(2,1)S(1)}, u32[]{:S(2)}, u32[]{:S(2)}) %collective-permute-start.1) | collective-permute-done | bytes 131104 | tf_op jit(solution)/shard_map/ppermute | solution.py:275
  16.9 1.8 %collective-permute-start.11 = (bf16[512,256]{1,0:T(8,128)(2,1)S(1)}, bf16[512,256]{1,0:T(8,128)(2,1)S(1)}, u32[]{:S(2)}, u32[]{:S(2)}) collective-permute-start(bf16[512,256]{1,0:T(8,128)(2,1)S(1)} %collective-permute-done.9.rest_1_), channel_id=1, source_target_pairs={{0,8},{8,16},{16,24},{24,28},{28,20},{20,12},{12,4},{4,0},{1,9},{9... | collective-permute-start | bytes 786440 | tf_op jit(solution)/shard_map/ppermute | solution.py:275
  18.7 1.6 %collective-permute-start.14 = (bf16[512,256]{1,0:T(8,128)(2,1)S(1)}, bf16[512,256]{1,0:T(8,128)(2,1)S(1)}, u32[]{:S(2)}, u32[]{:S(2)}) collective-permute-start(bf16[512,256]{1,0:T(8,128)(2,1)S(1)} %collective-permute-done.10.rest_2_), channel_id=1, source_target_pairs={{0,8},{8,16},{16,24},{24,28},{28,20},{20,12},{12,4},{4,0},{1,9},{9... | collective-permute-start | bytes 786440 | tf_op jit(solution)/shard_map/ppermute | solution.py:275
  20.3 2.5 %collective-permute-done.5.rest_4_ = bf16[256,256]{1,0:T(8,128)(2,1)S(1)} collective-permute-done((bf16[256,256]{1,0:T(8,128)(2,1)S(1)}, bf16[256,256]{1,0:T(8,128)(2,1)S(1)}, u32[]{:S(2)}, u32[]{:S(2)}) %collective-permute-start.5) | collective-permute-done | bytes 131104 | tf_op jit(solution)/shard_map/ppermute | solution.py:275
  24.8 8.6 %collective-permute-done.2.rest_5_ = bf16[256,256]{1,0:T(8,128)(2,1)S(1)} collective-permute-done((bf16[256,256]{1,0:T(8,128)(2,1)S(1)}, bf16[256,256]{1,0:T(8,128)(2,1)S(1)}, u32[]{:S(2)}, u32[]{:S(2)}) %collective-permute-start.2) | collective-permute-done | bytes 131104 | tf_op jit(solution)/shard_map/ppermute | solution.py:275
  37.4 1.6 %collective-permute-start.3 = (bf16[128,256]{1,0:T(8,128)(2,1)S(1)}, bf16[128,256]{1,0:T(8,128)(2,1)S(1)}, u32[]{:S(2)}, u32[]{:S(2)}) collective-permute-start(bf16[128,256]{1,0:T(8,128)(2,1)S(1)} %slice.32), channel_id=1, source_target_pairs={{0,8},{8,16},{16,24},{24,28},{28,20},{20,12},{12,4},{4,0},{1,9},{9... | collective-permute-start | bytes 196616 | tf_op jit(solution)/shard_map/ppermute | solution.py:275
  39.1 10.8 %collective-permute-done.3.rest_0_ = bf16[128,256]{1,0:T(8,128)(2,1)S(1)} collective-permute-done((bf16[128,256]{1,0:T(8,128)(2,1)S(1)}, bf16[128,256]{1,0:T(8,128)(2,1)S(1)}, u32[]{:S(2)}, u32[]{:S(2)}) %collective-permute-start.3) | collective-permute-done | bytes 65568 | tf_op jit(solution)/shard_map/ppermute | solution.py:275
  51.4 2.7 %attend.2 = (f32[2,512,128]{2,1,0:T(8,128)S(1)}, f32[2,512,128]{2,1,0:T(8,128)S(1)}, f32[2,512,128]{2,1,0:T(8,128)S(1)}) custom-call(s32[16]{0:T(128)S(1)} %copy-done.2, s32[2048]{0:T(1024)S(1)} %copy-done.1, s32[16,128]{1,0:T(8,128)S(1)} %bitcast.1, bf16[256,512]{1,0:T(8,128)(2,1)S(1)} %copy-done, bf16[256,256]{1,0:T(8,128)(2,1)S(1)} %pad_maximum_fusion.rest_0_, ...), custom_call_target="tpu_custom_call" | custom-call | flops 939524096 | bytes 917504 | tf_op jit(solution)/shard_map/attend/pallas_call | solution.py:312
  54.1 1.9 %attend.3.a_ref = bf16[256,512]{1,0:T(8,128)(2,1)S(1)} custom-call(s32[16]{0:T(128)S(1)} %copy-done.2, s32[2048]{0:T(1024)S(1)} %copy-done.1, s32[16,128]{1,0:T(8,128)S(1)} %bitcast.2, bf16[256,512]{1,0:T(8,128)(2,1)S(1)} %copy-done, bf16[128,256]{1,0:T(8,128)(2,1)S(1)} %collective-permute-done.3.rest_0_, ...), custom_call_target="tpu_custom_call" | custom-call | flops 134217728 | bytes 131072 | tf_op jit(solution)/shard_map/attend/pallas_call | solution.py:312
  56.1 4.4 %collective-permute-start.21 = (bf16[512,256]{1,0:T(8,128)(2,1)S(1)}, bf16[512,256]{1,0:T(8,128)(2,1)S(1)}, u32[]{:S(2)}, u32[]{:S(2)}) collective-permute-start(bf16[512,256]{1,0:T(8,128)(2,1)S(1)} %collective-permute-done.16.rest_8_), channel_id=1, source_target_pairs={{0,4},{8,0},{16,8},{24,16},{28,24},{20,28},{12,20},{4,12},{1,5},{9... | collective-permute-start | bytes 786440 | tf_op jit(solution)/shard_map/ppermute | solution.py:275
  60.6 2.0 %collective-permute-start.20 = (bf16[512,256]{1,0:T(8,128)(2,1)S(1)}, bf16[512,256]{1,0:T(8,128)(2,1)S(1)}, u32[]{:S(2)}, u32[]{:S(2)}) collective-permute-start(bf16[512,256]{1,0:T(8,128)(2,1)S(1)} %collective-permute-done.15.rest_7_), channel_id=1, source_target_pairs={{0,8},{8,16},{16,24},{24,28},{28,20},{20,12},{12,4},{4,0},{1,9},{9... | collective-permute-start | bytes 786440 | tf_op jit(solution)/shard_map/ppermute | solution.py:275
  62.7 2.0 %project.4 = (bf16[2,256,256]{2,1,0:T(8,128)(2,1)S(1)}, bf16[2,256,256]{2,1,0:T(8,128)(2,1)S(1)}, bf16[2,256,256]{2,1,0:T(8,128)(2,1)S(1)}) custom-call(bf16[256,512]{1,0:T(8,128)(2,1)S(1)} %attend.3.a_ref, bf16[256,512]{1,0:T(8,128)(2,1)S(1)} %collective-permute-done.8.b_ref, bf16[512,256]{1,0:T(8,128)(2,1)S(1)} %get-tuple-element.40.rest_0_, ...), custom_call_target="tpu_custom_call" | custom-call | flops 671088640 | bytes 2621440 | tf_op jit(solution)/shard_map/project/pallas_call | solution.py:376
  64.7 1.6 %collective-permute-start.26 = (bf16[2,256,256]{2,1,0:T(8,128)(2,1)S(1)}, bf16[2,256,256]{2,1,0:T(8,128)(2,1)S(1)}, u32[]{:S(2)}, u32[]{:S(2)}) collective-permute-start(bf16[2,256,256]{2,1,0:T(8,128)(2,1)S(1)} %get-tuple-element.33), channel_id=1, source_target_pairs={{0,2},{1,3},{2,0},{3,1},{4,6},{5,7},{6,4},{7,5},{8,10},{9,11},{10,... | collective-permute-start | bytes 786440 | tf_op jit(solution)/shard_map/ppermute | solution.py:389
  66.3 6.0 %collective-permute-done.19.down_ref = bf16[512,256]{1,0:T(8,128)(2,1)S(1)} collective-permute-done((bf16[512,256]{1,0:T(8,128)(2,1)S(1)}, bf16[512,256]{1,0:T(8,128)(2,1)S(1)}, u32[]{:S(2)}, u32[]{:S(2)}) %collective-permute-start.19) | collective-permute-done | bytes 262176 | tf_op jit(solution)/shard_map/ppermute | solution.py:275
  73.3 1.6 %collective-permute-start.27 = (bf16[2,256,256]{2,1,0:T(8,128)(2,1)S(1)}, bf16[2,256,256]{2,1,0:T(8,128)(2,1)S(1)}, u32[]{:S(2)}, u32[]{:S(2)}) collective-permute-start(bf16[2,256,256]{2,1,0:T(8,128)(2,1)S(1)} %get-tuple-element.34), channel_id=1, source_target_pairs={{0,2},{1,3},{2,0},{3,1},{4,6},{5,7},{6,4},{7,5},{8,10},{9,11},{10,... | collective-permute-start | bytes 786440 | tf_op jit(solution)/shard_map/ppermute | solution.py:389
  74.9 2.5 %collective-permute-start.23 = (bf16[512,128]{1,0:T(8,128)(2,1)S(1)}, bf16[512,128]{1,0:T(8,128)(2,1)S(1)}, u32[]{:S(2)}, u32[]{:S(2)}) collective-permute-start(bf16[512,128]{1,0:T(8,128)(2,1)S(1)} %get-tuple-element.44), channel_id=1, source_target_pairs={{0,4},{8,0},{16,8},{24,16},{28,24},{20,28},{12,20},{4,12},{1,5},{9... | collective-permute-start | bytes 393224 | tf_op jit(solution)/shard_map/ppermute | solution.py:275
  77.4 2.0 %collective-permute-start.25 = (bf16[512,128]{1,0:T(8,128)(2,1)S(1)}, bf16[512,128]{1,0:T(8,128)(2,1)S(1)}, u32[]{:S(2)}, u32[]{:S(2)}) collective-permute-start(bf16[512,128]{1,0:T(8,128)(2,1)S(1)} %get-tuple-element.43), channel_id=1, source_target_pairs={{0,4},{8,0},{16,8},{24,16},{28,24},{20,28},{12,20},{4,12},{1,5},{9... | collective-permute-start | bytes 393224 | tf_op jit(solution)/shard_map/ppermute | solution.py:275
  79.5 1.7 %collective-permute-done.23.rest_1_ = bf16[512,128]{1,0:T(8,128)(2,1)S(1)} collective-permute-done((bf16[512,128]{1,0:T(8,128)(2,1)S(1)}, bf16[512,128]{1,0:T(8,128)(2,1)S(1)}, u32[]{:S(2)}, u32[]{:S(2)}) %collective-permute-start.23) | collective-permute-done | bytes 131104 | tf_op jit(solution)/shard_map/ppermute | solution.py:275
  83.9 2.2 %collective-permute-done.28.rest_6_ = bf16[1,256,128]{2,1,0:T(8,128)(2,1)S(1)} collective-permute-done((bf16[1,256,128]{2,1,0:T(8,128)(2,1)S(1)}, bf16[1,256,128]{2,1,0:T(8,128)(2,1)S(1)}, u32[]{:S(2)}, u32[]{:S(2)}) %collective-permute-start.28) | collective-permute-done | bytes 65568 | tf_op jit(solution)/shard_map/ppermute | solution.py:389
  (65 shorter events, 19.6 us)
Async XLA Ops:
  1.2 11.5 %collective-permute-start.9 = (bf16[512,256]{1,0:T(8,128)(2,1)S(1)}, bf16[512,256]{1,0:T(8,128)(2,1)S(1)}, u32[]{:S(2)}, u32[]{:S(2)}) collective-permute-start(bf16[512,256]{1,0:T(8,128)(2,1)S(1)} %get-tuple-element.39), channel_id=1, source_target_pairs={{0,1},{1,0},{2,3},{3,2},{4,5},{5,4},{6,7},{7,6},{8,9},{9,8},{10,11... | collective-permute-start | bytes 786440 | tf_op jit(solution)/shard_map/ppermute | solution.py:303
  1.8 6.9 %collective-permute-start = (bf16[256,256]{1,0:T(8,128)(2,1)S(1)}, bf16[256,256]{1,0:T(8,128)(2,1)S(1)}, u32[]{:S(2)}, u32[]{:S(2)}) collective-permute-start(bf16[256,256]{1,0:T(8,128)(2,1)S(1)} %pad_maximum_fusion.rest_0_), channel_id=1, source_target_pairs={{0,8},{8,16},{16,24},{24,28},{28,20},{20,12},{12,4},{4,0},{1,9},{9... | collective-permute-start | bytes 393224 | tf_op jit(solution)/shard_map/ppermute | solution.py:275
  4.4 14.3 %collective-permute-start.10 = (bf16[512,256]{1,0:T(8,128)(2,1)S(1)}, bf16[512,256]{1,0:T(8,128)(2,1)S(1)}, u32[]{:S(2)}, u32[]{:S(2)}) collective-permute-start(bf16[512,256]{1,0:T(8,128)(2,1)S(1)} %get-tuple-element.40.rest_0_), channel_id=1, source_target_pairs={{0,8},{8,16},{16,24},{24,28},{28,20},{20,12},{12,4},{4,0},{1,9},{9... | collective-permute-start | bytes 786440 | tf_op jit(solution)/shard_map/ppermute | solution.py:275
  8.7 8.2 %collective-permute-start.1 = (bf16[256,256]{1,0:T(8,128)(2,1)S(1)}, bf16[256,256]{1,0:T(8,128)(2,1)S(1)}, u32[]{:S(2)}, u32[]{:S(2)}) collective-permute-start(bf16[256,256]{1,0:T(8,128)(2,1)S(1)} %collective-permute-done.rest_1_), channel_id=1, source_target_pairs={{0,8},{8,16},{16,24},{24,28},{28,20},{20,12},{12,4},{4,0},{1,9},{9... | collective-permute-start | bytes 393224 | tf_op jit(solution)/shard_map/ppermute | solution.py:275
  10.8 13.6 %collective-permute-start.12 = (bf16[512,256]{1,0:T(8,128)(2,1)S(1)}, bf16[512,256]{1,0:T(8,128)(2,1)S(1)}, u32[]{:S(2)}, u32[]{:S(2)}) collective-permute-start(bf16[512,256]{1,0:T(8,128)(2,1)S(1)} %get-tuple-element.40.rest_0_), channel_id=1, source_target_pairs={{0,4},{8,0},{16,8},{24,16},{28,24},{20,28},{12,20},{4,12},{1,5},{9... | collective-permute-start | bytes 786440 | tf_op jit(solution)/shard_map/ppermute | solution.py:275
  11.3 11.5 %collective-permute-start.5 = (bf16[256,256]{1,0:T(8,128)(2,1)S(1)}, bf16[256,256]{1,0:T(8,128)(2,1)S(1)}, u32[]{:S(2)}, u32[]{:S(2)}) collective-permute-start(bf16[256,256]{1,0:T(8,128)(2,1)S(1)} %collective-permute-done.4.rest_2_), channel_id=1, source_target_pairs={{0,4},{8,0},{16,8},{24,16},{28,24},{20,28},{12,20},{4,12},{1,5},{9... | collective-permute-start | bytes 393224 | tf_op jit(solution)/shard_map/ppermute | solution.py:275
  12.7 22.1 %collective-permute-start.13 = (bf16[512,256]{1,0:T(8,128)(2,1)S(1)}, bf16[512,256]{1,0:T(8,128)(2,1)S(1)}, u32[]{:S(2)}, u32[]{:S(2)}) collective-permute-start(bf16[512,256]{1,0:T(8,128)(2,1)S(1)} %collective-permute-done.9.rest_1_), channel_id=1, source_target_pairs={{0,4},{8,0},{16,8},{24,16},{28,24},{20,28},{12,20},{4,12},{1,5},{9... | collective-permute-start | bytes 786440 | tf_op jit(solution)/shard_map/ppermute | solution.py:275
  16.9 19.6 %collective-permute-start.11 = (bf16[512,256]{1,0:T(8,128)(2,1)S(1)}, bf16[512,256]{1,0:T(8,128)(2,1)S(1)}, u32[]{:S(2)}, u32[]{:S(2)}) collective-permute-start(bf16[512,256]{1,0:T(8,128)(2,1)S(1)} %collective-permute-done.9.rest_1_), channel_id=1, source_target_pairs={{0,8},{8,16},{16,24},{24,28},{28,20},{20,12},{12,4},{4,0},{1,9},{9... | collective-permute-start | bytes 786440 | tf_op jit(solution)/shard_map/ppermute | solution.py:275
  18.7 18.2 %collective-permute-start.14 = (bf16[512,256]{1,0:T(8,128)(2,1)S(1)}, bf16[512,256]{1,0:T(8,128)(2,1)S(1)}, u32[]{:S(2)}, u32[]{:S(2)}) collective-permute-start(bf16[512,256]{1,0:T(8,128)(2,1)S(1)} %collective-permute-done.10.rest_2_), channel_id=1, source_target_pairs={{0,8},{8,16},{16,24},{24,28},{28,20},{20,12},{12,4},{4,0},{1,9},{9... | collective-permute-start | bytes 786440 | tf_op jit(solution)/shard_map/ppermute | solution.py:275
  22.8 10.6 %collective-permute-start.2 = (bf16[256,256]{1,0:T(8,128)(2,1)S(1)}, bf16[256,256]{1,0:T(8,128)(2,1)S(1)}, u32[]{:S(2)}, u32[]{:S(2)}) collective-permute-start(bf16[256,256]{1,0:T(8,128)(2,1)S(1)} %collective-permute-done.1.rest_3_), channel_id=1, source_target_pairs={{0,8},{8,16},{16,24},{24,28},{28,20},{20,12},{12,4},{4,0},{1,9},{9... | collective-permute-start | bytes 393224 | tf_op jit(solution)/shard_map/ppermute | solution.py:275
  24.3 13.1 %collective-permute-start.6 = (bf16[256,256]{1,0:T(8,128)(2,1)S(1)}, bf16[256,256]{1,0:T(8,128)(2,1)S(1)}, u32[]{:S(2)}, u32[]{:S(2)}) collective-permute-start(bf16[256,256]{1,0:T(8,128)(2,1)S(1)} %collective-permute-done.5.rest_4_), channel_id=1, source_target_pairs={{0,4},{8,0},{16,8},{24,16},{28,24},{20,28},{12,20},{4,12},{1,5},{9... | collective-permute-start | bytes 393224 | tf_op jit(solution)/shard_map/ppermute | solution.py:275
  33.4 22.7 %collective-permute-start.16 = (bf16[512,256]{1,0:T(8,128)(2,1)S(1)}, bf16[512,256]{1,0:T(8,128)(2,1)S(1)}, u32[]{:S(2)}, u32[]{:S(2)}) collective-permute-start(bf16[512,256]{1,0:T(8,128)(2,1)S(1)} %collective-permute-done.12.rest_4_), channel_id=1, source_target_pairs={{0,4},{8,0},{16,8},{24,16},{28,24},{20,28},{12,20},{4,12},{1,5},{9... | collective-permute-start | bytes 786440 | tf_op jit(solution)/shard_map/ppermute | solution.py:275
  34.8 25.7 %collective-permute-start.17 = (bf16[512,256]{1,0:T(8,128)(2,1)S(1)}, bf16[512,256]{1,0:T(8,128)(2,1)S(1)}, u32[]{:S(2)}, u32[]{:S(2)}) collective-permute-start(bf16[512,256]{1,0:T(8,128)(2,1)S(1)} %collective-permute-done.13.rest_5_), channel_id=1, source_target_pairs={{0,4},{8,0},{16,8},{24,16},{28,24},{20,28},{12,20},{4,12},{1,5},{9... | collective-permute-start | bytes 786440 | tf_op jit(solution)/shard_map/ppermute | solution.py:275
  36.4 24.2 %collective-permute-start.15 = (bf16[512,256]{1,0:T(8,128)(2,1)S(1)}, bf16[512,256]{1,0:T(8,128)(2,1)S(1)}, u32[]{:S(2)}, u32[]{:S(2)}) collective-permute-start(bf16[512,256]{1,0:T(8,128)(2,1)S(1)} %collective-permute-done.11.rest_3_), channel_id=1, source_target_pairs={{0,8},{8,16},{16,24},{24,28},{28,20},{20,12},{12,4},{4,0},{1,9},{9... | collective-permute-start | bytes 786440 | tf_op jit(solution)/shard_map/ppermute | solution.py:275
  36.9 25.7 %collective-permute-start.18 = (bf16[512,256]{1,0:T(8,128)(2,1)S(1)}, bf16[512,256]{1,0:T(8,128)(2,1)S(1)}, u32[]{:S(2)}, u32[]{:S(2)}) collective-permute-start(bf16[512,256]{1,0:T(8,128)(2,1)S(1)} %collective-permute-done.14.rest_6_), channel_id=1, source_target_pairs={{0,8},{8,16},{16,24},{24,28},{28,20},{20,12},{12,4},{4,0},{1,9},{9... | collective-permute-start | bytes 786440 | tf_op jit(solution)/shard_map/ppermute | solution.py:275
  37.4 12.4 %collective-permute-start.3 = (bf16[128,256]{1,0:T(8,128)(2,1)S(1)}, bf16[128,256]{1,0:T(8,128)(2,1)S(1)}, u32[]{:S(2)}, u32[]{:S(2)}) collective-permute-start(bf16[128,256]{1,0:T(8,128)(2,1)S(1)} %slice.32), channel_id=1, source_target_pairs={{0,8},{8,16},{16,24},{24,28},{28,20},{20,12},{12,4},{4,0},{1,9},{9... | collective-permute-start | bytes 196616 | tf_op jit(solution)/shard_map/ppermute | solution.py:275
  56.0 6.7 %collective-permute-start.8 = (bf16[256,512]{1,0:T(8,128)(2,1)S(1)}, bf16[256,512]{1,0:T(8,128)(2,1)S(1)}, u32[]{:S(2)}, u32[]{:S(2)}) collective-permute-start(bf16[256,512]{1,0:T(8,128)(2,1)S(1)} %attend.3.a_ref), channel_id=1, source_target_pairs={{0,1},{1,0},{2,3},{3,2},{4,5},{5,4},{6,7},{7,6},{8,9},{9,8},{10,11... | collective-permute-start | bytes 786440 | tf_op jit(solution)/shard_map/ppermute | solution.py:346
  56.1 16.5 %collective-permute-start.21 = (bf16[512,256]{1,0:T(8,128)(2,1)S(1)}, bf16[512,256]{1,0:T(8,128)(2,1)S(1)}, u32[]{:S(2)}, u32[]{:S(2)}) collective-permute-start(bf16[512,256]{1,0:T(8,128)(2,1)S(1)} %collective-permute-done.16.rest_8_), channel_id=1, source_target_pairs={{0,4},{8,0},{16,8},{24,16},{28,24},{20,28},{12,20},{4,12},{1,5},{9... | collective-permute-start | bytes 786440 | tf_op jit(solution)/shard_map/ppermute | solution.py:275
  60.5 11.8 %collective-permute-start.19 = (bf16[512,256]{1,0:T(8,128)(2,1)S(1)}, bf16[512,256]{1,0:T(8,128)(2,1)S(1)}, u32[]{:S(2)}, u32[]{:S(2)}) collective-permute-start(bf16[512,256]{1,0:T(8,128)(2,1)S(1)} %collective-permute-done.17.rest_9_), channel_id=1, source_target_pairs={{0,4},{8,0},{16,8},{24,16},{28,24},{20,28},{12,20},{4,12},{1,5},{9... | collective-permute-start | bytes 786440 | tf_op jit(solution)/shard_map/ppermute | solution.py:275
  60.6 12.0 %collective-permute-start.20 = (bf16[512,256]{1,0:T(8,128)(2,1)S(1)}, bf16[512,256]{1,0:T(8,128)(2,1)S(1)}, u32[]{:S(2)}, u32[]{:S(2)}) collective-permute-start(bf16[512,256]{1,0:T(8,128)(2,1)S(1)} %collective-permute-done.15.rest_7_), channel_id=1, source_target_pairs={{0,8},{8,16},{16,24},{24,28},{28,20},{20,12},{12,4},{4,0},{1,9},{9... | collective-permute-start | bytes 786440 | tf_op jit(solution)/shard_map/ppermute | solution.py:275
  62.6 14.9 %collective-permute-start.22 = (bf16[512,128]{1,0:T(8,128)(2,1)S(1)}, bf16[512,128]{1,0:T(8,128)(2,1)S(1)}, u32[]{:S(2)}, u32[]{:S(2)}) collective-permute-start(bf16[512,128]{1,0:T(8,128)(2,1)S(1)} %get-tuple-element.46), channel_id=1, source_target_pairs={{0,8},{8,16},{16,24},{24,28},{28,20},{20,12},{12,4},{4,0},{1,9},{9... | collective-permute-start | bytes 393224 | tf_op jit(solution)/shard_map/ppermute | solution.py:275
  64.7 19.2 %collective-permute-start.26 = (bf16[2,256,256]{2,1,0:T(8,128)(2,1)S(1)}, bf16[2,256,256]{2,1,0:T(8,128)(2,1)S(1)}, u32[]{:S(2)}, u32[]{:S(2)}) collective-permute-start(bf16[2,256,256]{2,1,0:T(8,128)(2,1)S(1)} %get-tuple-element.33), channel_id=1, source_target_pairs={{0,2},{1,3},{2,0},{3,1},{4,6},{5,7},{6,4},{7,5},{8,10},{9,11},{10,... | collective-permute-start | bytes 786440 | tf_op jit(solution)/shard_map/ppermute | solution.py:389
  73.3 14.1 %collective-permute-start.27 = (bf16[2,256,256]{2,1,0:T(8,128)(2,1)S(1)}, bf16[2,256,256]{2,1,0:T(8,128)(2,1)S(1)}, u32[]{:S(2)}, u32[]{:S(2)}) collective-permute-start(bf16[2,256,256]{2,1,0:T(8,128)(2,1)S(1)} %get-tuple-element.34), channel_id=1, source_target_pairs={{0,2},{1,3},{2,0},{3,1},{4,6},{5,7},{6,4},{7,5},{8,10},{9,11},{10,... | collective-permute-start | bytes 786440 | tf_op jit(solution)/shard_map/ppermute | solution.py:389
  74.9 6.2 %collective-permute-start.23 = (bf16[512,128]{1,0:T(8,128)(2,1)S(1)}, bf16[512,128]{1,0:T(8,128)(2,1)S(1)}, u32[]{:S(2)}, u32[]{:S(2)}) collective-permute-start(bf16[512,128]{1,0:T(8,128)(2,1)S(1)} %get-tuple-element.44), channel_id=1, source_target_pairs={{0,4},{8,0},{16,8},{24,16},{28,24},{20,28},{12,20},{4,12},{1,5},{9... | collective-permute-start | bytes 393224 | tf_op jit(solution)/shard_map/ppermute | solution.py:275
  (12 other events, 145.4 us)
